TPU v7x, 8 devices: a whole 2x2x1 slice. The times are simulated.
8 devices in a mesh: tp: 2 (over z, y), dp: 4 (over x, core).
Axes of the slice: x: 2, y: 2, z: 1, core: 2. Of those that a mesh axis runs over, the one named last changes fastest.
Arguments:
- prompts: bfloat16 [16, 1024, 4096], P('dp')
- lengths: int32 [16], P('dp')
- targets: int32 [16], P('dp')
- norm_attn: bfloat16 [1, 4096], replicated
- norm_mlp: bfloat16 [1, 4096], replicated
- norm_final: bfloat16 [4096], replicated
- w_query: bfloat16 [1, 4096, 4096], P(None, ('dp', 'tp'))
- w_key: bfloat16 [1, 4096, 1024], P(None, ('dp', 'tp'))
- w_value: bfloat16 [1, 4096, 1024], P(None, ('dp', 'tp'))
- w_out: bfloat16 [1, 4096, 4096], P(None, ('dp', 'tp'))
- w_gate: bfloat16 [1, 4096, 14336], P(None, ('dp', 'tp'))
- w_up: bfloat16 [1, 4096, 14336], P(None, ('dp', 'tp'))
- w_down: bfloat16 [1, 14336, 4096], P(None, ('dp', 'tp'))
- w_head: bfloat16 [4096, 32000], P(('dp', 'tp'))
Outputs:
- output 1: bfloat16 [1, 4096, 4096], P(None, None, 'tp')
- output 2: bfloat16 [1, 4096, 1024], P(None, None, 'tp')
- output 3: bfloat16 [1, 4096, 1024], P(None, None, 'tp')
- output 4: bfloat16 [1, 4096, 4096], P(None, 'tp')
- output 5: bfloat16 [1, 4096, 14336], P(None, None, 'tp')
- output 6: bfloat16 [1, 4096, 14336], P(None, None, 'tp')
- output 7: bfloat16 [1, 14336, 4096], P(None, 'tp')
- output 8: bfloat16 [4096, 32000], P(None, 'tp')
- output 9: bfloat16 [1, 16, 8, 1024, 128], P(None, 'dp', 'tp')
- output 10: bfloat16 [1, 16, 8, 1024, 128], P(None, 'dp', 'tp')
- output 11: float32 [16], P('dp')
All inputs are finite; a program needn't handle non-finite values.
Results may differ from a plain program's by a relative error of at most 0.00231272.
Values are sent between devices in bfloat16 or wider.
A program may use at most 2 GiB of HBM per device.

v0:
```python
import jax
import jax.numpy as jnp
from jax import lax
from jax.sharding import PartitionSpec as P

HEAD_DIM = 128
RMS_EPS = 1e-5
ROPE_BASE = 10000.0


def rms_norm(hidden, gain):
    hidden_f32 = hidden.astype(jnp.float32)
    inv_rms = lax.rsqrt(jnp.mean(hidden_f32 * hidden_f32, axis=-1, keepdims=True) + RMS_EPS)
    return (hidden_f32 * inv_rms * gain.astype(jnp.float32)).astype(jnp.bfloat16)


def rotate(projected, cosines, sines):
    half_dim = HEAD_DIM // 2
    first_half = projected[..., :half_dim]
    second_half = projected[..., half_dim:]
    return jnp.concatenate([first_half * cosines - second_half * sines, second_half * cosines + first_half * sines], axis=-1)


def rope_and_mask(lengths, seq_len):
    positions = jnp.arange(seq_len)
    inv_freq = ROPE_BASE ** (-jnp.arange(HEAD_DIM // 2, dtype=jnp.float32) * (2.0 / HEAD_DIM))
    angles = positions.astype(jnp.float32)[:, None, None] * inv_freq
    causal = positions[None, :] <= positions[:, None]
    key_ok = causal[None] & (positions[None, None, :] < lengths[:, None, None])
    return jnp.cos(angles), jnp.sin(angles), key_ok[:, None, None]


def attention(normed, q_weight, k_weight, v_weight, key_ok, cosines, sines):
    batch_rows = normed.shape[0]
    seq_len = normed.shape[1]
    head_count = q_weight.shape[1] // HEAD_DIM
    kv_count = k_weight.shape[1] // HEAD_DIM
    queries = jnp.dot(normed, q_weight, preferred_element_type=jnp.float32).reshape(batch_rows, seq_len, head_count, HEAD_DIM)
    keys_raw = jnp.dot(normed, k_weight, preferred_element_type=jnp.float32).reshape(batch_rows, seq_len, kv_count, HEAD_DIM)
    values = jnp.dot(normed, v_weight, preferred_element_type=jnp.float32).astype(jnp.bfloat16).reshape(batch_rows, seq_len, kv_count, HEAD_DIM)
    queries = rotate(queries, cosines, sines).astype(jnp.bfloat16).reshape(batch_rows, seq_len, kv_count, head_count // kv_count, HEAD_DIM)
    keys_rot = rotate(keys_raw, cosines, sines).astype(jnp.bfloat16)
    scores = jnp.einsum("bqkgh,bskh->bkgqs", queries, keys_rot, preferred_element_type=jnp.float32) * HEAD_DIM ** -0.5
    attn_probs = jax.nn.softmax(jnp.where(key_ok, scores, -1e30), axis=-1).astype(jnp.bfloat16)
    attn_out = jnp.einsum("bkgqs,bskh->bqkgh", attn_probs, values, preferred_element_type=jnp.float32)
    attn_out = attn_out.astype(jnp.bfloat16).reshape(batch_rows, seq_len, head_count * HEAD_DIM)
    return attn_out, jnp.transpose(keys_rot, (0, 2, 1, 3)), jnp.transpose(values, (0, 2, 1, 3))


def gated_mlp(normed, gate_weight, up_weight):
    gate_proj = jnp.dot(normed, gate_weight, preferred_element_type=jnp.float32)
    up_proj = jnp.dot(normed, up_weight, preferred_element_type=jnp.float32)
    return (jax.nn.silu(gate_proj) * up_proj).astype(jnp.bfloat16)


def col_layout(shard_mat):
    own_rows = lax.all_to_all(shard_mat, "tp", 1, 0, tiled=True)
    return lax.all_gather(own_rows, "dp", axis=0, tiled=True)


def row_layout(shard_mat, tp_size, dp_size):
    perm_pairs = [(source_idx, (source_idx % dp_size) * tp_size + source_idx // dp_size) for source_idx in range(tp_size * dp_size)]
    placed = lax.ppermute(shard_mat, ("tp", "dp"), perm_pairs)
    return lax.all_gather(placed, "dp", axis=0, tiled=True)


def add_partials(hidden, partial):
    gathered = lax.all_gather(partial, "tp", axis=0)
    return (hidden.astype(jnp.float32) + jnp.sum(gathered.astype(jnp.float32), axis=0)).astype(jnp.bfloat16)


def solution(mesh):
    tp_size = mesh.shape["tp"]
    dp_size = mesh.shape["dp"]
    train_spec = P(None, ("dp", "tp"), None)
    col_spec = P(None, None, "tp")
    row_spec = P(None, "tp", None)
    cache_spec = P(None, "dp", "tp", None, None)

    def device_program(prompts, lengths, targets, norm_attn, norm_mlp, norm_final, w_query, w_key, w_value, w_out, w_gate, w_up, w_down, w_head):
        cosines, sines, key_ok = rope_and_mask(lengths, prompts.shape[1])
        hidden = prompts
        collected = [[], [], [], [], [], [], []]
        key_list = []
        value_list = []
        for layer_idx in range(w_query.shape[0]):
            q_weight = col_layout(w_query[layer_idx])
            k_weight = col_layout(w_key[layer_idx])
            v_weight = col_layout(w_value[layer_idx])
            o_weight = row_layout(w_out[layer_idx], tp_size, dp_size)
            gate_weight = col_layout(w_gate[layer_idx])
            up_weight = col_layout(w_up[layer_idx])
            down_weight = row_layout(w_down[layer_idx], tp_size, dp_size)
            for store_list, weight_mat in zip(collected, (q_weight, k_weight, v_weight, o_weight, gate_weight, up_weight, down_weight)):
                store_list.append(weight_mat)
            attn_out, keys_rot, values = attention(rms_norm(hidden, norm_attn[layer_idx]), q_weight, k_weight, v_weight, key_ok, cosines, sines)
            key_list.append(keys_rot)
            value_list.append(values)
            hidden = add_partials(hidden, jnp.dot(attn_out, o_weight, preferred_element_type=jnp.float32).astype(jnp.bfloat16))
            mlp_act = gated_mlp(rms_norm(hidden, norm_mlp[layer_idx]), gate_weight, up_weight)
            hidden = add_partials(hidden, jnp.dot(mlp_act, down_weight, preferred_element_type=jnp.float32).astype(jnp.bfloat16))
        head_weight = col_layout(w_head)
        last_rows = jnp.take_along_axis(hidden, (lengths - 1)[:, None, None], axis=1)[:, 0]
        logits = jnp.dot(rms_norm(last_rows, norm_final), head_weight, preferred_element_type=jnp.float32)
        vocab_local = logits.shape[1]
        vocab_ids = lax.axis_index("tp") * vocab_local + jnp.arange(vocab_local)
        local_lse = jax.nn.logsumexp(logits, axis=-1)
        total_lse = jax.nn.logsumexp(lax.all_gather(local_lse, "tp", axis=0), axis=0)
        picked = lax.psum(jnp.sum(jnp.where(vocab_ids[None, :] == targets[:, None], logits, 0.0), axis=-1), "tp")
        logprobs = picked - total_lse
        stacked = tuple(jnp.stack(store_list) for store_list in collected)
        return stacked + (head_weight, jnp.stack(key_list), jnp.stack(value_list), logprobs)

    return jax.shard_map(
        device_program,
        mesh=mesh,
        in_specs=(P("dp", None, None), P("dp"), P("dp"), P(), P(), P(), train_spec, train_spec, train_spec, train_spec, train_spec, train_spec, train_spec, P(("dp", "tp"), None)),
        out_specs=(col_spec, col_spec, col_spec, row_spec, col_spec, col_spec, row_spec, P(None, "tp"), cache_spec, cache_spec, P("dp")),
        check_vma=False,
    )
```

profile of v0, /device:TPU:0, one launch (start us, length us, event | category | flops | bytes accessed | tf_op | source)
XLA Modules:
  0.0 5449.2 jit_solution(11314399831138632091)
XLA Ops:
  7.2 1.5 copy.41
  8.8 18.0 all_to_all.114
  26.8 1.1 copy.64
  28.0 1.5 copy.43
  29.5 15.2 all_to_all.115
  44.7 1.1 copy.65
  45.9 7.8 all_to_all.84
  53.7 4.1 copy.40
  57.7 49.3 all_to_all.116
  107.2 32.9 collective-permute-start
  140.5 11.3 fusion.6
  151.9 1.9 multiply_cosine_fusion
  153.8 3.6 broadcast_and_fusion
  158.0 23.2 fusion.30
  181.2 4.2 fusion.67
  185.5 6.9 copy.61
  192.3 6.9 copy.62
  199.2 9.5 subtract_convert_fusion.1
  208.7 24.0 fusion.44
  232.7 16.7 all-gather.14.cloned.1.call-done
  249.4 79.0 %fusion.26 = f32[4,1024,2048]{2,1,0:T(8,128)} fusion(bf16[4,1024,4096]{2,1,0:T(8,128)(2,1)} %param.14, f32[4096]{0:T(1024)S(1)} %bitcast.165, f32[4,1024]{1,0:T(4,128)S(1)} %add_rsqrt_fusion.1, bf16[4096,2048]{1,0:T(8,128)(2,1)} %all-gather.14.cloned.1.call-done), kind=kOutput, calls=%fused_computation.38 | convolution fusion | flops 68786585600 | bytes 83918848 | tf_op jit(solution)/shard_map/dot_general | solution.py:38
  328.4 27.7 copy.66
  356.1 28.1 subtract_convert_fusion
  384.2 15.1 copy.51
  399.4 10.7 copy.52
  410.1 127.2 %fusion.68 = (f32[4,4,4,1024]{3,2,1,0:T(4,128)S(1)}, f32[4,4,4,1024,1024]{3,4,2,1,0:T(8,128)}) fusion(pred[4,1024,1024]{1,2,0:T(8,128)(4,1)} %broadcast_and_fusion, bf16[4,1024,4,4,64]{4,1,3,2,0:T(8,128)(2,1)} %bitcast.149, bf16[4,1024,4,4,64]{4,1,3,2,0:T(8,128)(2,1)} %bitcast.148, bf16[4,1024,4,64]{3,1,2,0:T(8,128)(2,1)} %get-tuple-element.40, ...), kind=kOutput, calls=%fused_computation.94 | convolution fusion | flops 17490247680 | bytes 293863424 | tf_op jit(solution)/shard_map/sub | solution.py:44
  537.2 87.3 %fusion.34 = bf16[4,4,128,4,1024]{4,2,3,1,0:T(8,128)(2,1)} fusion(bf16[4,1024,4,128,1]{1,3,4,2,0:T(8,128)(2,1)} %bitcast.154, f32[4,4,4,1024,1024]{3,4,2,1,0:T(8,128)} %get-tuple-element.46, f32[4,4,4,1024]{3,2,1,0:T(4,128)S(1)} %get-tuple-element.45), kind=kOutput, calls=%fused_computation.44 | convolution fusion | flops 17322475520 | bytes 289669120 | tf_op jit(solution)/shard_map/bkgqs,bskh->bqkgh/dot_general | solution.py:45
  624.5 78.7 %convolution_convert_fusion = bf16[4,1024,4096]{2,1,0:T(8,128)(2,1)} fusion(bf16[4,1024,2048]{1,2,0:T(8,128)(2,1)} %bitcast.171, bf16[2048,4096]{1,0:T(8,128)(2,1)} %all-gather.20.cloned.1.call-done), kind=kOutput, calls=%fused_computation.36 | convolution fusion | flops 68736253952 | bytes 67108864 | tf_op jit(solution)/shard_map/dot_general | solution.py:99
  703.3 30.1 all_to_all.100
  733.4 9.9 copy.46
  743.3 380.9 %all_to_all.117 = bf16[512,2,7168]{2,0,1:T(8,128)(2,1)} all-to-all(bf16[512,2,7168]{2,0,1:T(8,128)(2,1)S(1)} %copy.46), channel_id=1, replica_groups=mesh['tp'=2,'dp'=4] {'tp'}, dimensions={1} | all-to-all | bytes 29360128 | tf_op jit(solution)/shard_map/all_to_all | solution.py:57
  1124.3 30.2 all_to_all.96
  1154.5 9.9 copy.45
  1164.5 323.7 %all_to_all.118 = bf16[512,2,7168]{2,0,1:T(8,128)(2,1)} all-to-all(bf16[512,2,7168]{2,0,1:T(8,128)(2,1)S(1)} %copy.45), channel_id=1, replica_groups=mesh['tp'=2,'dp'=4] {'tp'}, dimensions={1} | all-to-all | bytes 29360128 | tf_op jit(solution)/shard_map/all_to_all | solution.py:57
  1488.3 110.9 %collective-permute-start.1 = (bf16[1792,4096]{1,0:T(8,128)(2,1)}, bf16[1792,4096]{1,0:T(8,128)(2,1)}, u32[]{:S(2)}, u32[]{:S(2)}) collective-permute-start(bf16[1792,4096]{1,0:T(8,128)(2,1)} %bitcast.169), channel_id=1, source_target_pairs={{0,0},{1,2},{2,4},{3,6},{4,1},{5,3},{6,5},{7,7}} | collective-permute-start | bytes 44040200 | tf_op jit(solution)/shard_map/ppermute | solution.py:63
  1599.3 399.6 %all-gather.30.cloned.1.call-done = bf16[8,1024,4096]{2,1,0:T(8,128)(2,1)} async-done(((bf16[4,1024,4096]{2,1,0:T(8,128)(2,1)}), bf16[8,1024,4096]{2,1,0:T(8,128)(2,1)}) %all-gather.30.cloned.1.call-update) | async-done | bytes 67108880 | tf_op jit(solution)/shard_map/all_gather | solution.py:68
  1998.9 44.2 convert_reduce_fusion.1
  2043.1 42.7 fusion.10
  2085.8 256.3 %all-gather.24.cloned.1.call-done = bf16[4096,7168]{1,0:T(8,128)(2,1)} async-done(((bf16[1024,7168]{1,0:T(8,128)(2,1)}), bf16[4096,7168]{1,0:T(8,128)(2,1)}) %all-gather.24.cloned.1.call-update) | async-done | bytes 58720272 | tf_op jit(solution)/shard_map/all_gather | solution.py:58
  2342.1 256.5 %fusion.16 = f32[4,1024,7168]{2,1,0:T(8,128)} fusion(bf16[4096,7168]{1,0:T(8,128)(2,1)} %all-gather.24.cloned.1.call-done, bf16[4,1024,4096]{2,1,0:T(8,128)(2,1)} %get-tuple-element.36, f32[4096]{0:T(1024)S(1)} %bitcast.166, f32[4,1024]{1,0:T(4,128)S(1)} %add_rsqrt_fusion), kind=kOutput, calls=%fused_computation.29 | convolution fusion | flops 240585277440 | bytes 209747968 | tf_op jit(solution)/shard_map/dot_general | solution.py:52
  2598.6 88.2 %all-gather.22.cloned.1.call-done = bf16[4096,7168]{1,0:T(8,128)(2,1)} async-done(((bf16[1024,7168]{1,0:T(8,128)(2,1)}), bf16[4096,7168]{1,0:T(8,128)(2,1)}) %all-gather.22.cloned.1.call-update) | async-done | bytes 58720272 | tf_op jit(solution)/shard_map/all_gather | solution.py:58
  2686.9 269.5 %multiply_convert_fusion = bf16[4,1024,7168]{2,1,0:T(8,128)(2,1)} fusion(f32[4,1024,7168]{2,1,0:T(8,128)} %fusion.16, bf16[4096,7168]{1,0:T(8,128)(2,1)} %all-gather.22.cloned.1.call-done, bf16[4,1024,4096]{2,1,0:T(8,128)(2,1)} %get-tuple-element.36, f32[4096]{0:T(1024)S(1)} %bitcast.167, f32[4,1024]{1,0:T(4,128)S(1)} %add_rsqrt_fusion), kind=kOutput, calls=%fused_computation.12 | convolution fusion | flops 240761438208 | bytes 268468224 | tf_op jit(solution)/shard_map/dot_general | solution.py:51
  2956.4 75.2 %all-gather.26.cloned.1.call-done = bf16[7168,4096]{1,0:T(8,128)(2,1)} async-done(((bf16[1792,4096]{1,0:T(8,128)(2,1)}), bf16[7168,4096]{1,0:T(8,128)(2,1)}) %all-gather.26.cloned.1.call-update) | async-done | bytes 58720272 | tf_op jit(solution)/shard_map/all_gather | solution.py:64
  3031.6 258.0 %fusion.21 = bf16[4,1024,4096]{2,1,0:T(8,128)(2,1)} fusion(bf16[4,1024,7168]{2,1,0:T(8,128)(2,1)} %multiply_convert_fusion, bf16[7168,4096]{1,0:T(8,128)(2,1)} %all-gather.26.cloned.1.call-done), kind=kOutput, calls=%fused_computation.37 | convolution fusion | flops 240534945792 | bytes 150994944 | tf_op jit(solution)/shard_map/dot_general | solution.py:101
  3289.7 22.7 copy.68
  3312.4 737.5 %all_to_all.119 = bf16[512,2,16000]{2,0,1:T(8,128)(2,1)} all-to-all(bf16[512,2,16000]{2,0,1:T(8,128)(2,1)} %bitcast.138), channel_id=1, replica_groups=mesh['tp'=2,'dp'=4] {'tp'}, dimensions={1} | all-to-all | bytes 65536000 | tf_op jit(solution)/shard_map/all_to_all | solution.py:57
  4050.1 6.2 copy.50
  4056.3 6.4 copy.55
  4062.7 6.4 copy.56
  4069.1 5.9 fusion.65
  4075.0 329.1 %all-gather.32.cloned.1.call-done = bf16[8,1024,4096]{2,1,0:T(8,128)(2,1)} async-done(((bf16[4,1024,4096]{2,1,0:T(8,128)(2,1)}), bf16[8,1024,4096]{2,1,0:T(8,128)(2,1)}) %all-gather.32.cloned.1.call-update) | async-done | bytes 67108880 | tf_op jit(solution)/shard_map/all_gather | solution.py:68
  4404.1 44.2 convert_reduce_fusion
  4448.3 42.3 fusion.13
  4490.6 1.5 gather_fusion
  4492.4 665.9 %all-gather.28.cloned.1.call-done = bf16[4096,16000]{1,0:T(8,128)(2,1)} async-done(((bf16[1024,16000]{1,0:T(8,128)(2,1)}), bf16[4096,16000]{1,0:T(8,128)(2,1)}) %all-gather.28.cloned.1.call-update) | async-done | bytes 131072016 | tf_op jit(solution)/shard_map/all_gather | solution.py:58
  5158.3 41.7 fusion.73
  5200.4 4.2 all-gather.2
  5204.7 4.9 psum.7
  5210.2 14.2 copy.75
  5224.3 14.1 copy.76
  5238.4 39.0 copy.77
  5277.3 39.0 copy.78
  5316.3 39.2 copy.79
  5355.5 86.4 %copy.80 = bf16[4096,16000]{1,0:T(8,128)(2,1)} copy(bf16[4096,16000]{1,0:T(8,128)(2,1)} %all-gather.28.cloned.1.call-done) | data formatting | bytes 262144000
  (69 shorter events, 2.9 us)
Async XLA Ops:
  7.2 133.2 %copy-start.4 = (bf16[1,4096]{1,0:T(2,128)(2,1)S(1)}, bf16[1,4096]{1,0:T(2,128)(2,1)}, u32[]{:S(2)}) copy-start(bf16[1,4096]{1,0:T(2,128)(2,1)} %param.17) | copy-start | bytes 24580
  7.2 133.2 %copy-start.8 = (s32[4]{0:T(128)S(1)}, s32[4]{0:T(128)}, u32[]{:S(2)}) copy-start(s32[4]{0:T(128)} %param.15) | copy-start | bytes 52
  7.2 150.8 %all-gather.16.cloned.1.call-start = ((), (), s32[]{:S(2)}) async-start(), calls=%async_computation.7 | async-start | bytes 5242880 | tf_op jit(solution)/shard_map/all_gather | solution.py:58
  27.9 180.8 %all-gather.18.cloned.1.call-start = ((), (), s32[]{:S(2)}) async-start(), calls=%async_computation.8 | async-start | bytes 5242880 | tf_op jit(solution)/shard_map/all_gather | solution.py:58
  45.8 203.6 %all-gather.14.cloned.1.call-start = ((), (), s32[]{:S(2)}) async-start(), calls=%async_computation.6 | async-start | bytes 20971520 | tf_op jit(solution)/shard_map/all_gather | solution.py:58
  107.1 517.4 %all-gather.20.cloned.1.call-start = ((), (), s32[]{:S(2)}) async-start(), calls=%async_computation.9 | async-start | bytes 20971520 | tf_op jit(solution)/shard_map/all_gather | solution.py:64
  107.2 50.2 collective-permute-start
  153.8 45.5 copy-start
  153.8 45.4 copy-start.2
  157.4 1841.4 %all-gather.30.cloned.1.call-start = ((), (), s32[]{:S(2)}) async-start(), calls=%async_computation.14 | async-start | bytes 100663296 | tf_op jit(solution)/shard_map/all_gather | solution.py:68
  328.4 27.7 copy-start.1
  328.4 27.7 copy-start.3
  703.3 1638.8 %all-gather.24.cloned.1.call-start = ((), (), s32[]{:S(2)}) async-start(), calls=%async_computation.11 | async-start | bytes 73400320 | tf_op jit(solution)/shard_map/all_gather | solution.py:58
  1124.3 1562.6 %all-gather.22.cloned.1.call-start = ((), (), s32[]{:S(2)}) async-start(), calls=%async_computation.10 | async-start | bytes 73400320 | tf_op jit(solution)/shard_map/all_gather | solution.py:58
  1154.5 444.7 %copy-start.5 = (bf16[1,4096]{1,0:T(2,128)(2,1)S(1)}, bf16[1,4096]{1,0:T(2,128)(2,1)}, u32[]{:S(2)}) copy-start(bf16[1,4096]{1,0:T(2,128)(2,1)} %param.18) | copy-start | bytes 24580
  1488.2 1543.4 %all-gather.26.cloned.1.call-start = ((), (), s32[]{:S(2)}) async-start(), calls=%async_computation.12 | async-start | bytes 73400320 | tf_op jit(solution)/shard_map/all_gather | solution.py:64
  1488.3 110.9 %collective-permute-start.1 = (bf16[1792,4096]{1,0:T(8,128)(2,1)}, bf16[1792,4096]{1,0:T(8,128)(2,1)}, u32[]{:S(2)}, u32[]{:S(2)}) collective-permute-start(bf16[1792,4096]{1,0:T(8,128)(2,1)} %bitcast.169), channel_id=1, source_target_pairs={{0,0},{1,2},{2,4},{3,6},{4,1},{5,3},{6,5},{7,7}} | collective-permute-start | bytes 44040200 | tf_op jit(solution)/shard_map/ppermute | solution.py:63
  1599.3 2804.8 %all-gather.32.cloned.1.call-start = ((), (), s32[]{:S(2)}) async-start(), calls=%async_computation.15 | async-start | bytes 100663296 | tf_op jit(solution)/shard_map/all_gather | solution.py:68
  3289.7 1868.7 %all-gather.28.cloned.1.call-start = ((), (), s32[]{:S(2)}) async-start(), calls=%async_computation.13 | async-start | bytes 163840000 | tf_op jit(solution)/shard_map/all_gather | solution.py:58
  3312.4 737.6 %copy-start.6 = (bf16[4096]{0:T(1024)(128)(2,1)S(1)}, bf16[4096]{0:T(1024)(128)(2,1)}, u32[]{:S(2)}) copy-start(bf16[4096]{0:T(1024)(128)(2,1)} %param.19) | copy-start | bytes 24580
  3312.4 737.6 %copy-start.9 = (s32[4]{0:T(128)S(1)}, s32[4]{0:T(128)}, u32[]{:S(2)}) copy-start(s32[4]{0:T(128)} %param.15) | copy-start | bytes 52
  4492.4 707.6 %copy-start.7 = (s32[4]{0:T(128)S(1)}, s32[4]{0:T(128)}, u32[]{:S(2)}) copy-start(s32[4]{0:T(128)} %param.16) | copy-start | bytes 52
Sparse Core Ops, SparseCore 0:
  28.1 31.6 all-gather.15
  61.9 31.4 all-gather.17
  107.2 142.1 all-gather.13
  250.8 104.1 all-gather.19
  703.4 1295.4 all-gather.29
  2000.3 341.7 all-gather.23
  2343.6 343.1 all-gather.21
  2688.4 343.1 all-gather.25
  3289.8 1114.2 all-gather.31
  4405.5 752.8 all-gather.27
where the time goes:
time: 5470 us; the launch traced here: 5450 us
  waiting for transfers between devices  1830 us (33%)
  blocking collectives  1530 us (28%)
  matrix products  1250 us (23%)
  local copies, waits for them, and re-layouts  444 us (8%)
  other arithmetic  236 us (4%)
  starting transfers between devices  145 us (3%)
    all_to_all x6, blocking collectives, col_layout(): own_rows = lax.all_to_all(shard_mat, 'tp', 1, 0, tiled=True)  1520 us
    all_gather x6, waiting for transfers between devices, col_layout(): return lax.all_gather(own_rows, 'dp', axis=0, tiled=True)  1030 us
    all_gather x2, waiting for transfers between devices, add_partials(): gathered = lax.all_gather(partial, 'tp', axis=0)  729 us
    unnamed x34, local copies, waits for them, and re-layouts  289 us
    dot_general x1, matrix products, gated_mlp(): gate_proj = jnp.dot(normed, gate_weight, preferred_element_type=jnp.float32)  270 us
    dot_general x1, matrix products, device_program(): jnp.dot(mlp_act, down_weight, preferred_element_type=jnp.float32)  258 us
    dot_general x1, matrix products, gated_mlp(): up_proj = jnp.dot(normed, up_weight, preferred_element_type=jnp.float32)  257 us
    ppermute x2, starting transfers between devices, row_layout(): placed = lax.ppermute(shard_mat, ('tp', 'dp'), perm_pairs)  144 us
  transfers between devices with their start and end apart: 12, of which 7 were waited for; matrix products, arithmetic and copies ran while one was open for 23% of the time, Pallas kernels for 0%

commit v1 on v0

v1 whole, which is shorter than its diff:
```python
import functools

import jax
import jax.numpy as jnp
from jax import lax
from jax.experimental import pallas as pl
from jax.experimental.pallas import tpu as pltpu
from jax.sharding import PartitionSpec as P


HEAD_DIM = 128
RMS_EPS = 1e-5
ROPE_BASE = 10000.0
SLOTS = 8
LAG = 4
TILE_BYTES = 1 << 20

HEAD_CUTS = (0, 256, 384, 448, 480, 512)
HEAD_TILE = 128
LOGIT_ROWS = 16


def rms_norm(hidden, gain):
    hidden_f32 = hidden.astype(jnp.float32)
    inv_rms = lax.rsqrt(jnp.mean(hidden_f32 * hidden_f32, axis=-1, keepdims=True) + RMS_EPS)
    return (hidden_f32 * inv_rms * gain.astype(jnp.float32)).astype(jnp.bfloat16)


def rotate(projected, cosines, sines):
    half_dim = HEAD_DIM // 2
    first_half = projected[..., :half_dim]
    second_half = projected[..., half_dim:]
    return jnp.concatenate([first_half * cosines - second_half * sines, second_half * cosines + first_half * sines], axis=-1)


def angles_at(positions):
    inv_freq = ROPE_BASE ** (-jnp.arange(HEAD_DIM // 2, dtype=jnp.float32) * (2.0 / HEAD_DIM))
    angles = positions.astype(jnp.float32)[..., None, None] * inv_freq
    return jnp.cos(angles), jnp.sin(angles)


def place_kernel(steps, n_in, n_alias, n_out, slot_of, *refs):
    ins = refs[:n_in]
    outs = refs[n_in + n_alias : n_in + n_alias + n_out]
    buf, in_sem, out_sem = refs[n_in + n_alias + n_out :]
    me = lax.axis_index("dp") * 2 + lax.axis_index("tp")

    def load(s):
        piece, row, rows, cols, _ = steps[s]
        slot = s % SLOTS
        return pltpu.make_async_copy(ins[piece].at[pl.ds(row, rows)], buf.at[slot, pl.ds(0, rows), pl.ds(0, cols)], in_sem.at[slot])

    def stores(s):
        piece, row, rows, _, dests = steps[s]
        slot = s % SLOTS
        for out, base, stride, first, width in dests:
            at = base + slot_of(piece, me) * stride + row
            yield pltpu.make_async_copy(
                buf.at[slot, pl.ds(0, rows), pl.ds(first, width)],
                outs[out].at[pl.ds(pl.multiple_of(at, 8), rows)],
                out_sem.at[slot],
            )

    total = len(steps)
    for s in range(total + LAG):
        if s < total:
            if s >= SLOTS:
                for copy in stores(s - SLOTS):
                    copy.wait()
            load(s).start()
        if s >= LAG:
            load(s - LAG).wait()
            for copy in stores(s - LAG):
                copy.start()
    for s in range(max(0, total - SLOTS), total):
        for copy in stores(s):
            copy.wait()


def place(pieces, outputs, slot_of, stride, base=0, into=None):
    rows, cols = pieces[0].shape
    tile = rows
    while tile * cols * 2 > TILE_BYTES and tile % 16 == 0:
        tile //= 2
    steps = []
    for piece in range(len(pieces)):
        for row in range(0, rows, tile):
            dests = [(out, base, stride, first, shape[1]) for out, (shape, first) in enumerate(outputs)]
            steps.append((piece, row, tile, cols, dests))
    alias = [] if into is None else list(into)
    return pl.pallas_call(
        functools.partial(place_kernel, steps, len(pieces), len(alias), len(outputs), slot_of),
        out_shape=[jax.ShapeDtypeStruct(shape, jnp.bfloat16) for shape, _ in outputs],
        in_specs=[pl.BlockSpec(memory_space=pl.ANY)] * (len(pieces) + len(alias)),
        out_specs=[pl.BlockSpec(memory_space=pl.ANY)] * len(outputs),
        scratch_shapes=[
            pltpu.VMEM((SLOTS, tile, cols), jnp.bfloat16),
            pltpu.SemaphoreType.DMA((SLOTS,)),
            pltpu.SemaphoreType.DMA((SLOTS,)),
        ],
        input_output_aliases={len(pieces) + k: k for k in range(len(alias))},
        compiler_params=pltpu.CompilerParams(vmem_limit_bytes=24 << 20),
    )(*pieces, *alias)


def head_kernel(rows, tile, n_in, n_alias, slot_of, *refs):
    z_ref, acc_ref = refs[:2]
    ins = refs[2 : 2 + n_in]
    out_ref, logits_ref, buf, in_sem, out_sem = refs[2 + n_in + n_alias :]
    me = lax.axis_index("dp") * 2 + lax.axis_index("tp")
    base, block, slots, lag = rows
    cols = out_ref.shape[1]
    steps = [(piece, row) for piece in range(n_in) for row in range(0, ins[0].shape[0], tile)]

    def load(s):
        piece, row = steps[s]
        slot = s % slots
        return pltpu.make_async_copy(ins[piece].at[pl.ds(row, tile)], buf.at[slot], in_sem.at[slot])

    def store(s):
        piece, row = steps[s]
        slot = s % slots
        at = pl.multiple_of(slot_of(piece, me) * block + base + row, 8)
        return pltpu.make_async_copy(buf.at[slot], out_ref.at[pl.ds(at, tile)], out_sem.at[slot])

    logits_ref[...] = acc_ref[...]
    width = cols // 5
    total = len(steps)
    for s in range(total + lag):
        if s < total:
            if s >= slots:
                store(s - slots).wait()
            load(s).start()
        if s >= lag:
            done = s - lag
            piece, row = steps[done]
            load(done).wait()
            store(done).start()
            z = z_ref[slot_of(piece, me)][:, row : row + tile]

            @pl.loop(0, 5)
            def _(j, z=z, slot=done % slots):
                at = pl.ds(pl.multiple_of(j * width, 128), width)
                logits_ref[:, at] += jnp.dot(z, buf[slot, :, at], preferred_element_type=jnp.float32)

    for s in range(max(0, total - slots), total):
        store(s).wait()


def place_head(pieces, shape, slot_of, block, base, z, acc, into):
    rows, cols = pieces[0].shape
    tile = min(rows, HEAD_TILE)
    slots, lag = 5, 2
    alias = [] if into is None else [into]
    any_spec = pl.BlockSpec(memory_space=pl.ANY)
    vmem = pl.BlockSpec(memory_space=pltpu.VMEM)
    return pl.pallas_call(
        functools.partial(head_kernel, (base, block, slots, lag), tile, len(pieces), len(alias), slot_of),
        out_shape=[jax.ShapeDtypeStruct(shape, jnp.bfloat16), jax.ShapeDtypeStruct(acc.shape, jnp.float32)],
        in_specs=[vmem, vmem] + [any_spec] * (len(pieces) + len(alias)),
        out_specs=[any_spec, vmem],
        scratch_shapes=[
            pltpu.VMEM((slots, tile, cols), jnp.bfloat16),
            pltpu.SemaphoreType.DMA((slots,)),
            pltpu.SemaphoreType.DMA((slots,)),
        ],
        input_output_aliases={2 + len(pieces): 0} if alias else {},
        compiler_params=pltpu.CompilerParams(vmem_limit_bytes=40 << 20),
    )(z, acc, *pieces, *alias)


def solution(mesh):
    tp_size = mesh.shape["tp"]
    dp_size = mesh.shape["dp"]
    train_spec = P(None, ("dp", "tp"), None)
    col_spec = P(None, None, "tp")
    row_spec = P(None, "tp", None)
    cache_spec = P(None, "dp", "tp", None, None)
    x_pairs = [(i, i ^ 2) for i in range(dp_size)]
    core_pairs = [(i, i ^ 1) for i in range(dp_size)]
    y_pairs = [(0, 1), (1, 0)]

    def over_x(value):
        return lax.ppermute(value, "dp", x_pairs)

    def over_y(value):
        return lax.ppermute(value, "tp", y_pairs)

    def over_core(value):
        return lax.ppermute(value, "dp", core_pairs)

    def layer_program(prompts, lengths, targets, norm_attn, norm_mlp, norm_final, w_query, w_key, w_value, w_out, w_gate, w_up, w_down, w_head):
        tp_idx = lax.axis_index("tp")
        dp_idx = lax.axis_index("dp")

        def halves(mats, rows=None):
            own, other = [], []
            for mat in mats:
                first, last = (0, mat.shape[0]) if rows is None else rows
                half = mat.shape[1] // 2
                own.append(lax.dynamic_slice(mat, (first, tp_idx * half), (last - first, half)))
                other.append(lax.dynamic_slice(mat, (first, (1 - tp_idx) * half), (last - first, half)))
            return jnp.concatenate(own, 1), jnp.concatenate(other, 1)

        def column_pieces(mats, rows=None):
            own, other = halves(mats, rows)
            far = over_y(other)
            own_x = over_x(own)
            far_x = over_x(far)
            return [
                own, far, over_core(own), over_core(far),
                own_x, far_x, over_core(own_x), over_core(far_x),
            ]

        def row_pieces(mat):
            aligned = (dp_idx // 2) == tp_idx
            from_x = over_x(mat)
            far = over_y(jnp.where(aligned, from_x, mat))
            near = jnp.where(aligned, mat, from_x)
            return [near, far, over_core(near), over_core(far)]

        def column_slot(piece, me):
            slot = 0
            for bit in (1, 2, 4):
                mine = (me // bit) % 2
                slot = slot + (mine if not piece & bit else 1 - mine) * bit
            return slot

        def row_slot(piece, me):
            core = (me // 2) % 2
            tp = me % 2
            core = core if not piece & 2 else 1 - core
            tp = tp if not piece & 1 else 1 - tp
            return 2 * core + tp

        block = w_head.shape[0]
        model = block * tp_size * dp_size
        kv_half = w_key.shape[2] // 2
        q_half = w_query.shape[2] // 2
        ffn_half = w_gate.shape[2] // 2
        vocab_half = w_head.shape[1] // 2

        o_pieces = row_pieces(w_out[0])
        kvq = column_pieces([w_key[0], w_value[0], w_query[0]])
        k_weight, v_weight, q_weight = place(
            kvq, [((model, kv_half), 0), ((model, kv_half), kv_half), ((model, q_half), 2 * kv_half)], column_slot, block
        )
        gate = column_pieces([w_gate[0]])
        up = column_pieces([w_up[0]])
        (o_weight,) = place(o_pieces, [((q_half, model), 0)], row_slot, block)
        (gate_weight,) = place(gate, [((model, ffn_half), 0)], column_slot, block)
        (up_weight,) = place(up, [((model, ffn_half), 0)], column_slot, block)
        down = row_pieces(w_down[0])
        (down_weight,) = place(down, [((ffn_half, model), 0)], row_slot, w_down.shape[1])

        batch, seq_len, _ = prompts.shape
        kv_count = kv_half // HEAD_DIM
        q_count = q_half // HEAD_DIM
        normed = rms_norm(prompts, norm_attn[0])
        cosines, sines = angles_at(jnp.arange(seq_len))
        keys_raw = jnp.dot(normed, k_weight, preferred_element_type=jnp.float32).reshape(batch, seq_len, kv_count, HEAD_DIM)
        values = jnp.dot(normed, v_weight, preferred_element_type=jnp.float32).astype(jnp.bfloat16).reshape(batch, seq_len, kv_count, HEAD_DIM)
        keys = jnp.transpose(rotate(keys_raw, cosines, sines).astype(jnp.bfloat16), (0, 2, 1, 3))
        values = jnp.transpose(values, (0, 2, 1, 3))

        last = lengths - 1
        hidden = jnp.take_along_axis(prompts, last[:, None, None], axis=1)[:, 0]
        normed_last = rms_norm(hidden, norm_attn[0])
        cos_last, sin_last = angles_at(last)
        queries = jnp.dot(normed_last, q_weight, preferred_element_type=jnp.float32).reshape(batch, q_count, HEAD_DIM)
        queries = rotate(queries, cos_last, sin_last).astype(jnp.bfloat16).reshape(batch, kv_count, q_count // kv_count, HEAD_DIM)
        scores = jnp.einsum("bkgh,bksh->bkgs", queries, keys, preferred_element_type=jnp.float32) * HEAD_DIM ** -0.5
        seen = jnp.arange(seq_len)[None, :]
        key_ok = (seen <= last[:, None]) & (seen < lengths[:, None])
        probs = jax.nn.softmax(jnp.where(key_ok[:, None, None], scores, -1e30), axis=-1).astype(jnp.bfloat16)
        attn = jnp.einsum("bkgs,bksh->bkgh", probs, values, preferred_element_type=jnp.float32)
        attn = attn.astype(jnp.bfloat16).reshape(batch, q_half)

        def add_partials(hidden, partial):
            gathered = lax.all_gather(partial, "tp", axis=0)
            return (hidden.astype(jnp.float32) + jnp.sum(gathered.astype(jnp.float32), axis=0)).astype(jnp.bfloat16)

        hidden = add_partials(hidden, jnp.dot(attn, o_weight, preferred_element_type=jnp.float32).astype(jnp.bfloat16))
        normed_mlp = rms_norm(hidden, norm_mlp[0])
        gate_proj = jnp.dot(normed_mlp, gate_weight, preferred_element_type=jnp.float32)
        up_proj = jnp.dot(normed_mlp, up_weight, preferred_element_type=jnp.float32)
        act = (jax.nn.silu(gate_proj) * up_proj).astype(jnp.bfloat16)
        hidden = add_partials(hidden, jnp.dot(act, down_weight, preferred_element_type=jnp.float32).astype(jnp.bfloat16))
        final = rms_norm(hidden, norm_final)

        per_block = jnp.transpose(final.reshape(batch, -1, block), (1, 0, 2))
        per_block = jnp.pad(per_block, ((0, 0), (0, LOGIT_ROWS - batch), (0, 0)))
        head = None
        acc = jnp.zeros((LOGIT_ROWS, vocab_half), jnp.float32)
        for first, last in zip(HEAD_CUTS, HEAD_CUTS[1:]):
            pieces = column_pieces([w_head], (first, last))
            z = per_block[:, :, first:last]
            head, acc = place_head(pieces, (model, vocab_half), column_slot, block, first, z, acc, head)
        logits = acc[:batch]

        vocab_ids = tp_idx * vocab_half + jnp.arange(vocab_half)
        local_lse = jax.nn.logsumexp(logits, axis=-1)
        local_picked = jnp.sum(jnp.where(vocab_ids[None, :] == targets[:, None], logits, 0.0), axis=-1)
        both = lax.all_gather(jnp.stack([local_lse, local_picked]), "tp", axis=0)
        logprobs = jnp.sum(both[:, 1], axis=0) - jax.nn.logsumexp(both[:, 0], axis=0)
        return (
            q_weight[None], k_weight[None], v_weight[None], o_weight[None], gate_weight[None], up_weight[None], down_weight[None],
            head, keys[None], values[None], logprobs,
        )

    return jax.shard_map(
        layer_program,
        mesh=mesh,
        in_specs=(P("dp", None, None), P("dp"), P("dp"), P(), P(), P(), train_spec, train_spec, train_spec, train_spec, train_spec, train_spec, train_spec, P(("dp", "tp"), None)),
        out_specs=(col_spec, col_spec, col_spec, row_spec, col_spec, col_spec, row_spec, P(None, "tp"), cache_spec, cache_spec, P("dp")),
        check_vma=False,
    )
```

time: 5470 us -> 2340 us (0.43)
  blocking collectives: 1530 us -> 13.4 us
  matrix products: 1250 us -> 129 us
  local copies, waits for them, and re-layouts: 444 us -> 164 us
  Pallas kernels: 0 us -> 223 us
  other arithmetic: 236 us -> 57 us
  starting transfers between devices: 145 us -> 34.6 us
  waiting for transfers between devices: 1830 us -> 1720 us
    all_gather x10 -> x0, waiting for transfers between devices: 1830 us -> none  [the longest x6 1030 us: col_layout(): return lax.all_gather(own_rows, 'dp', axis=0, tiled=True)]
    ppermute x2 -> x64, waiting for transfers between devices: 0.01 us -> 1720 us  [the longest x18 940 us: over_x(): return lax.ppermute(value, 'dp', x_pairs)]
    all_to_all x6 -> x0, blocking collectives: 1520 us -> none  [col_layout(): own_rows = lax.all_to_all(shard_mat, 'tp', 1, 0, tiled=True)]
    dot_general x9 -> x8, matrix products: 1120 us -> 129 us  [the longest x1 38.2 us: layer_program(): jnp.dot(act, down_weight, preferred_element_type=jnp.float32)]
    pallas_call x0 -> x10, Pallas kernels: none -> 223 us  [the longest x5 128 us: place(): pl.pallas_call(functools.partial(place_kernel, steps, len(pieces), len(al...]
    unnamed x34 -> x163, local copies, waits for them, and re-layouts: 289 us -> 74.9 us
    sub x1 -> x0, matrix products: 127 us -> none  [attention(): jax.nn.softmax(jnp.where(key_ok, scores, -1e+30), axis=-1)]
    all_to_all x9 -> x0, local copies, waits for them, and re-layouts: 117 us -> none  [col_layout(): own_rows = lax.all_to_all(shard_mat, 'tp', 1, 0, tiled=True)]
  transfers between devices with their start and end apart: 12 -> 64, of which waited for: 7 -> 20; matrix products, arithmetic and copies ran while one was open for 23% -> 12% of each run, Pallas kernels for 0% -> 9%
where the time goes in v1:
time: 2340 us
  waiting for transfers between devices  1720 us (74%)
  Pallas kernels  223 us (10%)
  local copies, waits for them, and re-layouts  164 us (7%)
  matrix products  129 us (6%)
  other arithmetic  57 us (2%)
  starting transfers between devices  34.6 us (1%)
    ppermute x18, waiting for transfers between devices, over_x(): return lax.ppermute(value, 'dp', x_pairs)  940 us
    ppermute x10, waiting for transfers between devices, over_y(): return lax.ppermute(value, 'tp', y_pairs)  763 us
    pallas_call x5, Pallas kernels, place(): pl.pallas_call(functools.partial(place_kernel, steps, len(pieces), len(al...  128 us
    pallas_call x5, Pallas kernels, place_head(): pl.pallas_call(functools.partial(head_kernel, (base, block, slots, lag),...  95.3 us
    unnamed x163, local copies, waits for them, and re-layouts  74.9 us
    dynamic_slice x8, local copies, waits for them, and re-layouts, halves(): lax.dynamic_slice(mat, (first, (1 - tp_idx) * half), (last - first, half))  50.4 us
  transfers between devices with their start and end apart: 64, of which 20 were waited for; matrix products, arithmetic and copies ran while one was open for 12% of the time, Pallas kernels for 9%

profile of v1, /device:TPU:0, one launch (start us, length us, event | category | flops | bytes accessed | tf_op | source)
XLA Modules:
  0.0 2337.3 jit_solution(15644455002869632670)
XLA Ops:
  0.7 3.4 constant_dynamic-slice_fusion.2
  4.0 3.3 collective-permute-start.53
  8.9 3.8 constant_dynamic-slice_fusion.6
  13.3 19.5 collective-permute-done.50.refs_3_
  35.9 2.6 dynamic-slice_bitcast_fusion.6
  38.5 4.1 dynamic-slice_bitcast_fusion.4
  44.7 53.7 %collective-permute-done.57.refs_3_ = bf16[32,16000]{1,0:T(8,128)(2,1)} collective-permute-done((bf16[32,16000]{1,0:T(8,128)(2,1)}, bf16[32,16000]{1,0:T(8,128)(2,1)}, u32[]{:S(2)}, u32[]{:S(2)}) %collective-permute-start.57) | collective-permute-done | bytes 1024032 | tf_op jit(solution)/shard_map/ppermute | solution.py:187
  102.4 5.9 constant_dynamic-slice_fusion.8
  108.3 17.0 collective-permute-done.54.refs_7_
  131.9 15.5 collective-permute-done.61.refs_7_
  147.4 22.1 collective-permute-done.refs_1_
  169.5 45.2 %collective-permute-done.3.refs_4_ = bf16[512,3072]{1,0:T(8,128)(2,1)S(1)} collective-permute-done((bf16[512,3072]{1,0:T(8,128)(2,1)S(1)}, bf16[512,3072]{1,0:T(8,128)(2,1)S(1)}, u32[]{:S(2)}, u32[]{:S(2)}) %collective-permute-start.3) | collective-permute-done | bytes 3145760 | tf_op jit(solution)/shard_map/ppermute | solution.py:184
  218.4 37.7 %collective-permute-done.36.refs_3_ = bf16[128,16000]{1,0:T(8,128)(2,1)} collective-permute-done((bf16[128,16000]{1,0:T(8,128)(2,1)}, bf16[128,16000]{1,0:T(8,128)(2,1)}, u32[]{:S(2)}, u32[]{:S(2)}) %collective-permute-start.36) | collective-permute-done | bytes 4096032 | tf_op jit(solution)/shard_map/ppermute | solution.py:187
  256.6 46.0 %collective-permute-done.39.refs_6_ = bf16[128,16000]{1,0:T(8,128)(2,1)} collective-permute-done((bf16[128,16000]{1,0:T(8,128)(2,1)S(1)}, bf16[128,16000]{1,0:T(8,128)(2,1)}, u32[]{:S(2)}, u32[]{:S(2)}) %collective-permute-start.39) | collective-permute-done | bytes 4096032 | tf_op jit(solution)/shard_map/ppermute | solution.py:184
  305.0 444.3 %collective-permute-done.47.refs_7_ = bf16[64,16000]{1,0:T(8,128)(2,1)} collective-permute-done((bf16[64,16000]{1,0:T(8,128)(2,1)}, bf16[64,16000]{1,0:T(8,128)(2,1)}, u32[]{:S(2)}, u32[]{:S(2)}) %collective-permute-start.47) | collective-permute-done | bytes 2048032 | tf_op jit(solution)/shard_map/ppermute | solution.py:184
  750.1 8.8 dynamic-slice_bitcast_fusion
  759.5 60.6 %collective-permute-done.4.refs_5_ = bf16[512,3072]{1,0:T(8,128)(2,1)S(1)} collective-permute-done((bf16[512,3072]{1,0:T(8,128)(2,1)}, bf16[512,3072]{1,0:T(8,128)(2,1)S(1)}, u32[]{:S(2)}, u32[]{:S(2)}) %collective-permute-start.4) | collective-permute-done | bytes 3145760 | tf_op jit(solution)/shard_map/ppermute | solution.py:184
  823.5 10.4 dynamic-slice_bitcast_fusion.2
  834.5 85.7 %collective-permute-done.18.refs_1_ = bf16[512,7168]{1,0:T(8,128)(2,1)} collective-permute-done((bf16[512,7168]{1,0:T(8,128)(2,1)}, bf16[512,7168]{1,0:T(8,128)(2,1)}, u32[]{:S(2)}, u32[]{:S(2)}) %collective-permute-start.18) | collective-permute-done | bytes 7340064 | tf_op jit(solution)/shard_map/ppermute | solution.py:187
  921.6 11.3 constant_dynamic-slice_fusion
  933.0 48.0 %collective-permute-done.21.refs_4_ = bf16[512,7168]{1,0:T(8,128)(2,1)S(1)} collective-permute-done((bf16[512,7168]{1,0:T(8,128)(2,1)S(1)}, bf16[512,7168]{1,0:T(8,128)(2,1)S(1)}, u32[]{:S(2)}, u32[]{:S(2)}) %collective-permute-start.21) | collective-permute-done | bytes 7340064 | tf_op jit(solution)/shard_map/ppermute | solution.py:184
  983.9 2.9 copy-done.9
  986.8 90.6 %collective-permute-done.11.refs_1_ = bf16[512,7168]{1,0:T(8,128)(2,1)} collective-permute-done((bf16[512,7168]{1,0:T(8,128)(2,1)}, bf16[512,7168]{1,0:T(8,128)(2,1)}, u32[]{:S(2)}, u32[]{:S(2)}) %collective-permute-start.11) | collective-permute-done | bytes 7340064 | tf_op jit(solution)/shard_map/ppermute | solution.py:187
  1078.9 21.2 broadcast_select_fusion
  1100.2 38.2 %collective-permute-done.14.refs_4_ = bf16[512,7168]{1,0:T(8,128)(2,1)} collective-permute-done((bf16[512,7168]{1,0:T(8,128)(2,1)}, bf16[512,7168]{1,0:T(8,128)(2,1)}, u32[]{:S(2)}, u32[]{:S(2)}) %collective-permute-start.14) | collective-permute-done | bytes 7340064 | tf_op jit(solution)/shard_map/ppermute | solution.py:184
  1138.9 2.8 broadcast_select_fusion.2
  1142.9 110.1 %collective-permute-done.29.refs_3_ = bf16[256,16000]{1,0:T(8,128)(2,1)} collective-permute-done((bf16[256,16000]{1,0:T(8,128)(2,1)}, bf16[256,16000]{1,0:T(8,128)(2,1)}, u32[]{:S(2)}, u32[]{:S(2)}) %collective-permute-start.29) | collective-permute-done | bytes 8192032 | tf_op jit(solution)/shard_map/ppermute | solution.py:187
  1255.1 57.5 %collective-permute-done.32.refs_6_ = bf16[256,16000]{1,0:T(8,128)(2,1)S(1)} collective-permute-done((bf16[256,16000]{1,0:T(8,128)(2,1)}, bf16[256,16000]{1,0:T(8,128)(2,1)S(1)}, u32[]{:S(2)}, u32[]{:S(2)}) %collective-permute-start.32) | collective-permute-done | bytes 8192032 | tf_op jit(solution)/shard_map/ppermute | solution.py:184
  1313.1 343.6 %collective-permute-done.8.refs_1_ = bf16[512,4096]{1,0:T(8,128)(2,1)S(1)} collective-permute-done((bf16[512,4096]{1,0:T(8,128)(2,1)S(1)}, bf16[512,4096]{1,0:T(8,128)(2,1)S(1)}, u32[]{:S(2)}, u32[]{:S(2)}) %collective-permute-start.8) | collective-permute-done | bytes 4194336 | tf_op jit(solution)/shard_map/ppermute | solution.py:187
  1661.1 11.3 fusion.1
  1672.5 12.6 collective-permute-done.10.refs_3_
  1693.0 3.0 multiply_cosine_fusion
  1709.8 8.7 shard_map.221
  1718.5 21.2 copy.47
  1739.7 24.5 %fusion.6 = f32[4,1024,512]{1,2,0:T(8,128)} fusion(bf16[4,1024,4096]{2,1,0:T(8,128)(2,1)} %param.14, f32[4096]{0:T(1024)S(1)} %bitcast.130, f32[4,1024]{1,0:T(4,128)S(1)} %add_rsqrt_fusion, bf16[4096,512]{1,0:T(8,128)(2,1)} %get-tuple-element.25), kind=kOutput, calls=%fused_computation.8 | convolution fusion | flops 17246978048 | bytes 46170112 | tf_op jit(solution)/shard_map/dot_general | solution.py:261
  1764.3 83.1 %collective-permute-done.15.refs_5_ = bf16[512,7168]{1,0:T(8,128)(2,1)} collective-permute-done((bf16[512,7168]{1,0:T(8,128)(2,1)}, bf16[512,7168]{1,0:T(8,128)(2,1)}, u32[]{:S(2)}, u32[]{:S(2)}) %collective-permute-start.15) | collective-permute-done | bytes 7340064 | tf_op jit(solution)/shard_map/ppermute | solution.py:184
  1848.9 8.2 fusion.45
  1857.1 8.5 fusion.71
  1865.7 6.9 copy.50
  1872.5 6.9 copy.51
  1880.0 24.3 %fusion.16 = bf16[4,1024,512]{1,2,0:T(8,128)(2,1)} fusion(bf16[4096,512]{1,0:T(8,128)(2,1)} %get-tuple-element.26, bf16[4,1024,4096]{2,1,0:T(8,128)(2,1)} %param.14, f32[4096]{0:T(1024)S(1)} %bitcast.132, f32[4,1024]{1,0:T(4,128)S(1)} %add_rsqrt_fusion), kind=kOutput, calls=%fused_computation.32 | convolution fusion | flops 17249075200 | bytes 41975808 | tf_op jit(solution)/shard_map/dot_general | solution.py:262
  1904.4 6.3 copy.44
  1910.7 7.1 subtract_convert_fusion
  1922.3 2.9 fusion.29
  1934.2 6.8 shard_map.222
  1940.9 84.2 %collective-permute-done.33.refs_7_ = bf16[256,16000]{1,0:T(8,128)(2,1)} collective-permute-done((bf16[256,16000]{1,0:T(8,128)(2,1)}, bf16[256,16000]{1,0:T(8,128)(2,1)}, u32[]{:S(2)}, u32[]{:S(2)}) %collective-permute-start.33) | collective-permute-done | bytes 8192032 | tf_op jit(solution)/shard_map/ppermute | solution.py:184
  2026.6 8.0 fusion.9
  2035.7 4.6 all-gather.3
  2041.0 3.1 copy-done.10
  2044.1 36.5 %shard_map.224 = bf16[4096,7168]{1,0:T(8,128)(2,1)} custom-call(bf16[512,7168]{1,0:T(8,128)(2,1)S(1)} %bitcast.112, bf16[512,7168]{1,0:T(8,128)(2,1)} %collective-permute-done.18.refs_1_, bf16[512,7168]{1,0:T(8,128)(2,1)S(1)} %copy-done.10, bf16[512,7168]{1,0:T(8,128)(2,1)} %collective-permute-done.20.refs_3_, bf16[512,7168]{1,0:T(8,128)(2,1)} %copy-done.60, ...), custom_call_target="tpu_custom_call" | custom-call | tf_op jit(solution)/shard_map/pallas_call | solution.py:91
  2080.5 39.9 %shard_map.223 = bf16[4096,7168]{1,0:T(8,128)(2,1)} custom-call(bf16[512,7168]{1,0:T(8,128)(2,1)} %get-tuple-element.60.refs_0_, bf16[512,7168]{1,0:T(8,128)(2,1)} %collective-permute-done.11.refs_1_, bf16[512,7168]{1,0:T(8,128)(2,1)} %collective-permute-done.12.refs_2_, bf16[512,7168]{1,0:T(8,128)(2,1)} %collective-permute-done.13.refs_3_, ...), custom_call_target="tpu_custom_call" | custom-call | tf_op jit(solution)/shard_map/pallas_call | solution.py:91
  2120.4 20.0 fusion.62
  2140.4 5.2 copy-done
  2145.6 36.1 %shard_map.225 = bf16[7168,4096]{1,0:T(8,128)(2,1)} custom-call(bf16[1792,4096]{1,0:T(8,128)(2,1)S(1)} %copy-done, bf16[1792,4096]{1,0:T(8,128)(2,1)} %collective-permute-done.26.refs_1_, bf16[1792,4096]{1,0:T(8,128)(2,1)} %collective-permute-done.27.refs_2_, bf16[1792,4096]{1,0:T(8,128)(2,1)} %collective-permute-done.28.refs_3_), custom_call_target="tpu_custom_call" | custom-call | tf_op jit(solution)/shard_map/pallas_call | solution.py:91
  2182.3 38.2 %fusion.8 = bf16[1,4,4096]{2,1,0:T(4,128)(2,1)S(1)} fusion(bf16[7168,4096]{1,0:T(8,128)(2,1)} %shard_map.225, f32[4,7168]{1,0:T(4,128)S(1)} %fusion.62, bf16[4096,7168]{1,0:T(8,128)(2,1)} %shard_map.223, bf16[4,4096]{1,0:T(4,128)(2,1)S(1)} %get-tuple-element.42, f32[4096]{0:T(1024)S(1)} %bitcast.127, f32[4]{0:T(128)S(1)} %add_rsqrt_fusion.2), kind=kOutput, calls=%fused_computation.19 | convolution fusion | flops 470016000 | bytes 117637136 | tf_op jit(solution)/shard_map/dot_general | solution.py:288
  2220.5 4.6 all-gather.4
  2226.7 3.3 copy-done.1
  2230.0 42.5 %shard_map.226 = (bf16[4096,16000]{1,0:T(8,128)(2,1)}, f32[16,16000]{1,0:T(8,128)S(1)}) custom-call(bf16[8,16,256]{2,1,0:T(8,128)(2,1)S(1)} %pad_slice_fusion.refs_0_, f32[16,16000]{1,0:T(8,128)S(1)} %broadcast_in_dim.104.refs_1_, bf16[256,16000]{1,0:T(8,128)(2,1)S(1)} %copy-done.1, bf16[256,16000]{1,0:T(8,128)(2,1)} %collective-permute-done.29.refs_3_, ...), custom_call_target="tpu_custom_call" | custom-call | tf_op jit(solution)/shard_map/pallas_call | solution.py:157
  2272.5 21.0 shard_map.227
  2295.8 13.7 shard_map.228
  2309.6 9.2 shard_map.229
  2319.0 8.9 shard_map.230
  2328.6 3.7 fusion.32
  2332.2 4.2 all-gather.5
  (310 shorter events, 90.6 us)
Async XLA Ops:
  4.0 28.8 %collective-permute-start.53 = (bf16[32,16000]{1,0:T(8,128)(2,1)S(1)}, bf16[32,16000]{1,0:T(8,128)(2,1)S(1)}, u32[]{:S(2)}, u32[]{:S(2)}) collective-permute-start(bf16[32,16000]{1,0:T(8,128)(2,1)S(1)} %get-tuple-element.45.refs_2_), channel_id=1, source_target_pairs={{0,2},{1,3},{2,0},{3,1},{4,6},{5,7},{6,4},{7,5}} | collective-permute-start | bytes 3072008 | tf_op jit(solution)/shard_map/ppermute | solution.py:184
  7.3 27.1 %collective-permute-start.51 = (bf16[32,16000]{1,0:T(8,128)(2,1)S(1)}, bf16[32,16000]{1,0:T(8,128)(2,1)S(1)}, u32[]{:S(2)}, u32[]{:S(2)}) collective-permute-start(bf16[32,16000]{1,0:T(8,128)(2,1)S(1)} %get-tuple-element.45.refs_2_), channel_id=1, source_target_pairs={{0,1},{1,0},{2,3},{3,2},{4,5},{5,4},{6,7},{7,6}} | collective-permute-start | bytes 3072008 | tf_op jit(solution)/shard_map/ppermute | solution.py:190
  7.3 25.5 %collective-permute-start.50 = (bf16[32,16000]{1,0:T(8,128)(2,1)S(1)}, bf16[32,16000]{1,0:T(8,128)(2,1)S(1)}, u32[]{:S(2)}, u32[]{:S(2)}) collective-permute-start(bf16[32,16000]{1,0:T(8,128)(2,1)S(1)} %get-tuple-element.44), channel_id=1, source_target_pairs={{0,4},{4,0},{1,5},{5,1},{2,6},{6,2},{3,7},{7,3}} | collective-permute-start | bytes 3072008 | tf_op jit(solution)/shard_map/ppermute | solution.py:187
  12.6 87.8 %collective-permute-start.43 = (bf16[64,16000]{1,0:T(8,128)(2,1)}, bf16[64,16000]{1,0:T(8,128)(2,1)}, u32[]{:S(2)}, u32[]{:S(2)}) collective-permute-start(bf16[64,16000]{1,0:T(8,128)(2,1)} %get-tuple-element.47), channel_id=1, source_target_pairs={{0,4},{4,0},{1,5},{5,1},{2,6},{6,2},{3,7},{7,3}} | collective-permute-start | bytes 6144008 | tf_op jit(solution)/shard_map/ppermute | solution.py:187
  13.1 87.3 %collective-permute-start.46 = (bf16[64,16000]{1,0:T(8,128)(2,1)S(1)}, bf16[64,16000]{1,0:T(8,128)(2,1)}, u32[]{:S(2)}, u32[]{:S(2)}) collective-permute-start(bf16[64,16000]{1,0:T(8,128)(2,1)S(1)} %get-tuple-element.48.refs_2_), channel_id=1, source_target_pairs={{0,2},{1,3},{2,0},{3,1},{4,6},{5,7},{6,4},{7,5}} | collective-permute-start | bytes 6144008 | tf_op jit(solution)/shard_map/ppermute | solution.py:184
  32.9 68.1 %collective-permute-start.44 = (bf16[64,16000]{1,0:T(8,128)(2,1)S(1)}, bf16[64,16000]{1,0:T(8,128)(2,1)}, u32[]{:S(2)}, u32[]{:S(2)}) collective-permute-start(bf16[64,16000]{1,0:T(8,128)(2,1)S(1)} %get-tuple-element.48.refs_2_), channel_id=1, source_target_pairs={{0,1},{1,0},{2,3},{3,2},{4,5},{5,4},{6,7},{7,6}} | collective-permute-start | bytes 6144008 | tf_op jit(solution)/shard_map/ppermute | solution.py:190
  32.9 65.5 %collective-permute-start.57 = (bf16[32,16000]{1,0:T(8,128)(2,1)}, bf16[32,16000]{1,0:T(8,128)(2,1)}, u32[]{:S(2)}, u32[]{:S(2)}) collective-permute-start(bf16[32,16000]{1,0:T(8,128)(2,1)} %get-tuple-element.43), channel_id=1, source_target_pairs={{0,4},{4,0},{1,5},{5,1},{2,6},{6,2},{3,7},{7,3}} | collective-permute-start | bytes 3072008 | tf_op jit(solution)/shard_map/ppermute | solution.py:187
  35.4 64.5 %collective-permute-start.60 = (bf16[32,16000]{1,0:T(8,128)(2,1)S(1)}, bf16[32,16000]{1,0:T(8,128)(2,1)}, u32[]{:S(2)}, u32[]{:S(2)}) collective-permute-start(bf16[32,16000]{1,0:T(8,128)(2,1)S(1)} %get-tuple-element.46.refs_2_), channel_id=1, source_target_pairs={{0,2},{1,3},{2,0},{3,1},{4,6},{5,7},{6,4},{7,5}} | collective-permute-start | bytes 3072008 | tf_op jit(solution)/shard_map/ppermute | solution.py:184
  98.3 71.2 %collective-permute-start = (bf16[512,3072]{1,0:T(8,128)(2,1)}, bf16[512,3072]{1,0:T(8,128)(2,1)S(1)}, u32[]{:S(2)}, u32[]{:S(2)}) collective-permute-start(bf16[512,3072]{1,0:T(8,128)(2,1)} %pad_maximum_fusion.2), channel_id=1, source_target_pairs={{0,4},{4,0},{1,5},{5,1},{2,6},{6,2},{3,7},{7,3}} | collective-permute-start | bytes 9437192 | tf_op jit(solution)/shard_map/ppermute | solution.py:187
  99.9 25.5 %collective-permute-start.54 = (bf16[32,16000]{1,0:T(8,128)(2,1)S(1)}, bf16[32,16000]{1,0:T(8,128)(2,1)S(1)}, u32[]{:S(2)}, u32[]{:S(2)}) collective-permute-start(bf16[32,16000]{1,0:T(8,128)(2,1)S(1)} %copy-done.45), channel_id=1, source_target_pairs={{0,2},{1,3},{2,0},{3,1},{4,6},{5,7},{6,4},{7,5}} | collective-permute-start | bytes 3072008 | tf_op jit(solution)/shard_map/ppermute | solution.py:184
  100.4 28.9 %collective-permute-start.52 = (bf16[32,16000]{1,0:T(8,128)(2,1)S(1)}, bf16[32,16000]{1,0:T(8,128)(2,1)S(1)}, u32[]{:S(2)}, u32[]{:S(2)}) collective-permute-start(bf16[32,16000]{1,0:T(8,128)(2,1)S(1)} %copy-done.45), channel_id=1, source_target_pairs={{0,1},{1,0},{2,3},{3,2},{4,5},{5,4},{6,7},{7,6}} | collective-permute-start | bytes 3072008 | tf_op jit(solution)/shard_map/ppermute | solution.py:190
  100.4 27.5 %collective-permute-start.55 = (bf16[32,16000]{1,0:T(8,128)(2,1)S(1)}, bf16[32,16000]{1,0:T(8,128)(2,1)S(1)}, u32[]{:S(2)}, u32[]{:S(2)}) collective-permute-start(bf16[32,16000]{1,0:T(8,128)(2,1)S(1)} %copy-done.40), channel_id=1, source_target_pairs={{0,1},{1,0},{2,3},{3,2},{4,5},{5,4},{6,7},{7,6}} | collective-permute-start | bytes 3072008 | tf_op jit(solution)/shard_map/ppermute | solution.py:190
  100.9 46.5 %collective-permute-start.61 = (bf16[32,16000]{1,0:T(8,128)(2,1)}, bf16[32,16000]{1,0:T(8,128)(2,1)}, u32[]{:S(2)}, u32[]{:S(2)}) collective-permute-start(bf16[32,16000]{1,0:T(8,128)(2,1)} %collective-permute-done.57.refs_3_), channel_id=1, source_target_pairs={{0,2},{1,3},{2,0},{3,1},{4,6},{5,7},{6,4},{7,5}} | collective-permute-start | bytes 3072008 | tf_op jit(solution)/shard_map/ppermute | solution.py:184
  125.4 130.7 %collective-permute-start.36 = (bf16[128,16000]{1,0:T(8,128)(2,1)}, bf16[128,16000]{1,0:T(8,128)(2,1)}, u32[]{:S(2)}, u32[]{:S(2)}) collective-permute-start(bf16[128,16000]{1,0:T(8,128)(2,1)} %get-tuple-element.49), channel_id=1, source_target_pairs={{0,4},{4,0},{1,5},{5,1},{2,6},{6,2},{3,7},{7,3}} | collective-permute-start | bytes 12288008 | tf_op jit(solution)/shard_map/ppermute | solution.py:187
  128.9 85.8 %collective-permute-start.3 = (bf16[512,3072]{1,0:T(8,128)(2,1)S(1)}, bf16[512,3072]{1,0:T(8,128)(2,1)S(1)}, u32[]{:S(2)}, u32[]{:S(2)}) collective-permute-start(bf16[512,3072]{1,0:T(8,128)(2,1)S(1)} %pad_maximum_fusion.1.refs_0_), channel_id=1, source_target_pairs={{0,2},{1,3},{2,0},{3,1},{4,6},{5,7},{6,4},{7,5}} | collective-permute-start | bytes 9437192 | tf_op jit(solution)/shard_map/ppermute | solution.py:184
  130.3 172.3 %collective-permute-start.39 = (bf16[128,16000]{1,0:T(8,128)(2,1)S(1)}, bf16[128,16000]{1,0:T(8,128)(2,1)}, u32[]{:S(2)}, u32[]{:S(2)}) collective-permute-start(bf16[128,16000]{1,0:T(8,128)(2,1)S(1)} %get-tuple-element.50.refs_2_), channel_id=1, source_target_pairs={{0,2},{1,3},{2,0},{3,1},{4,6},{5,7},{6,4},{7,5}} | collective-permute-start | bytes 12288008 | tf_op jit(solution)/shard_map/ppermute | solution.py:184
  147.4 155.2 %collective-permute-start.37 = (bf16[128,16000]{1,0:T(8,128)(2,1)S(1)}, bf16[128,16000]{1,0:T(8,128)(2,1)S(1)}, u32[]{:S(2)}, u32[]{:S(2)}) collective-permute-start(bf16[128,16000]{1,0:T(8,128)(2,1)S(1)} %get-tuple-element.50.refs_2_), channel_id=1, source_target_pairs={{0,1},{1,0},{2,3},{3,2},{4,5},{5,4},{6,7},{7,6}} | collective-permute-start | bytes 12288008 | tf_op jit(solution)/shard_map/ppermute | solution.py:190
  169.5 45.7 %collective-permute-start.1 = (bf16[512,3072]{1,0:T(8,128)(2,1)S(1)}, bf16[512,3072]{1,0:T(8,128)(2,1)S(1)}, u32[]{:S(2)}, u32[]{:S(2)}) collective-permute-start(bf16[512,3072]{1,0:T(8,128)(2,1)S(1)} %pad_maximum_fusion.1.refs_0_), channel_id=1, source_target_pairs={{0,1},{1,0},{2,3},{3,2},{4,5},{5,4},{6,7},{7,6}} | collective-permute-start | bytes 9437192 | tf_op jit(solution)/shard_map/ppermute | solution.py:190
  214.7 544.2 %collective-permute-start.7 = (bf16[512,4096]{1,0:T(8,128)(2,1)}, bf16[512,4096]{1,0:T(8,128)(2,1)}, u32[]{:S(2)}, u32[]{:S(2)}) collective-permute-start(bf16[512,4096]{1,0:T(8,128)(2,1)} %bitcast.122), channel_id=1, source_target_pairs={{0,2},{1,3},{2,0},{3,1},{4,6},{5,7},{6,4},{7,5}} | collective-permute-start | bytes 12582920 | tf_op jit(solution)/shard_map/ppermute | solution.py:184
  217.3 861.7 %collective-permute-start.25 = (bf16[1792,4096]{1,0:T(8,128)(2,1)}, bf16[1792,4096]{1,0:T(8,128)(2,1)}, u32[]{:S(2)}, u32[]{:S(2)}) collective-permute-start(bf16[1792,4096]{1,0:T(8,128)(2,1)} %bitcast.120), channel_id=1, source_target_pairs={{0,2},{1,3},{2,0},{3,1},{4,6},{5,7},{6,4},{7,5}} | collective-permute-start | bytes 44040200 | tf_op jit(solution)/shard_map/ppermute | solution.py:184
  256.1 493.3 %collective-permute-start.47 = (bf16[64,16000]{1,0:T(8,128)(2,1)}, bf16[64,16000]{1,0:T(8,128)(2,1)}, u32[]{:S(2)}, u32[]{:S(2)}) collective-permute-start(bf16[64,16000]{1,0:T(8,128)(2,1)} %collective-permute-done.43.refs_3_), channel_id=1, source_target_pairs={{0,2},{1,3},{2,0},{3,1},{4,6},{5,7},{6,4},{7,5}} | collective-permute-start | bytes 6144008 | tf_op jit(solution)/shard_map/ppermute | solution.py:184
  302.6 446.8 %collective-permute-start.48 = (bf16[64,16000]{1,0:T(8,128)(2,1)}, bf16[64,16000]{1,0:T(8,128)(2,1)}, u32[]{:S(2)}, u32[]{:S(2)}) collective-permute-start(bf16[64,16000]{1,0:T(8,128)(2,1)} %collective-permute-done.46.refs_6_), channel_id=1, source_target_pairs={{0,1},{1,0},{2,3},{3,2},{4,5},{5,4},{6,7},{7,6}} | collective-permute-start | bytes 6144008 | tf_op jit(solution)/shard_map/ppermute | solution.py:190
  304.5 445.4 %collective-permute-start.45 = (bf16[64,16000]{1,0:T(8,128)(2,1)}, bf16[64,16000]{1,0:T(8,128)(2,1)}, u32[]{:S(2)}, u32[]{:S(2)}) collective-permute-start(bf16[64,16000]{1,0:T(8,128)(2,1)} %collective-permute-done.43.refs_3_), channel_id=1, source_target_pairs={{0,1},{1,0},{2,3},{3,2},{4,5},{5,4},{6,7},{7,6}} | collective-permute-start | bytes 6144008 | tf_op jit(solution)/shard_map/ppermute | solution.py:190
  749.4 10.1 collective-permute-start.49
  749.4 70.7 %collective-permute-start.4 = (bf16[512,3072]{1,0:T(8,128)(2,1)}, bf16[512,3072]{1,0:T(8,128)(2,1)S(1)}, u32[]{:S(2)}, u32[]{:S(2)}) collective-permute-start(bf16[512,3072]{1,0:T(8,128)(2,1)} %copy-done.23), channel_id=1, source_target_pairs={{0,2},{1,3},{2,0},{3,1},{4,6},{5,7},{6,4},{7,5}} | collective-permute-start | bytes 9437192 | tf_op jit(solution)/shard_map/ppermute | solution.py:184
  749.9 71.9 %collective-permute-start.5 = (bf16[512,3072]{1,0:T(8,128)(2,1)}, bf16[512,3072]{1,0:T(8,128)(2,1)S(1)}, u32[]{:S(2)}, u32[]{:S(2)}) collective-permute-start(bf16[512,3072]{1,0:T(8,128)(2,1)} %copy-done.26), channel_id=1, source_target_pairs={{0,1},{1,0},{2,3},{3,2},{4,5},{5,4},{6,7},{7,6}} | collective-permute-start | bytes 9437192 | tf_op jit(solution)/shard_map/ppermute | solution.py:190
  759.0 161.2 %collective-permute-start.18 = (bf16[512,7168]{1,0:T(8,128)(2,1)}, bf16[512,7168]{1,0:T(8,128)(2,1)}, u32[]{:S(2)}, u32[]{:S(2)}) collective-permute-start(bf16[512,7168]{1,0:T(8,128)(2,1)} %get-tuple-element.57), channel_id=1, source_target_pairs={{0,4},{4,0},{1,5},{5,1},{2,6},{6,2},{3,7},{7,3}} | collective-permute-start | bytes 22020104 | tf_op jit(solution)/shard_map/ppermute | solution.py:187
  759.5 74.4 %collective-permute-start.2 = (bf16[512,3072]{1,0:T(8,128)(2,1)S(1)}, bf16[512,3072]{1,0:T(8,128)(2,1)S(1)}, u32[]{:S(2)}, u32[]{:S(2)}) collective-permute-start(bf16[512,3072]{1,0:T(8,128)(2,1)S(1)} %copy-done.24), channel_id=1, source_target_pairs={{0,1},{1,0},{2,3},{3,2},{4,5},{5,4},{6,7},{7,6}} | collective-permute-start | bytes 9437192 | tf_op jit(solution)/shard_map/ppermute | solution.py:190
  820.1 160.9 %collective-permute-start.21 = (bf16[512,7168]{1,0:T(8,128)(2,1)S(1)}, bf16[512,7168]{1,0:T(8,128)(2,1)S(1)}, u32[]{:S(2)}, u32[]{:S(2)}) collective-permute-start(bf16[512,7168]{1,0:T(8,128)(2,1)S(1)} %get-tuple-element.58.refs_0_), channel_id=1, source_target_pairs={{0,2},{1,3},{2,0},{3,1},{4,6},{5,7},{6,4},{7,5}} | collective-permute-start | bytes 22020104 | tf_op jit(solution)/shard_map/ppermute | solution.py:184
  823.5 158.0 %collective-permute-start.19 = (bf16[512,7168]{1,0:T(8,128)(2,1)S(1)}, bf16[512,7168]{1,0:T(8,128)(2,1)S(1)}, u32[]{:S(2)}, u32[]{:S(2)}) collective-permute-start(bf16[512,7168]{1,0:T(8,128)(2,1)S(1)} %get-tuple-element.58.refs_0_), channel_id=1, source_target_pairs={{0,1},{1,0},{2,3},{3,2},{4,5},{5,4},{6,7},{7,6}} | collective-permute-start | bytes 22020104 | tf_op jit(solution)/shard_map/ppermute | solution.py:190
  833.9 243.5 %collective-permute-start.11 = (bf16[512,7168]{1,0:T(8,128)(2,1)}, bf16[512,7168]{1,0:T(8,128)(2,1)}, u32[]{:S(2)}, u32[]{:S(2)}) collective-permute-start(bf16[512,7168]{1,0:T(8,128)(2,1)} %get-tuple-element.59), channel_id=1, source_target_pairs={{0,4},{4,0},{1,5},{5,1},{2,6},{6,2},{3,7},{7,3}} | collective-permute-start | bytes 22020104 | tf_op jit(solution)/shard_map/ppermute | solution.py:187
  920.1 218.2 %collective-permute-start.14 = (bf16[512,7168]{1,0:T(8,128)(2,1)}, bf16[512,7168]{1,0:T(8,128)(2,1)}, u32[]{:S(2)}, u32[]{:S(2)}) collective-permute-start(bf16[512,7168]{1,0:T(8,128)(2,1)} %get-tuple-element.60.refs_0_), channel_id=1, source_target_pairs={{0,2},{1,3},{2,0},{3,1},{4,6},{5,7},{6,4},{7,5}} | collective-permute-start | bytes 22020104 | tf_op jit(solution)/shard_map/ppermute | solution.py:184
  981.0 272.0 %collective-permute-start.29 = (bf16[256,16000]{1,0:T(8,128)(2,1)}, bf16[256,16000]{1,0:T(8,128)(2,1)}, u32[]{:S(2)}, u32[]{:S(2)}) collective-permute-start(bf16[256,16000]{1,0:T(8,128)(2,1)} %get-tuple-element.51), channel_id=1, source_target_pairs={{0,4},{4,0},{1,5},{5,1},{2,6},{6,2},{3,7},{7,3}} | collective-permute-start | bytes 24576008 | tf_op jit(solution)/shard_map/ppermute | solution.py:187
  986.8 154.8 %collective-permute-start.12 = (bf16[512,7168]{1,0:T(8,128)(2,1)}, bf16[512,7168]{1,0:T(8,128)(2,1)}, u32[]{:S(2)}, u32[]{:S(2)}) collective-permute-start(bf16[512,7168]{1,0:T(8,128)(2,1)} %get-tuple-element.60.refs_0_), channel_id=1, source_target_pairs={{0,1},{1,0},{2,3},{3,2},{4,5},{5,4},{6,7},{7,6}} | collective-permute-start | bytes 22020104 | tf_op jit(solution)/shard_map/ppermute | solution.py:190
  1077.4 235.1 %collective-permute-start.32 = (bf16[256,16000]{1,0:T(8,128)(2,1)}, bf16[256,16000]{1,0:T(8,128)(2,1)S(1)}, u32[]{:S(2)}, u32[]{:S(2)}) collective-permute-start(bf16[256,16000]{1,0:T(8,128)(2,1)} %get-tuple-element.52.refs_2_), channel_id=1, source_target_pairs={{0,2},{1,3},{2,0},{3,1},{4,6},{5,7},{6,4},{7,5}} | collective-permute-start | bytes 24576008 | tf_op jit(solution)/shard_map/ppermute | solution.py:184
  1078.9 233.6 %collective-permute-start.30 = (bf16[256,16000]{1,0:T(8,128)(2,1)}, bf16[256,16000]{1,0:T(8,128)(2,1)}, u32[]{:S(2)}, u32[]{:S(2)}) collective-permute-start(bf16[256,16000]{1,0:T(8,128)(2,1)} %get-tuple-element.52.refs_2_), channel_id=1, source_target_pairs={{0,1},{1,0},{2,3},{3,2},{4,5},{5,4},{6,7},{7,6}} | collective-permute-start | bytes 24576008 | tf_op jit(solution)/shard_map/ppermute | solution.py:190
  1138.4 557.7 %collective-permute-start.26 = (bf16[1792,4096]{1,0:T(8,128)(2,1)}, bf16[1792,4096]{1,0:T(8,128)(2,1)}, u32[]{:S(2)}, u32[]{:S(2)}) collective-permute-start(bf16[1792,4096]{1,0:T(8,128)(2,1)} %get-tuple-element.53), channel_id=1, source_target_pairs={{0,4},{4,0},{1,5},{5,1},{2,6},{6,2},{3,7},{7,3}} | collective-permute-start | bytes 44040200 | tf_op jit(solution)/shard_map/ppermute | solution.py:187
  1141.6 515.0 %collective-permute-start.8 = (bf16[512,4096]{1,0:T(8,128)(2,1)S(1)}, bf16[512,4096]{1,0:T(8,128)(2,1)S(1)}, u32[]{:S(2)}, u32[]{:S(2)}) collective-permute-start(bf16[512,4096]{1,0:T(8,128)(2,1)S(1)} %get-tuple-element.63), channel_id=1, source_target_pairs={{0,4},{4,0},{1,5},{5,1},{2,6},{6,2},{3,7},{7,3}} | collective-permute-start | bytes 12582920 | tf_op jit(solution)/shard_map/ppermute | solution.py:187
  1253.0 403.7 %collective-permute-start.9 = (bf16[512,4096]{1,0:T(8,128)(2,1)S(1)}, bf16[512,4096]{1,0:T(8,128)(2,1)S(1)}, u32[]{:S(2)}, u32[]{:S(2)}) collective-permute-start(bf16[512,4096]{1,0:T(8,128)(2,1)S(1)} %get-tuple-element.64.refs_0_), channel_id=1, source_target_pairs={{0,1},{1,0},{2,3},{3,2},{4,5},{5,4},{6,7},{7,6}} | collective-permute-start | bytes 12582920 | tf_op jit(solution)/shard_map/ppermute | solution.py:190
  1312.6 346.9 %collective-permute-start.6 = (bf16[512,3072]{1,0:T(8,128)(2,1)S(1)}, bf16[512,3072]{1,0:T(8,128)(2,1)S(1)}, u32[]{:S(2)}, u32[]{:S(2)}) collective-permute-start(bf16[512,3072]{1,0:T(8,128)(2,1)S(1)} %copy-done.31), channel_id=1, source_target_pairs={{0,1},{1,0},{2,3},{3,2},{4,5},{5,4},{6,7},{7,6}} | collective-permute-start | bytes 9437192 | tf_op jit(solution)/shard_map/ppermute | solution.py:190
  1312.6 379.1 %collective-permute-start.22 = (bf16[512,7168]{1,0:T(8,128)(2,1)}, bf16[512,7168]{1,0:T(8,128)(2,1)}, u32[]{:S(2)}, u32[]{:S(2)}) collective-permute-start(bf16[512,7168]{1,0:T(8,128)(2,1)} %collective-permute-done.18.refs_1_), channel_id=1, source_target_pairs={{0,2},{1,3},{2,0},{3,1},{4,6},{5,7},{6,4},{7,5}} | collective-permute-start | bytes 22020104 | tf_op jit(solution)/shard_map/ppermute | solution.py:184
  1656.7 35.8 %collective-permute-start.23 = (bf16[512,7168]{1,0:T(8,128)(2,1)}, bf16[512,7168]{1,0:T(8,128)(2,1)}, u32[]{:S(2)}, u32[]{:S(2)}) collective-permute-start(bf16[512,7168]{1,0:T(8,128)(2,1)} %copy-done.60), channel_id=1, source_target_pairs={{0,1},{1,0},{2,3},{3,2},{4,5},{5,4},{6,7},{7,6}} | collective-permute-start | bytes 22020104 | tf_op jit(solution)/shard_map/ppermute | solution.py:190
  1658.7 37.3 %collective-permute-start.20 = (bf16[512,7168]{1,0:T(8,128)(2,1)}, bf16[512,7168]{1,0:T(8,128)(2,1)}, u32[]{:S(2)}, u32[]{:S(2)}) collective-permute-start(bf16[512,7168]{1,0:T(8,128)(2,1)} %collective-permute-done.18.refs_1_), channel_id=1, source_target_pairs={{0,1},{1,0},{2,3},{3,2},{4,5},{5,4},{6,7},{7,6}} | collective-permute-start | bytes 22020104 | tf_op jit(solution)/shard_map/ppermute | solution.py:190
  1661.1 23.9 %collective-permute-start.10 = (bf16[512,4096]{1,0:T(8,128)(2,1)S(1)}, bf16[512,4096]{1,0:T(8,128)(2,1)S(1)}, u32[]{:S(2)}, u32[]{:S(2)}) collective-permute-start(bf16[512,4096]{1,0:T(8,128)(2,1)S(1)} %collective-permute-done.8.refs_1_), channel_id=1, source_target_pairs={{0,1},{1,0},{2,3},{3,2},{4,5},{5,4},{6,7},{7,6}} | collective-permute-start | bytes 12582920 | tf_op jit(solution)/shard_map/ppermute | solution.py:190
  1687.0 160.3 %collective-permute-start.15 = (bf16[512,7168]{1,0:T(8,128)(2,1)}, bf16[512,7168]{1,0:T(8,128)(2,1)}, u32[]{:S(2)}, u32[]{:S(2)}) collective-permute-start(bf16[512,7168]{1,0:T(8,128)(2,1)} %collective-permute-done.11.refs_1_), channel_id=1, source_target_pairs={{0,2},{1,3},{2,0},{3,1},{4,6},{5,7},{6,4},{7,5}} | collective-permute-start | bytes 22020104 | tf_op jit(solution)/shard_map/ppermute | solution.py:184
  1691.7 165.4 %collective-permute-start.16 = (bf16[512,7168]{1,0:T(8,128)(2,1)}, bf16[512,7168]{1,0:T(8,128)(2,1)}, u32[]{:S(2)}, u32[]{:S(2)}) collective-permute-start(bf16[512,7168]{1,0:T(8,128)(2,1)} %collective-permute-done.14.refs_4_), channel_id=1, source_target_pairs={{0,1},{1,0},{2,3},{3,2},{4,5},{5,4},{6,7},{7,6}} | collective-permute-start | bytes 22020104 | tf_op jit(solution)/shard_map/ppermute | solution.py:190
  1692.5 187.0 %collective-permute-start.13 = (bf16[512,7168]{1,0:T(8,128)(2,1)}, bf16[512,7168]{1,0:T(8,128)(2,1)}, u32[]{:S(2)}, u32[]{:S(2)}) collective-permute-start(bf16[512,7168]{1,0:T(8,128)(2,1)} %collective-permute-done.11.refs_1_), channel_id=1, source_target_pairs={{0,1},{1,0},{2,3},{3,2},{4,5},{5,4},{6,7},{7,6}} | collective-permute-start | bytes 22020104 | tf_op jit(solution)/shard_map/ppermute | solution.py:190
  1696.0 339.1 %collective-permute-start.27 = (bf16[1792,4096]{1,0:T(8,128)(2,1)}, bf16[1792,4096]{1,0:T(8,128)(2,1)}, u32[]{:S(2)}, u32[]{:S(2)}) collective-permute-start(bf16[1792,4096]{1,0:T(8,128)(2,1)} %get-tuple-element.54.refs_0_), channel_id=1, source_target_pairs={{0,1},{1,0},{2,3},{3,2},{4,5},{5,4},{6,7},{7,6}} | collective-permute-start | bytes 44040200 | tf_op jit(solution)/shard_map/ppermute | solution.py:190
  1696.1 339.1 %collective-permute-start.28 = (bf16[1792,4096]{1,0:T(8,128)(2,1)}, bf16[1792,4096]{1,0:T(8,128)(2,1)}, u32[]{:S(2)}, u32[]{:S(2)}) collective-permute-start(bf16[1792,4096]{1,0:T(8,128)(2,1)} %collective-permute-done.26.refs_1_), channel_id=1, source_target_pairs={{0,1},{1,0},{2,3},{3,2},{4,5},{5,4},{6,7},{7,6}} | collective-permute-start | bytes 44040200 | tf_op jit(solution)/shard_map/ppermute | solution.py:190
  1847.4 177.7 %collective-permute-start.33 = (bf16[256,16000]{1,0:T(8,128)(2,1)}, bf16[256,16000]{1,0:T(8,128)(2,1)}, u32[]{:S(2)}, u32[]{:S(2)}) collective-permute-start(bf16[256,16000]{1,0:T(8,128)(2,1)} %collective-permute-done.29.refs_3_), channel_id=1, source_target_pairs={{0,2},{1,3},{2,0},{3,1},{4,6},{5,7},{6,4},{7,5}} | collective-permute-start | bytes 24576008 | tf_op jit(solution)/shard_map/ppermute | solution.py:184
  1857.1 169.5 %collective-permute-start.24 = (bf16[512,7168]{1,0:T(8,128)(2,1)}, bf16[512,7168]{1,0:T(8,128)(2,1)}, u32[]{:S(2)}, u32[]{:S(2)}) collective-permute-start(bf16[512,7168]{1,0:T(8,128)(2,1)} %collective-permute-done.22.refs_5_), channel_id=1, source_target_pairs={{0,1},{1,0},{2,3},{3,2},{4,5},{5,4},{6,7},{7,6}} | collective-permute-start | bytes 22020104 | tf_op jit(solution)/shard_map/ppermute | solution.py:190
  1879.5 155.1 %collective-permute-start.17 = (bf16[512,7168]{1,0:T(8,128)(2,1)}, bf16[512,7168]{1,0:T(8,128)(2,1)}, u32[]{:S(2)}, u32[]{:S(2)}) collective-permute-start(bf16[512,7168]{1,0:T(8,128)(2,1)} %collective-permute-done.15.refs_5_), channel_id=1, source_target_pairs={{0,1},{1,0},{2,3},{3,2},{4,5},{5,4},{6,7},{7,6}} | collective-permute-start | bytes 22020104 | tf_op jit(solution)/shard_map/ppermute | solution.py:190
  2025.1 156.7 %collective-permute-start.40 = (bf16[128,16000]{1,0:T(8,128)(2,1)}, bf16[128,16000]{1,0:T(8,128)(2,1)}, u32[]{:S(2)}, u32[]{:S(2)}) collective-permute-start(bf16[128,16000]{1,0:T(8,128)(2,1)} %collective-permute-done.36.refs_3_), channel_id=1, source_target_pairs={{0,2},{1,3},{2,0},{3,1},{4,6},{5,7},{6,4},{7,5}} | collective-permute-start | bytes 12288008 | tf_op jit(solution)/shard_map/ppermute | solution.py:184
  2026.6 155.2 %collective-permute-start.41 = (bf16[128,16000]{1,0:T(8,128)(2,1)}, bf16[128,16000]{1,0:T(8,128)(2,1)}, u32[]{:S(2)}, u32[]{:S(2)}) collective-permute-start(bf16[128,16000]{1,0:T(8,128)(2,1)} %collective-permute-done.39.refs_6_), channel_id=1, source_target_pairs={{0,1},{1,0},{2,3},{3,2},{4,5},{5,4},{6,7},{7,6}} | collective-permute-start | bytes 12288008 | tf_op jit(solution)/shard_map/ppermute | solution.py:190
  2034.7 191.1 %collective-permute-start.31 = (bf16[256,16000]{1,0:T(8,128)(2,1)}, bf16[256,16000]{1,0:T(8,128)(2,1)}, u32[]{:S(2)}, u32[]{:S(2)}) collective-permute-start(bf16[256,16000]{1,0:T(8,128)(2,1)} %collective-permute-done.29.refs_3_), channel_id=1, source_target_pairs={{0,1},{1,0},{2,3},{3,2},{4,5},{5,4},{6,7},{7,6}} | collective-permute-start | bytes 24576008 | tf_op jit(solution)/shard_map/ppermute | solution.py:190
  2035.2 190.5 %collective-permute-start.34 = (bf16[256,16000]{1,0:T(8,128)(2,1)}, bf16[256,16000]{1,0:T(8,128)(2,1)}, u32[]{:S(2)}, u32[]{:S(2)}) collective-permute-start(bf16[256,16000]{1,0:T(8,128)(2,1)} %copy-done.59), channel_id=1, source_target_pairs={{0,1},{1,0},{2,3},{3,2},{4,5},{5,4},{6,7},{7,6}} | collective-permute-start | bytes 24576008 | tf_op jit(solution)/shard_map/ppermute | solution.py:190
  2035.2 191.0 %collective-permute-start.35 = (bf16[256,16000]{1,0:T(8,128)(2,1)}, bf16[256,16000]{1,0:T(8,128)(2,1)}, u32[]{:S(2)}, u32[]{:S(2)}) collective-permute-start(bf16[256,16000]{1,0:T(8,128)(2,1)} %collective-permute-done.33.refs_7_), channel_id=1, source_target_pairs={{0,1},{1,0},{2,3},{3,2},{4,5},{5,4},{6,7},{7,6}} | collective-permute-start | bytes 24576008 | tf_op jit(solution)/shard_map/ppermute | solution.py:190
  2181.8 43.3 %collective-permute-start.38 = (bf16[128,16000]{1,0:T(8,128)(2,1)}, bf16[128,16000]{1,0:T(8,128)(2,1)}, u32[]{:S(2)}, u32[]{:S(2)}) collective-permute-start(bf16[128,16000]{1,0:T(8,128)(2,1)} %collective-permute-done.36.refs_3_), channel_id=1, source_target_pairs={{0,1},{1,0},{2,3},{3,2},{4,5},{5,4},{6,7},{7,6}} | collective-permute-start | bytes 12288008 | tf_op jit(solution)/shard_map/ppermute | solution.py:190
  2181.8 43.4 %collective-permute-start.42 = (bf16[128,16000]{1,0:T(8,128)(2,1)}, bf16[128,16000]{1,0:T(8,128)(2,1)}, u32[]{:S(2)}, u32[]{:S(2)}) collective-permute-start(bf16[128,16000]{1,0:T(8,128)(2,1)} %collective-permute-done.40.refs_7_), channel_id=1, source_target_pairs={{0,1},{1,0},{2,3},{3,2},{4,5},{5,4},{6,7},{7,6}} | collective-permute-start | bytes 12288008 | tf_op jit(solution)/shard_map/ppermute | solution.py:190
  2225.2 93.7 %collective-permute-start.58 = (bf16[32,16000]{1,0:T(8,128)(2,1)S(1)}, bf16[32,16000]{1,0:T(8,128)(2,1)S(1)}, u32[]{:S(2)}, u32[]{:S(2)}) collective-permute-start(bf16[32,16000]{1,0:T(8,128)(2,1)S(1)} %copy-done.20), channel_id=1, source_target_pairs={{0,1},{1,0},{2,3},{3,2},{4,5},{5,4},{6,7},{7,6}} | collective-permute-start | bytes 3072008 | tf_op jit(solution)/shard_map/ppermute | solution.py:190
  2225.2 93.7 %collective-permute-start.59 = (bf16[32,16000]{1,0:T(8,128)(2,1)}, bf16[32,16000]{1,0:T(8,128)(2,1)S(1)}, u32[]{:S(2)}, u32[]{:S(2)}) collective-permute-start(bf16[32,16000]{1,0:T(8,128)(2,1)} %collective-permute-done.57.refs_3_), channel_id=1, source_target_pairs={{0,1},{1,0},{2,3},{3,2},{4,5},{5,4},{6,7},{7,6}} | collective-permute-start | bytes 3072008 | tf_op jit(solution)/shard_map/ppermute | solution.py:190
  2225.7 93.2 %collective-permute-start.62 = (bf16[32,16000]{1,0:T(8,128)(2,1)}, bf16[32,16000]{1,0:T(8,128)(2,1)}, u32[]{:S(2)}, u32[]{:S(2)}) collective-permute-start(bf16[32,16000]{1,0:T(8,128)(2,1)} %collective-permute-done.60.refs_6_), channel_id=1, source_target_pairs={{0,1},{1,0},{2,3},{3,2},{4,5},{5,4},{6,7},{7,6}} | collective-permute-start | bytes 3072008 | tf_op jit(solution)/shard_map/ppermute | solution.py:190
  2225.7 83.8 %collective-permute-start.56 = (bf16[32,16000]{1,0:T(8,128)(2,1)S(1)}, bf16[32,16000]{1,0:T(8,128)(2,1)}, u32[]{:S(2)}, u32[]{:S(2)}) collective-permute-start(bf16[32,16000]{1,0:T(8,128)(2,1)S(1)} %copy-done.48), channel_id=1, source_target_pairs={{0,1},{1,0},{2,3},{3,2},{4,5},{5,4},{6,7},{7,6}} | collective-permute-start | bytes 3072008 | tf_op jit(solution)/shard_map/ppermute | solution.py:190
  2226.2 92.7 %collective-permute-start.63 = (bf16[32,16000]{1,0:T(8,128)(2,1)}, bf16[32,16000]{1,0:T(8,128)(2,1)}, u32[]{:S(2)}, u32[]{:S(2)}) collective-permute-start(bf16[32,16000]{1,0:T(8,128)(2,1)} %collective-permute-done.61.refs_7_), channel_id=1, source_target_pairs={{0,1},{1,0},{2,3},{3,2},{4,5},{5,4},{6,7},{7,6}} | collective-permute-start | bytes 3072008 | tf_op jit(solution)/shard_map/ppermute | solution.py:190
  (80 other events, 4561.5 us)

commit v2 on v1

--- a/solution.py
+++ b/solution.py
@@ -15,8 +15,9 @@
 LAG = 4
 TILE_BYTES = 1 << 20
 
-HEAD_CUTS = (0, 256, 384, 448, 480, 512)
-HEAD_TILE = 128
+HEAD_CUTS = (0, 64, 128, 192, 256, 320, 384, 448, 496, 512)
+HEAD_TILE = 256
+TOKEN_TILE = 256
 LOGIT_ROWS = 16
 
 
@@ -24,13 +25,6 @@
     hidden_f32 = hidden.astype(jnp.float32)
     inv_rms = lax.rsqrt(jnp.mean(hidden_f32 * hidden_f32, axis=-1, keepdims=True) + RMS_EPS)
     return (hidden_f32 * inv_rms * gain.astype(jnp.float32)).astype(jnp.bfloat16)
-
-
-def rotate(projected, cosines, sines):
-    half_dim = HEAD_DIM // 2
-    first_half = projected[..., :half_dim]
-    second_half = projected[..., half_dim:]
-    return jnp.concatenate([first_half * cosines - second_half * sines, second_half * cosines + first_half * sines], axis=-1)
 
 
 def angles_at(positions):
@@ -103,7 +97,138 @@
     )(*pieces, *alias)
 
 
-def head_kernel(rows, tile, n_in, n_alias, slot_of, *refs):
+def project_kernel(x_ref, gain_ref, w_ref, cos_ref, sin_ref, k_ref, v_ref, q_ref):
+    hidden = x_ref[0].astype(jnp.float32)
+    inv_rms = lax.rsqrt(jnp.mean(hidden * hidden, axis=-1, keepdims=True) + RMS_EPS)
+    normed = (hidden * inv_rms * gain_ref[...].astype(jnp.float32)).astype(jnp.bfloat16)
+
+    def turn(part):
+        return part * cos_ref[...] + pltpu.roll(part, HEAD_DIM // 2, 1) * sin_ref[...]
+
+    def four_at(number):
+        at = pl.ds(pl.multiple_of(number * 4 * HEAD_DIM, 4 * HEAD_DIM), 4 * HEAD_DIM)
+        four = jnp.dot(normed, w_ref[:, at], preferred_element_type=jnp.float32)
+        return [four[:, side * HEAD_DIM : (side + 1) * HEAD_DIM] for side in range(4)]
+
+    for side, part in enumerate(four_at(0)):
+        k_ref[0, side] = turn(part).astype(jnp.bfloat16)
+    for side, part in enumerate(four_at(1)):
+        v_ref[0, side] = part.astype(jnp.bfloat16)
+
+    @pl.loop(0, q_ref.shape[1] // 4)
+    def _(number):
+        for side, part in enumerate(four_at(number + 2)):
+            q_ref[0, 4 * number + side] = turn(part).astype(jnp.bfloat16)
+
+
+def project(prompts, gain, weight, kv_heads, cosines, sines):
+    batch, seq_len, model = prompts.shape
+    q_heads = weight.shape[1] // HEAD_DIM - 2 * kv_heads
+    tile = TOKEN_TILE
+    cos_both = jnp.concatenate([cosines, cosines], axis=-1)
+    sin_both = jnp.concatenate([-sines, sines], axis=-1)
+
+    def shape(heads):
+        return jax.ShapeDtypeStruct((batch, heads, seq_len, HEAD_DIM), jnp.bfloat16)
+
+    def out_spec(heads):
+        return pl.BlockSpec((1, heads, tile, HEAD_DIM), lambda b, i: (b, 0, i, 0))
+
+    angle_spec = pl.BlockSpec((tile, HEAD_DIM), lambda b, i: (i, 0))
+    counts = (kv_heads, kv_heads, q_heads)
+    return pl.pallas_call(
+        project_kernel,
+        grid=(batch, seq_len // tile),
+        out_shape=[shape(heads) for heads in counts],
+        in_specs=[
+            pl.BlockSpec((1, tile, model), lambda b, i: (b, i, 0)),
+            pl.BlockSpec((1, model), lambda b, i: (0, 0)),
+            pl.BlockSpec(weight.shape, lambda b, i: (0, 0), pipeline_mode=pl.Buffered(1)),
+            angle_spec,
+            angle_spec,
+        ],
+        out_specs=[out_spec(heads) for heads in counts],
+        compiler_params=pltpu.CompilerParams(vmem_limit_bytes=60 << 20),
+        cost_estimate=pl.CostEstimate(flops=2 * batch * seq_len * model * weight.shape[1], bytes_accessed=2 * prompts.size, transcendentals=0),
+        name="project",
+    )(prompts, gain, weight, cos_both, sin_both)
+
+
+def attend_kernel(prompt, length_ref, q_ref, k_ref, v_ref, o_ref):
+    block = pl.program_id(1)
+    rows = q_ref.shape[2]
+    length = length_ref[prompt]
+    for count in range(1, k_ref.shape[2] // rows + 1):
+
+        @pl.when(block == count - 1)
+        def _(count=count):
+            keys = count * rows
+
+            @pl.loop(0, q_ref.shape[1])
+            def _(head):
+                scores = lax.dot_general(
+                    q_ref[0, head], k_ref[0, 0, :keys], (((1,), (1,)), ((), ())), preferred_element_type=jnp.float32
+                ) * HEAD_DIM ** -0.5
+                query_pos = (count - 1) * rows + lax.broadcasted_iota(jnp.int32, (rows, keys), 0)
+                key_pos = lax.broadcasted_iota(jnp.int32, (rows, keys), 1)
+                scores = jnp.where((key_pos <= query_pos) & (key_pos < length), scores, -1e30)
+                weights = jnp.exp(scores - jnp.max(scores, axis=-1, keepdims=True))
+                probs = (weights * (1.0 / jnp.sum(weights, axis=-1, keepdims=True))).astype(jnp.bfloat16)
+                out = jnp.dot(probs, v_ref[0, 0, :keys], preferred_element_type=jnp.float32)
+                o_ref[:, pl.ds(pl.multiple_of(head * HEAD_DIM, HEAD_DIM), HEAD_DIM)] = out.astype(jnp.bfloat16)
+
+
+def attend(prompt, lengths, queries, keys, values):
+    _, q_heads, seq_len, _ = queries.shape
+    kv_heads = keys.shape[1]
+    group = q_heads // kv_heads
+    tile = TOKEN_TILE
+    kv_spec = pl.BlockSpec((1, 1, seq_len, HEAD_DIM), lambda h, i: (prompt, h, 0, 0))
+    return pl.pallas_call(
+        functools.partial(attend_kernel, prompt),
+        grid=(kv_heads, seq_len // tile),
+        out_shape=jax.ShapeDtypeStruct((seq_len, q_heads * HEAD_DIM), jnp.bfloat16),
+        in_specs=[
+            pl.BlockSpec(memory_space=pltpu.SMEM),
+            pl.BlockSpec((1, group, tile, HEAD_DIM), lambda h, i: (prompt, h, i, 0)),
+            kv_spec,
+            kv_spec,
+        ],
+        out_specs=pl.BlockSpec((tile, group * HEAD_DIM), lambda h, i: (i, h)),
+        compiler_params=pltpu.CompilerParams(vmem_limit_bytes=32 << 20),
+        cost_estimate=pl.CostEstimate(flops=4 * q_heads * seq_len * seq_len * HEAD_DIM, bytes_accessed=1 << 24, transcendentals=0),
+        name="attend",
+    )(lengths, queries, keys, values)
+
+
+def mix_kernel(x_ref, mine_ref, other_ref, gain_ref, hidden_ref, normed_ref):
+    total = mine_ref[...].astype(jnp.float32) + other_ref[...].astype(jnp.float32)
+    hidden = (x_ref[0].astype(jnp.float32) + total).astype(jnp.bfloat16)
+    hidden_ref[...] = hidden
+    wide = hidden.astype(jnp.float32)
+    inv_rms = lax.rsqrt(jnp.mean(wide * wide, axis=-1, keepdims=True) + RMS_EPS)
+    normed_ref[...] = (wide * inv_rms * gain_ref[...].astype(jnp.float32)).astype(jnp.bfloat16)
+
+
+def mix(prompt, prompts, mine, other, gain):
+    rows, model = mine.shape
+    tile = 128
+    spec = pl.BlockSpec((tile, model), lambda i: (i, 0))
+    shape = jax.ShapeDtypeStruct((rows, model), jnp.bfloat16)
+    return pl.pallas_call(
+        mix_kernel,
+        grid=(rows // tile,),
+        out_shape=[shape, shape],
+        in_specs=[pl.BlockSpec((1, tile, model), lambda i: (prompt, i, 0)), spec, spec, pl.BlockSpec((1, model), lambda i: (0, 0))],
+        out_specs=[spec, spec],
+        compiler_params=pltpu.CompilerParams(vmem_limit_bytes=32 << 20),
+        cost_estimate=pl.CostEstimate(flops=10 * rows * model, bytes_accessed=10 * rows * model, transcendentals=0),
+        name="mix",
+    )(prompts, mine, other, gain)
+
+
+def head_kernel(rows, tile, numbers, n_alias, slot_of, *refs):
+    n_in = len(numbers)
     z_ref, acc_ref = refs[:2]
     ins = refs[2 : 2 + n_in]
     out_ref, logits_ref, buf, in_sem, out_sem = refs[2 + n_in + n_alias :]
@@ -120,7 +245,7 @@
     def store(s):
         piece, row = steps[s]
         slot = s % slots
-        at = pl.multiple_of(slot_of(piece, me) * block + base + row, 8)
+        at = pl.multiple_of(slot_of(numbers[piece], me) * block + base + row, 8)
         return pltpu.make_async_copy(buf.at[slot], out_ref.at[pl.ds(at, tile)], out_sem.at[slot])
 
     logits_ref[...] = acc_ref[...]
@@ -136,7 +261,7 @@
             piece, row = steps[done]
             load(done).wait()
             store(done).start()
-            z = z_ref[slot_of(piece, me)][:, row : row + tile]
+            z = z_ref[slot_of(numbers[piece], me)][:, row : row + tile]
 
             @pl.loop(0, 5)
             def _(j, z=z, slot=done % slots):
@@ -147,15 +272,15 @@
         store(s).wait()
 
 
-def place_head(pieces, shape, slot_of, block, base, z, acc, into):
+def place_head(numbers, pieces, shape, slot_of, block, base, z, acc, into):
     rows, cols = pieces[0].shape
     tile = min(rows, HEAD_TILE)
-    slots, lag = 5, 2
+    slots, lag = (4, 2) if tile > 128 else (8, 4)
     alias = [] if into is None else [into]
     any_spec = pl.BlockSpec(memory_space=pl.ANY)
     vmem = pl.BlockSpec(memory_space=pltpu.VMEM)
     return pl.pallas_call(
-        functools.partial(head_kernel, (base, block, slots, lag), tile, len(pieces), len(alias), slot_of),
+        functools.partial(head_kernel, (base, block, slots, lag), tile, numbers, len(alias), slot_of),
         out_shape=[jax.ShapeDtypeStruct(shape, jnp.bfloat16), jax.ShapeDtypeStruct(acc.shape, jnp.float32)],
         in_specs=[vmem, vmem] + [any_spec] * (len(pieces) + len(alias)),
         out_specs=[any_spec, vmem],
@@ -165,7 +290,7 @@
             pltpu.SemaphoreType.DMA((slots,)),
         ],
         input_output_aliases={2 + len(pieces): 0} if alias else {},
-        compiler_params=pltpu.CompilerParams(vmem_limit_bytes=40 << 20),
+        compiler_params=pltpu.CompilerParams(vmem_limit_bytes=48 << 20),
     )(z, acc, *pieces, *alias)
 
 
@@ -215,8 +340,9 @@
         def row_pieces(mat):
             aligned = (dp_idx // 2) == tp_idx
             from_x = over_x(mat)
-            far = over_y(jnp.where(aligned, from_x, mat))
+            sent = jnp.where(aligned, from_x, mat)
             near = jnp.where(aligned, mat, from_x)
+            far = over_y(sent)
             return [near, far, over_core(near), over_core(far)]
 
         def column_slot(piece, me):
@@ -242,8 +368,11 @@
 
         o_pieces = row_pieces(w_out[0])
         kvq = column_pieces([w_key[0], w_value[0], w_query[0]])
-        k_weight, v_weight, q_weight = place(
-            kvq, [((model, kv_half), 0), ((model, kv_half), kv_half), ((model, q_half), 2 * kv_half)], column_slot, block
+        whole_q = 2 * kv_half + q_half
+        k_weight, v_weight, q_weight, kvq_weight = place(
+            kvq,
+            [((model, kv_half), 0), ((model, kv_half), kv_half), ((model, q_half), 2 * kv_half), ((model, whole_q), 0)],
+            column_slot, block,
         )
         gate = column_pieces([w_gate[0]])
         up = column_pieces([w_up[0]])
@@ -255,54 +384,56 @@
 
         batch, seq_len, _ = prompts.shape
         kv_count = kv_half // HEAD_DIM
-        q_count = q_half // HEAD_DIM
-        normed = rms_norm(prompts, norm_attn[0])
         cosines, sines = angles_at(jnp.arange(seq_len))
-        keys_raw = jnp.dot(normed, k_weight, preferred_element_type=jnp.float32).reshape(batch, seq_len, kv_count, HEAD_DIM)
-        values = jnp.dot(normed, v_weight, preferred_element_type=jnp.float32).astype(jnp.bfloat16).reshape(batch, seq_len, kv_count, HEAD_DIM)
-        keys = jnp.transpose(rotate(keys_raw, cosines, sines).astype(jnp.bfloat16), (0, 2, 1, 3))
-        values = jnp.transpose(values, (0, 2, 1, 3))
+        keys, values, queries = project(prompts, norm_attn, kvq_weight, kv_count, cosines[:, 0], sines[:, 0])
+
+        hidden, partials = [], []
+        for n in range(batch):
+            attn = attend(n, lengths, queries, keys, values)
+            partial = jnp.dot(attn, o_weight, preferred_element_type=jnp.float32).astype(jnp.bfloat16)
+            other = over_y(partial)
+            hidden_n, normed_mlp = mix(n, prompts, partial, other, norm_mlp)
+            hidden.append(hidden_n)
+            gate_proj = jnp.dot(normed_mlp, gate_weight, preferred_element_type=jnp.float32)
+            up_proj = jnp.dot(normed_mlp, up_weight, preferred_element_type=jnp.float32)
+            act = (jax.nn.silu(gate_proj) * up_proj).astype(jnp.bfloat16)
+            partials.append(jnp.dot(act, down_weight, preferred_element_type=jnp.float32).astype(jnp.bfloat16))
 
         last = lengths - 1
-        hidden = jnp.take_along_axis(prompts, last[:, None, None], axis=1)[:, 0]
-        normed_last = rms_norm(hidden, norm_attn[0])
-        cos_last, sin_last = angles_at(last)
-        queries = jnp.dot(normed_last, q_weight, preferred_element_type=jnp.float32).reshape(batch, q_count, HEAD_DIM)
-        queries = rotate(queries, cos_last, sin_last).astype(jnp.bfloat16).reshape(batch, kv_count, q_count // kv_count, HEAD_DIM)
-        scores = jnp.einsum("bkgh,bksh->bkgs", queries, keys, preferred_element_type=jnp.float32) * HEAD_DIM ** -0.5
-        seen = jnp.arange(seq_len)[None, :]
-        key_ok = (seen <= last[:, None]) & (seen < lengths[:, None])
-        probs = jax.nn.softmax(jnp.where(key_ok[:, None, None], scores, -1e30), axis=-1).astype(jnp.bfloat16)
-        attn = jnp.einsum("bkgs,bksh->bkgh", probs, values, preferred_element_type=jnp.float32)
-        attn = attn.astype(jnp.bfloat16).reshape(batch, q_half)
-
-        def add_partials(hidden, partial):
-            gathered = lax.all_gather(partial, "tp", axis=0)
-            return (hidden.astype(jnp.float32) + jnp.sum(gathered.astype(jnp.float32), axis=0)).astype(jnp.bfloat16)
-
-        hidden = add_partials(hidden, jnp.dot(attn, o_weight, preferred_element_type=jnp.float32).astype(jnp.bfloat16))
-        normed_mlp = rms_norm(hidden, norm_mlp[0])
-        gate_proj = jnp.dot(normed_mlp, gate_weight, preferred_element_type=jnp.float32)
-        up_proj = jnp.dot(normed_mlp, up_weight, preferred_element_type=jnp.float32)
-        act = (jax.nn.silu(gate_proj) * up_proj).astype(jnp.bfloat16)
-        hidden = add_partials(hidden, jnp.dot(act, down_weight, preferred_element_type=jnp.float32).astype(jnp.bfloat16))
-        final = rms_norm(hidden, norm_final)
+
+        def last_rows(mats):
+            return jnp.concatenate([lax.dynamic_slice_in_dim(mat, last[n], 1, 0) for n, mat in enumerate(mats)], 0)
+
+        partial = last_rows(partials)
+        total = partial.astype(jnp.float32) + lax.ppermute(partial, "tp", y_pairs).astype(jnp.float32)
+        final = rms_norm((last_rows(hidden).astype(jnp.float32) + total).astype(jnp.bfloat16), norm_final)
 
         per_block = jnp.transpose(final.reshape(batch, -1, block), (1, 0, 2))
         per_block = jnp.pad(per_block, ((0, 0), (0, LOGIT_ROWS - batch), (0, 0)))
-        head = None
-        acc = jnp.zeros((LOGIT_ROWS, vocab_half), jnp.float32)
-        for first, last in zip(HEAD_CUTS, HEAD_CUTS[1:]):
-            pieces = column_pieces([w_head], (first, last))
-            z = per_block[:, :, first:last]
-            head, acc = place_head(pieces, (model, vocab_half), column_slot, block, first, z, acc, head)
+        own, _ = halves([w_head])
+        own_x = over_x(own)
+        near = {0: own, 2: over_core(own), 4: own_x, 6: over_core(own_x)}
+        (head,) = place(
+            list(near.values()), [((model, vocab_half), 0)], lambda j, me: column_slot(list(near)[j], me), block
+        )
+        me = 2 * dp_idx + tp_idx
+        acc = sum(jnp.dot(per_block[column_slot(j, me)], piece, preferred_element_type=jnp.float32) for j, piece in near.items())
+        for first, last_row in zip(HEAD_CUTS, HEAD_CUTS[1:]):
+            _, other = halves([w_head], (first, last_row))
+            far = over_y(other)
+            far_x = over_x(far)
+            pieces = {1: far, 3: over_core(far), 5: far_x, 7: over_core(far_x)}
+            head, acc = place_head(
+                tuple(pieces), list(pieces.values()), (model, vocab_half), column_slot, block, first, per_block[:, :, first:last_row], acc, head
+            )
         logits = acc[:batch]
 
         vocab_ids = tp_idx * vocab_half + jnp.arange(vocab_half)
         local_lse = jax.nn.logsumexp(logits, axis=-1)
         local_picked = jnp.sum(jnp.where(vocab_ids[None, :] == targets[:, None], logits, 0.0), axis=-1)
-        both = lax.all_gather(jnp.stack([local_lse, local_picked]), "tp", axis=0)
-        logprobs = jnp.sum(both[:, 1], axis=0) - jax.nn.logsumexp(both[:, 0], axis=0)
+        local = jnp.stack([local_lse, local_picked])
+        other = lax.ppermute(local, "tp", y_pairs)
+        logprobs = local[1] + other[1] - jnp.logaddexp(local[0], other[0])
         return (
             q_weight[None], k_weight[None], v_weight[None], o_weight[None], gate_weight[None], up_weight[None], down_weight[None],
             head, keys[None], values[None], logprobs,

time: 2340 us -> 3190 us (1.36)
  matrix products: 129 us -> 952 us
  Pallas kernels: 223 us -> 626 us
  waiting for transfers between devices: 1720 us -> 1430 us
  local copies, waits for them, and re-layouts: 164 us -> 95.1 us
    pallas_call x0 -> x9, Pallas kernels: none -> 371 us  [the longest x4 177 us: attend(): pl.pallas_call(functools.partial(attend_kernel, prompt), grid=(kv_heads,...]
    dot_general x1 -> x4, matrix products: 38.2 us -> 293 us  [layer_program(): jnp.dot(act, down_weight, preferred_element_type=jnp.float32)]
    dot_general x1 -> x4, matrix products: 20 us -> 271 us  [layer_program(): up_proj = jnp.dot(normed_mlp, up_weight, preferred_element_type=jnp.float32)]
    dot_general x5 -> x8, matrix products: 62.3 us -> 302 us  [the longest x4 275 us: layer_program(): jnp.dot(normed_mlp, gate_weight, preferred_element_type=jnp.float32)]
    ppermute x18, waiting for transfers between devices: 940 us -> 757 us  [over_x(): return lax.ppermute(value, 'dp', x_pairs)]
    ppermute x10 -> x18, waiting for transfers between devices: 763 us -> 666 us  [over_y(): return lax.ppermute(value, 'tp', y_pairs)]
    dot_general x1 -> x4, matrix products: 8.04 us -> 86.5 us  [layer_program(): jnp.dot(attn, o_weight, preferred_element_type=jnp.float32)]
    pallas_call x5 -> x6, Pallas kernels: 128 us -> 200 us  [place(): pl.pallas_call(functools.partial(place_kernel, steps, len(pieces), len(al...]
  transfers between devices with their start and end apart: 64 -> 74, of which waited for: 20 -> 19; matrix products, arithmetic and copies ran while one was open for 12% -> 33% of each run, Pallas kernels for 9% -> 20%
where the time goes in v2:
time: 3190 us; the launch traced here: 3180 us
  waiting for transfers between devices  1430 us (45%)
  matrix products  952 us (30%)
  Pallas kernels  626 us (20%)
  local copies, waits for them, and re-layouts  95.1 us (3%)
  starting transfers between devices  43.8 us (1%)
    ppermute x18, waiting for transfers between devices, over_x(): return lax.ppermute(value, 'dp', x_pairs)  757 us
    ppermute x18, waiting for transfers between devices, over_y(): return lax.ppermute(value, 'tp', y_pairs)  666 us
    dot_general x4, matrix products, layer_program(): jnp.dot(act, down_weight, preferred_element_type=jnp.float32)  293 us
    dot_general x4, matrix products, layer_program(): jnp.dot(normed_mlp, gate_weight, preferred_element_type=jnp.float32)  275 us
    dot_general x4, matrix products, layer_program(): up_proj = jnp.dot(normed_mlp, up_weight, preferred_element_type=jnp.float32)  271 us
    pallas_call x6, Pallas kernels, place(): pl.pallas_call(functools.partial(place_kernel, steps, len(pieces), len(al...  200 us
    pallas_call x4, Pallas kernels, attend(): pl.pallas_call(functools.partial(attend_kernel, prompt), grid=(kv_heads,...  177 us
    pallas_call x1, Pallas kernels, project(): pl.pallas_call(project_kernel, grid=(batch, seq_len // tile), out_shape=[...  145 us
  transfers between devices with their start and end apart: 74, of which 19 were waited for; matrix products, arithmetic and copies ran while one was open for 33% of the time, Pallas kernels for 20%

profile of v2, /device:TPU:0, one launch (start us, length us, event | category | flops | bytes accessed | tf_op | source)
XLA Modules:
  0.0 3183.3 jit_solution(12520434591186363105)
XLA Ops:
  9.8 67.2 %collective-permute-done.refs_1_ = bf16[512,3072]{1,0:T(8,128)(2,1)} collective-permute-done((bf16[512,3072]{1,0:T(8,128)(2,1)S(1)}, bf16[512,3072]{1,0:T(8,128)(2,1)}, u32[]{:S(2)}, u32[]{:S(2)}) %collective-permute-start) | collective-permute-done | bytes 3145760 | tf_op jit(solution)/shard_map/ppermute | solution.py:312
  77.5 18.2 collective-permute-done.7
  95.7 5.8 broadcast_select_fusion.2
  103.6 59.5 %collective-permute-done.3.refs_4_ = bf16[512,3072]{1,0:T(8,128)(2,1)} collective-permute-done((bf16[512,3072]{1,0:T(8,128)(2,1)S(1)}, bf16[512,3072]{1,0:T(8,128)(2,1)}, u32[]{:S(2)}, u32[]{:S(2)}) %collective-permute-start.3) | collective-permute-done | bytes 3145760 | tf_op jit(solution)/shard_map/ppermute | solution.py:309
  163.7 66.1 %collective-permute-done.4.refs_5_ = bf16[512,3072]{1,0:T(8,128)(2,1)} collective-permute-done((bf16[512,3072]{1,0:T(8,128)(2,1)}, bf16[512,3072]{1,0:T(8,128)(2,1)}, u32[]{:S(2)}, u32[]{:S(2)}) %collective-permute-start.4) | collective-permute-done | bytes 3145760 | tf_op jit(solution)/shard_map/ppermute | solution.py:309
  233.0 12.1 dynamic-slice_bitcast_fusion.2
  256.4 24.5 shard_map.221
  281.0 145.4 %project.1 = (bf16[4,4,1024,128]{3,2,1,0:T(8,128)(2,1)}, bf16[4,4,1024,128]{3,2,1,0:T(8,128)(2,1)}, bf16[4,16,1024,128]{3,2,1,0:T(8,128)(2,1)}) custom-call(bf16[4,1024,4096]{2,1,0:T(8,128)(2,1)} %x_ref.9, bf16[1,4096]{1,0:T(2,128)(2,1)} %gain_ref.5, bf16[4096,3072]{1,0:T(8,128)(2,1)} %get-tuple-element.47.w_ref, f32[1024,128]{1,0:T(8,128)} %get-tuple-element.118.cos_ref, ...), custom_call_target="tpu_custom_call" | custom-call | flops 103079215104 | bytes 33554432 | tf_op jit(solution)/shard_map/project/pallas_call | solution.py:139
  430.8 44.3 %attend.4 = bf16[1024,2048]{1,0:T(8,128)(2,1)S(1)} custom-call(s32[4]{0:T(128)S(1)} %copy-done.15, bf16[4,16,1024,128]{3,2,1,0:T(8,128)(2,1)} %get-tuple-element.48.q_ref, bf16[4,4,1024,128]{3,2,1,0:T(8,128)(2,1)S(1)} %copy-done.16, bf16[4,4,1024,128]{3,2,1,0:T(8,128)(2,1)S(1)} %copy-done.17), custom_call_target="tpu_custom_call" | custom-call | flops 8589934592 | bytes 16777216 | tf_op jit(solution)/shard_map/attend/pallas_call | solution.py:187
  475.0 44.3 %attend.5 = bf16[1024,2048]{1,0:T(8,128)(2,1)S(1)} custom-call(s32[4]{0:T(128)S(1)} %copy-done.15, bf16[4,16,1024,128]{3,2,1,0:T(8,128)(2,1)} %get-tuple-element.48.q_ref, bf16[4,4,1024,128]{3,2,1,0:T(8,128)(2,1)S(1)} %copy-done.16, bf16[4,4,1024,128]{3,2,1,0:T(8,128)(2,1)S(1)} %copy-done.17), custom_call_target="tpu_custom_call" | custom-call | flops 8589934592 | bytes 16777216 | tf_op jit(solution)/shard_map/attend/pallas_call | solution.py:187
  519.3 44.5 %attend.6 = bf16[1024,2048]{1,0:T(8,128)(2,1)S(1)} custom-call(s32[4]{0:T(128)S(1)} %copy-done.15, bf16[4,16,1024,128]{3,2,1,0:T(8,128)(2,1)} %get-tuple-element.48.q_ref, bf16[4,4,1024,128]{3,2,1,0:T(8,128)(2,1)S(1)} %copy-done.16, bf16[4,4,1024,128]{3,2,1,0:T(8,128)(2,1)S(1)} %copy-done.17), custom_call_target="tpu_custom_call" | custom-call | flops 8589934592 | bytes 16777216 | tf_op jit(solution)/shard_map/attend/pallas_call | solution.py:187
  563.8 44.3 %attend.7 = bf16[1024,2048]{1,0:T(8,128)(2,1)S(1)} custom-call(s32[4]{0:T(128)S(1)} %copy-done.15, bf16[4,16,1024,128]{3,2,1,0:T(8,128)(2,1)} %get-tuple-element.48.q_ref, bf16[4,4,1024,128]{3,2,1,0:T(8,128)(2,1)S(1)} %copy-done.16, bf16[4,4,1024,128]{3,2,1,0:T(8,128)(2,1)S(1)} %copy-done.17), custom_call_target="tpu_custom_call" | custom-call | flops 8589934592 | bytes 16777216 | tf_op jit(solution)/shard_map/attend/pallas_call | solution.py:187
  610.6 12.4 shard_map.222
  623.0 21.6 convolution_convert_fusion.3.mine_ref
  644.6 21.5 convolution_convert_fusion.2.mine_ref
  666.1 21.9 convolution_convert_fusion.1.mine_ref
  688.0 21.5 convolution_convert_fusion.mine_ref
  711.5 57.7 %collective-permute-done.18.refs_1_ = bf16[512,7168]{1,0:T(8,128)(2,1)} collective-permute-done((bf16[512,7168]{1,0:T(8,128)(2,1)}, bf16[512,7168]{1,0:T(8,128)(2,1)}, u32[]{:S(2)}, u32[]{:S(2)}) %collective-permute-start.18) | collective-permute-done | bytes 7340064 | tf_op jit(solution)/shard_map/ppermute | solution.py:312
  769.7 313.4 %collective-permute-done.15.refs_5_ = bf16[512,7168]{1,0:T(8,128)(2,1)} collective-permute-done((bf16[512,7168]{1,0:T(8,128)(2,1)}, bf16[512,7168]{1,0:T(8,128)(2,1)}, u32[]{:S(2)}, u32[]{:S(2)}) %collective-permute-start.15) | collective-permute-done | bytes 7340064 | tf_op jit(solution)/shard_map/ppermute | solution.py:309
  1089.1 10.5 constant_dynamic-slice_fusion.8
  1100.3 28.5 collective-permute-done.30.other_ref
  1128.8 179.8 %collective-permute-done.31.other_ref = bf16[1024,4096]{1,0:T(8,128)(2,1)} collective-permute-done((bf16[1024,4096]{1,0:T(8,128)(2,1)}, bf16[1024,4096]{1,0:T(8,128)(2,1)}, u32[]{:S(2)}, u32[]{:S(2)}) %collective-permute-start.31) | collective-permute-done | bytes 8388640 | tf_op jit(solution)/shard_map/ppermute | solution.py:312
  1309.1 178.3 %collective-permute-done.32.other_ref = bf16[1024,4096]{1,0:T(8,128)(2,1)} collective-permute-done((bf16[1024,4096]{1,0:T(8,128)(2,1)}, bf16[1024,4096]{1,0:T(8,128)(2,1)}, u32[]{:S(2)}, u32[]{:S(2)}) %collective-permute-start.32) | collective-permute-done | bytes 8388640 | tf_op jit(solution)/shard_map/ppermute | solution.py:312
  1497.3 15.6 constant_dynamic-slice_fusion.1.refs_0_
  1512.9 16.1 broadcast_select_fusion
  1529.0 12.0 mix.4
  1544.2 12.0 mix.5
  1562.8 12.0 mix.6
  1581.4 12.2 mix.7
  1605.5 39.9 %shard_map.223 = bf16[4096,7168]{1,0:T(8,128)(2,1)} custom-call(bf16[512,7168]{1,0:T(8,128)(2,1)} %get-tuple-element.93.refs_0_, bf16[512,7168]{1,0:T(8,128)(2,1)} %collective-permute-done.11.refs_1_, bf16[512,7168]{1,0:T(8,128)(2,1)} %collective-permute-done.12.refs_2_, bf16[512,7168]{1,0:T(8,128)(2,1)} %collective-permute-done.13.refs_3_, ...), custom_call_target="tpu_custom_call" | custom-call | tf_op jit(solution)/shard_map/pallas_call | solution.py:85
  1645.4 67.2 %fusion.29 = f32[1024,7168]{1,0:T(8,128)} fusion(bf16[1024,4096]{1,0:T(8,128)(2,1)S(1)} %bitcast.109, bf16[4096,7168]{1,0:T(8,128)(2,1)} %shard_map.223), kind=kOutput, calls=%fused_computation.112 | convolution fusion | flops 60129542144 | bytes 96468992 | tf_op jit(solution)/shard_map/dot_general | solution.py:397
  1716.6 39.9 %shard_map.224 = bf16[4096,7168]{1,0:T(8,128)(2,1)} custom-call(bf16[512,7168]{1,0:T(8,128)(2,1)} %get-tuple-element.91.refs_0_, bf16[512,7168]{1,0:T(8,128)(2,1)} %collective-permute-done.18.refs_1_, bf16[512,7168]{1,0:T(8,128)(2,1)} %collective-permute-done.19.refs_2_, bf16[512,7168]{1,0:T(8,128)(2,1)} %collective-permute-done.20.refs_3_, ...), custom_call_target="tpu_custom_call" | custom-call | tf_op jit(solution)/shard_map/pallas_call | solution.py:85
  1756.5 67.3 %fusion.30 = f32[1024,7168]{1,0:T(8,128)} fusion(bf16[1024,4096]{1,0:T(8,128)(2,1)S(1)} %bitcast.109, bf16[4096,7168]{1,0:T(8,128)(2,1)} %shard_map.224), kind=kOutput, calls=%fused_computation.113 | convolution fusion | flops 60129542144 | bytes 96468992 | tf_op jit(solution)/shard_map/dot_general | solution.py:398
  1823.9 72.1 %fusion.31 = f32[1024,7168]{1,0:T(8,128)} fusion(bf16[1024,4096]{1,0:T(8,128)(2,1)} %copy-done.13, bf16[4096,7168]{1,0:T(8,128)(2,1)} %shard_map.223), kind=kOutput, calls=%fused_computation.114 | convolution fusion | flops 60129542144 | bytes 96468992 | tf_op jit(solution)/shard_map/dot_general | solution.py:397
  1896.0 68.2 %fusion.32 = f32[1024,7168]{1,0:T(8,128)} fusion(bf16[1024,4096]{1,0:T(8,128)(2,1)S(1)} %copy-done.14, bf16[4096,7168]{1,0:T(8,128)(2,1)} %shard_map.224), kind=kOutput, calls=%fused_computation.115 | convolution fusion | flops 60129542144 | bytes 96468992 | tf_op jit(solution)/shard_map/dot_general | solution.py:398
  1964.1 67.6 %fusion.33 = f32[1024,7168]{1,0:T(8,128)} fusion(bf16[1024,4096]{1,0:T(8,128)(2,1)S(1)} %copy-done.11, bf16[4096,7168]{1,0:T(8,128)(2,1)} %shard_map.223), kind=kOutput, calls=%fused_computation.116 | convolution fusion | flops 60129542144 | bytes 96468992 | tf_op jit(solution)/shard_map/dot_general | solution.py:397
  2031.7 75.6 %collective-permute-done.26.refs_1_ = bf16[1792,4096]{1,0:T(8,128)(2,1)} collective-permute-done((bf16[1792,4096]{1,0:T(8,128)(2,1)}, bf16[1792,4096]{1,0:T(8,128)(2,1)}, u32[]{:S(2)}, u32[]{:S(2)}) %collective-permute-start.26) | collective-permute-done | bytes 14680096 | tf_op jit(solution)/shard_map/ppermute | solution.py:312
  2107.3 67.6 %fusion.34 = f32[1024,7168]{1,0:T(8,128)} fusion(bf16[1024,4096]{1,0:T(8,128)(2,1)S(1)} %copy-done.11, bf16[4096,7168]{1,0:T(8,128)(2,1)} %shard_map.224), kind=kOutput, calls=%fused_computation.117 | convolution fusion | flops 60129542144 | bytes 96468992 | tf_op jit(solution)/shard_map/dot_general | solution.py:398
  2175.0 67.8 %fusion.35 = f32[1024,7168]{1,0:T(8,128)} fusion(bf16[1024,4096]{1,0:T(8,128)(2,1)S(1)} %copy-done.9, bf16[4096,7168]{1,0:T(8,128)(2,1)} %shard_map.223), kind=kOutput, calls=%fused_computation.118 | convolution fusion | flops 60129542144 | bytes 96468992 | tf_op jit(solution)/shard_map/dot_general | solution.py:397
  2246.8 67.4 %fusion.36 = f32[1024,7168]{1,0:T(8,128)} fusion(bf16[1024,4096]{1,0:T(8,128)(2,1)S(1)} %copy-done.9, bf16[4096,7168]{1,0:T(8,128)(2,1)} %shard_map.224), kind=kOutput, calls=%fused_computation.119 | convolution fusion | flops 60129542144 | bytes 96468992 | tf_op jit(solution)/shard_map/dot_general | solution.py:398
  2314.3 39.9 %shard_map.225 = bf16[7168,4096]{1,0:T(8,128)(2,1)} custom-call(bf16[1792,4096]{1,0:T(8,128)(2,1)} %get-tuple-element.89.refs_0_, bf16[1792,4096]{1,0:T(8,128)(2,1)} %collective-permute-done.26.refs_1_, bf16[1792,4096]{1,0:T(8,128)(2,1)} %collective-permute-done.27.refs_2_, bf16[1792,4096]{1,0:T(8,128)(2,1)} %collective-permute-done.28.refs_3_), custom_call_target="tpu_custom_call" | custom-call | tf_op jit(solution)/shard_map/pallas_call | solution.py:85
  2356.6 21.8 collective-permute-done.49.refs_2_
  2378.7 43.6 %collective-permute-done.53.refs_2_ = bf16[64,16000]{1,0:T(8,128)(2,1)} collective-permute-done((bf16[64,16000]{1,0:T(8,128)(2,1)}, bf16[64,16000]{1,0:T(8,128)(2,1)}, u32[]{:S(2)}, u32[]{:S(2)}) %collective-permute-start.53) | collective-permute-done | bytes 2048032 | tf_op jit(solution)/shard_map/ppermute | solution.py:312
  2422.5 73.2 %fusion = bf16[1024,4096]{1,0:T(8,128)(2,1)} fusion(bf16[7168,4096]{1,0:T(8,128)(2,1)} %shard_map.225, f32[1024,7168]{1,0:T(8,128)} %fusion.30, f32[1024,7168]{1,0:T(8,128)} %fusion.29), kind=kOutput, calls=%fused_computation.7 | convolution fusion | flops 60173582336 | bytes 125829120 | tf_op jit(solution)/shard_map/dot_general | solution.py:400
  2495.8 13.6 collective-permute-done.61.refs_2_
  2509.7 232.3 %collective-permute-done.67.refs_4_ = bf16[48,16000]{1,0:T(8,128)(2,1)} collective-permute-done((bf16[48,16000]{1,0:T(8,128)(2,1)}, bf16[48,16000]{1,0:T(8,128)(2,1)}, u32[]{:S(2)}, u32[]{:S(2)}) %collective-permute-start.67) | collective-permute-done | bytes 1536032 | tf_op jit(solution)/shard_map/ppermute | solution.py:309
  2742.1 43.9 %collective-permute-done.39.refs_4_ = bf16[64,16000]{1,0:T(8,128)(2,1)} collective-permute-done((bf16[64,16000]{1,0:T(8,128)(2,1)}, bf16[64,16000]{1,0:T(8,128)(2,1)}, u32[]{:S(2)}, u32[]{:S(2)}) %collective-permute-start.39) | collective-permute-done | bytes 2048032 | tf_op jit(solution)/shard_map/ppermute | solution.py:309
  2786.3 73.6 %fusion.1 = bf16[1024,4096]{1,0:T(8,128)(2,1)} fusion(bf16[7168,4096]{1,0:T(8,128)(2,1)} %shard_map.225, f32[1024,7168]{1,0:T(8,128)} %fusion.32, f32[1024,7168]{1,0:T(8,128)} %fusion.31), kind=kOutput, calls=%fused_computation.8 | convolution fusion | flops 60173582336 | bytes 125829120 | tf_op jit(solution)/shard_map/dot_general | solution.py:400
  2862.1 11.7 collective-permute-done.47.refs_4_
  2874.3 73.1 %fusion.2 = bf16[1024,4096]{1,0:T(8,128)(2,1)} fusion(bf16[7168,4096]{1,0:T(8,128)(2,1)} %shard_map.225, f32[1024,7168]{1,0:T(8,128)} %fusion.34, f32[1024,7168]{1,0:T(8,128)} %fusion.33), kind=kOutput, calls=%fused_computation.9 | convolution fusion | flops 60173582336 | bytes 125829120 | tf_op jit(solution)/shard_map/dot_general | solution.py:400
  2949.4 73.2 %fusion.3 = bf16[1024,4096]{1,0:T(8,128)(2,1)} fusion(bf16[7168,4096]{1,0:T(8,128)(2,1)} %shard_map.225, f32[1024,7168]{1,0:T(8,128)} %fusion.36, f32[1024,7168]{1,0:T(8,128)} %fusion.35), kind=kOutput, calls=%fused_computation.10 | convolution fusion | flops 60173582336 | bytes 125829120 | tf_op jit(solution)/shard_map/dot_general | solution.py:400
  3026.7 12.3 collective-permute-done.59.refs_4_
  3042.0 5.6 copy-done
  3047.7 43.0 %shard_map.226.refs_6_ = bf16[4096,16000]{1,0:T(8,128)(2,1)} custom-call(bf16[512,16000]{1,0:T(8,128)(2,1)S(1)} %copy-done, bf16[512,16000]{1,0:T(8,128)(2,1)} %collective-permute-done.34.refs_1_, bf16[512,16000]{1,0:T(8,128)(2,1)} %collective-permute-done.35.refs_2_, bf16[512,16000]{1,0:T(8,128)(2,1)} %collective-permute-done.36.refs_3_), custom_call_target="tpu_custom_call" | custom-call | tf_op jit(solution)/shard_map/pallas_call | solution.py:85
  3095.2 8.5 convolution_add_fusion.2
  3104.2 8.2 convolution_add_fusion.1
  3113.0 8.6 convolution_add_fusion.refs_1_
  3121.7 6.9 shard_map.227
  3128.6 6.9 shard_map.228
  3135.5 6.9 shard_map.229
  3142.4 6.9 shard_map.230
  3149.3 6.9 shard_map.231
  3156.2 5.8 shard_map.232
  3162.0 6.2 shard_map.233
  (256 shorter events, 117.5 us)
Async XLA Ops:
  0.7 95.1 %collective-permute-start.7 = (bf16[512,4096]{1,0:T(8,128)(2,1)}, bf16[512,4096]{1,0:T(8,128)(2,1)}, u32[]{:S(2)}, u32[]{:S(2)}) collective-permute-start(bf16[512,4096]{1,0:T(8,128)(2,1)} %bitcast.121), channel_id=1, source_target_pairs={{0,2},{1,3},{2,0},{3,1},{4,6},{5,7},{6,4},{7,5}} | collective-permute-start | bytes 12582920 | tf_op jit(solution)/shard_map/ppermute | solution.py:309
  7.3 69.7 %collective-permute-start = (bf16[512,3072]{1,0:T(8,128)(2,1)S(1)}, bf16[512,3072]{1,0:T(8,128)(2,1)}, u32[]{:S(2)}, u32[]{:S(2)}) collective-permute-start(bf16[512,3072]{1,0:T(8,128)(2,1)S(1)} %pad_maximum_fusion.1), channel_id=1, source_target_pairs={{0,4},{4,0},{1,5},{5,1},{2,6},{6,2},{3,7},{7,3}} | collective-permute-start | bytes 9437192 | tf_op jit(solution)/shard_map/ppermute | solution.py:312
  9.2 153.9 %collective-permute-start.3 = (bf16[512,3072]{1,0:T(8,128)(2,1)S(1)}, bf16[512,3072]{1,0:T(8,128)(2,1)}, u32[]{:S(2)}, u32[]{:S(2)}) collective-permute-start(bf16[512,3072]{1,0:T(8,128)(2,1)S(1)} %pad_maximum_fusion.refs_0_), channel_id=1, source_target_pairs={{0,2},{1,3},{2,0},{3,1},{4,6},{5,7},{6,4},{7,5}} | collective-permute-start | bytes 9437192 | tf_op jit(solution)/shard_map/ppermute | solution.py:309
  77.0 152.7 %collective-permute-start.4 = (bf16[512,3072]{1,0:T(8,128)(2,1)}, bf16[512,3072]{1,0:T(8,128)(2,1)}, u32[]{:S(2)}, u32[]{:S(2)}) collective-permute-start(bf16[512,3072]{1,0:T(8,128)(2,1)} %collective-permute-done.refs_1_), channel_id=1, source_target_pairs={{0,2},{1,3},{2,0},{3,1},{4,6},{5,7},{6,4},{7,5}} | collective-permute-start | bytes 9437192 | tf_op jit(solution)/shard_map/ppermute | solution.py:309
  101.6 154.4 %collective-permute-start.8 = (bf16[512,4096]{1,0:T(8,128)(2,1)}, bf16[512,4096]{1,0:T(8,128)(2,1)}, u32[]{:S(2)}, u32[]{:S(2)}) collective-permute-start(bf16[512,4096]{1,0:T(8,128)(2,1)} %get-tuple-element.94), channel_id=1, source_target_pairs={{0,4},{4,0},{1,5},{5,1},{2,6},{6,2},{3,7},{7,3}} | collective-permute-start | bytes 12582920 | tf_op jit(solution)/shard_map/ppermute | solution.py:312
  103.6 148.8 %collective-permute-start.1 = (bf16[512,3072]{1,0:T(8,128)(2,1)S(1)}, bf16[512,3072]{1,0:T(8,128)(2,1)}, u32[]{:S(2)}, u32[]{:S(2)}) collective-permute-start(bf16[512,3072]{1,0:T(8,128)(2,1)S(1)} %pad_maximum_fusion.refs_0_), channel_id=1, source_target_pairs={{0,1},{1,0},{2,3},{3,2},{4,5},{5,4},{6,7},{7,6}} | collective-permute-start | bytes 9437192 | tf_op jit(solution)/shard_map/ppermute | solution.py:315
  163.1 91.0 %collective-permute-start.5 = (bf16[512,3072]{1,0:T(8,128)(2,1)}, bf16[512,3072]{1,0:T(8,128)(2,1)}, u32[]{:S(2)}, u32[]{:S(2)}) collective-permute-start(bf16[512,3072]{1,0:T(8,128)(2,1)} %collective-permute-done.3.refs_4_), channel_id=1, source_target_pairs={{0,1},{1,0},{2,3},{3,2},{4,5},{5,4},{6,7},{7,6}} | collective-permute-start | bytes 9437192 | tf_op jit(solution)/shard_map/ppermute | solution.py:315
  163.1 91.3 %collective-permute-start.2 = (bf16[512,3072]{1,0:T(8,128)(2,1)}, bf16[512,3072]{1,0:T(8,128)(2,1)}, u32[]{:S(2)}, u32[]{:S(2)}) collective-permute-start(bf16[512,3072]{1,0:T(8,128)(2,1)} %collective-permute-done.refs_1_), channel_id=1, source_target_pairs={{0,1},{1,0},{2,3},{3,2},{4,5},{5,4},{6,7},{7,6}} | collective-permute-start | bytes 9437192 | tf_op jit(solution)/shard_map/ppermute | solution.py:315
  252.4 457.1 %collective-permute-start.14 = (bf16[512,7168]{1,0:T(8,128)(2,1)}, bf16[512,7168]{1,0:T(8,128)(2,1)}, u32[]{:S(2)}, u32[]{:S(2)}) collective-permute-start(bf16[512,7168]{1,0:T(8,128)(2,1)} %get-tuple-element.93.refs_0_), channel_id=1, source_target_pairs={{0,2},{1,3},{2,0},{3,1},{4,6},{5,7},{6,4},{7,5}} | collective-permute-start | bytes 22020104 | tf_op jit(solution)/shard_map/ppermute | solution.py:309
  254.2 456.9 %collective-permute-start.12 = (bf16[512,7168]{1,0:T(8,128)(2,1)}, bf16[512,7168]{1,0:T(8,128)(2,1)}, u32[]{:S(2)}, u32[]{:S(2)}) collective-permute-start(bf16[512,7168]{1,0:T(8,128)(2,1)} %get-tuple-element.93.refs_0_), channel_id=1, source_target_pairs={{0,1},{1,0},{2,3},{3,2},{4,5},{5,4},{6,7},{7,6}} | collective-permute-start | bytes 22020104 | tf_op jit(solution)/shard_map/ppermute | solution.py:315
  254.4 353.6 %collective-permute-start.11 = (bf16[512,7168]{1,0:T(8,128)(2,1)}, bf16[512,7168]{1,0:T(8,128)(2,1)}, u32[]{:S(2)}, u32[]{:S(2)}) collective-permute-start(bf16[512,7168]{1,0:T(8,128)(2,1)} %get-tuple-element.92), channel_id=1, source_target_pairs={{0,4},{4,0},{1,5},{5,1},{2,6},{6,2},{3,7},{7,3}} | collective-permute-start | bytes 22020104 | tf_op jit(solution)/shard_map/ppermute | solution.py:312
  255.9 352.6 %collective-permute-start.9 = (bf16[512,4096]{1,0:T(8,128)(2,1)}, bf16[512,4096]{1,0:T(8,128)(2,1)}, u32[]{:S(2)}, u32[]{:S(2)}) collective-permute-start(bf16[512,4096]{1,0:T(8,128)(2,1)} %get-tuple-element.95.refs_0_), channel_id=1, source_target_pairs={{0,1},{1,0},{2,3},{3,2},{4,5},{5,4},{6,7},{7,6}} | collective-permute-start | bytes 12582920 | tf_op jit(solution)/shard_map/ppermute | solution.py:315
  255.9 353.0 %collective-permute-start.10 = (bf16[512,4096]{1,0:T(8,128)(2,1)}, bf16[512,4096]{1,0:T(8,128)(2,1)}, u32[]{:S(2)}, u32[]{:S(2)}) collective-permute-start(bf16[512,4096]{1,0:T(8,128)(2,1)} %collective-permute-done.8.refs_1_), channel_id=1, source_target_pairs={{0,1},{1,0},{2,3},{3,2},{4,5},{5,4},{6,7},{7,6}} | collective-permute-start | bytes 12582920 | tf_op jit(solution)/shard_map/ppermute | solution.py:315
  608.0 161.2 %collective-permute-start.18 = (bf16[512,7168]{1,0:T(8,128)(2,1)}, bf16[512,7168]{1,0:T(8,128)(2,1)}, u32[]{:S(2)}, u32[]{:S(2)}) collective-permute-start(bf16[512,7168]{1,0:T(8,128)(2,1)} %get-tuple-element.90), channel_id=1, source_target_pairs={{0,4},{4,0},{1,5},{5,1},{2,6},{6,2},{3,7},{7,3}} | collective-permute-start | bytes 22020104 | tf_op jit(solution)/shard_map/ppermute | solution.py:312
  608.6 491.1 %collective-permute-start.25 = (bf16[1792,4096]{1,0:T(8,128)(2,1)}, bf16[1792,4096]{1,0:T(8,128)(2,1)}, u32[]{:S(2)}, u32[]{:S(2)}) collective-permute-start(bf16[1792,4096]{1,0:T(8,128)(2,1)} %bitcast.118), channel_id=1, source_target_pairs={{0,2},{1,3},{2,0},{3,1},{4,6},{5,7},{6,4},{7,5}} | collective-permute-start | bytes 44040200 | tf_op jit(solution)/shard_map/ppermute | solution.py:309
  608.9 474.2 %collective-permute-start.15 = (bf16[512,7168]{1,0:T(8,128)(2,1)}, bf16[512,7168]{1,0:T(8,128)(2,1)}, u32[]{:S(2)}, u32[]{:S(2)}) collective-permute-start(bf16[512,7168]{1,0:T(8,128)(2,1)} %collective-permute-done.11.refs_1_), channel_id=1, source_target_pairs={{0,2},{1,3},{2,0},{3,1},{4,6},{5,7},{6,4},{7,5}} | collective-permute-start | bytes 22020104 | tf_op jit(solution)/shard_map/ppermute | solution.py:309
  709.5 390.8 %collective-permute-start.29 = (bf16[1024,4096]{1,0:T(8,128)(2,1)}, bf16[1024,4096]{1,0:T(8,128)(2,1)}, u32[]{:S(2)}, u32[]{:S(2)}) collective-permute-start(bf16[1024,4096]{1,0:T(8,128)(2,1)} %convolution_convert_fusion.3.mine_ref), channel_id=1, source_target_pairs={{0,4},{4,0},{1,5},{5,1},{2,6},{6,2},{3,7},{7,3}} | collective-permute-start | bytes 25165832 | tf_op jit(solution)/shard_map/ppermute | solution.py:312
  711.0 417.7 %collective-permute-start.30 = (bf16[1024,4096]{1,0:T(8,128)(2,1)}, bf16[1024,4096]{1,0:T(8,128)(2,1)}, u32[]{:S(2)}, u32[]{:S(2)}) collective-permute-start(bf16[1024,4096]{1,0:T(8,128)(2,1)} %convolution_convert_fusion.2.mine_ref), channel_id=1, source_target_pairs={{0,4},{4,0},{1,5},{5,1},{2,6},{6,2},{3,7},{7,3}} | collective-permute-start | bytes 25165832 | tf_op jit(solution)/shard_map/ppermute | solution.py:312
  769.2 539.3 %collective-permute-start.31 = (bf16[1024,4096]{1,0:T(8,128)(2,1)}, bf16[1024,4096]{1,0:T(8,128)(2,1)}, u32[]{:S(2)}, u32[]{:S(2)}) collective-permute-start(bf16[1024,4096]{1,0:T(8,128)(2,1)} %convolution_convert_fusion.1.mine_ref), channel_id=1, source_target_pairs={{0,4},{4,0},{1,5},{5,1},{2,6},{6,2},{3,7},{7,3}} | collective-permute-start | bytes 25165832 | tf_op jit(solution)/shard_map/ppermute | solution.py:312
  1083.1 404.2 %collective-permute-start.32 = (bf16[1024,4096]{1,0:T(8,128)(2,1)}, bf16[1024,4096]{1,0:T(8,128)(2,1)}, u32[]{:S(2)}, u32[]{:S(2)}) collective-permute-start(bf16[1024,4096]{1,0:T(8,128)(2,1)} %convolution_convert_fusion.mine_ref), channel_id=1, source_target_pairs={{0,4},{4,0},{1,5},{5,1},{2,6},{6,2},{3,7},{7,3}} | collective-permute-start | bytes 25165832 | tf_op jit(solution)/shard_map/ppermute | solution.py:312
  1099.7 504.2 %collective-permute-start.21 = (bf16[512,7168]{1,0:T(8,128)(2,1)}, bf16[512,7168]{1,0:T(8,128)(2,1)}, u32[]{:S(2)}, u32[]{:S(2)}) collective-permute-start(bf16[512,7168]{1,0:T(8,128)(2,1)} %get-tuple-element.91.refs_0_), channel_id=1, source_target_pairs={{0,2},{1,3},{2,0},{3,1},{4,6},{5,7},{6,4},{7,5}} | collective-permute-start | bytes 22020104 | tf_op jit(solution)/shard_map/ppermute | solution.py:309
  1100.3 504.6 %collective-permute-start.13 = (bf16[512,7168]{1,0:T(8,128)(2,1)}, bf16[512,7168]{1,0:T(8,128)(2,1)}, u32[]{:S(2)}, u32[]{:S(2)}) collective-permute-start(bf16[512,7168]{1,0:T(8,128)(2,1)} %collective-permute-done.11.refs_1_), channel_id=1, source_target_pairs={{0,1},{1,0},{2,3},{3,2},{4,5},{5,4},{6,7},{7,6}} | collective-permute-start | bytes 22020104 | tf_op jit(solution)/shard_map/ppermute | solution.py:315
  1128.8 475.6 %collective-permute-start.16 = (bf16[512,7168]{1,0:T(8,128)(2,1)}, bf16[512,7168]{1,0:T(8,128)(2,1)}, u32[]{:S(2)}, u32[]{:S(2)}) collective-permute-start(bf16[512,7168]{1,0:T(8,128)(2,1)} %collective-permute-done.14.refs_4_), channel_id=1, source_target_pairs={{0,1},{1,0},{2,3},{3,2},{4,5},{5,4},{6,7},{7,6}} | collective-permute-start | bytes 22020104 | tf_op jit(solution)/shard_map/ppermute | solution.py:315
  1308.5 296.4 %collective-permute-start.22 = (bf16[512,7168]{1,0:T(8,128)(2,1)}, bf16[512,7168]{1,0:T(8,128)(2,1)}, u32[]{:S(2)}, u32[]{:S(2)}) collective-permute-start(bf16[512,7168]{1,0:T(8,128)(2,1)} %collective-permute-done.18.refs_1_), channel_id=1, source_target_pairs={{0,2},{1,3},{2,0},{3,1},{4,6},{5,7},{6,4},{7,5}} | collective-permute-start | bytes 22020104 | tf_op jit(solution)/shard_map/ppermute | solution.py:309
  1487.4 118.1 %collective-permute-start.17 = (bf16[512,7168]{1,0:T(8,128)(2,1)}, bf16[512,7168]{1,0:T(8,128)(2,1)}, u32[]{:S(2)}, u32[]{:S(2)}) collective-permute-start(bf16[512,7168]{1,0:T(8,128)(2,1)} %collective-permute-done.15.refs_5_), channel_id=1, source_target_pairs={{0,1},{1,0},{2,3},{3,2},{4,5},{5,4},{6,7},{7,6}} | collective-permute-start | bytes 22020104 | tf_op jit(solution)/shard_map/ppermute | solution.py:315
  1603.9 110.2 %collective-permute-start.19 = (bf16[512,7168]{1,0:T(8,128)(2,1)}, bf16[512,7168]{1,0:T(8,128)(2,1)}, u32[]{:S(2)}, u32[]{:S(2)}) collective-permute-start(bf16[512,7168]{1,0:T(8,128)(2,1)} %get-tuple-element.91.refs_0_), channel_id=1, source_target_pairs={{0,1},{1,0},{2,3},{3,2},{4,5},{5,4},{6,7},{7,6}} | collective-permute-start | bytes 22020104 | tf_op jit(solution)/shard_map/ppermute | solution.py:315
  1604.4 108.1 %collective-permute-start.69 = (bf16[16,16000]{1,0:T(8,128)(2,1)}, bf16[16,16000]{1,0:T(8,128)(2,1)}, u32[]{:S(2)}, u32[]{:S(2)}) collective-permute-start(bf16[16,16000]{1,0:T(8,128)(2,1)} %constant_dynamic-slice_fusion.6), channel_id=1, source_target_pairs={{0,4},{4,0},{1,5},{5,1},{2,6},{6,2},{3,7},{7,3}} | collective-permute-start | bytes 1536008 | tf_op jit(solution)/shard_map/ppermute | solution.py:312
  1604.9 110.0 %collective-permute-start.20 = (bf16[512,7168]{1,0:T(8,128)(2,1)}, bf16[512,7168]{1,0:T(8,128)(2,1)}, u32[]{:S(2)}, u32[]{:S(2)}) collective-permute-start(bf16[512,7168]{1,0:T(8,128)(2,1)} %collective-permute-done.18.refs_1_), channel_id=1, source_target_pairs={{0,1},{1,0},{2,3},{3,2},{4,5},{5,4},{6,7},{7,6}} | collective-permute-start | bytes 22020104 | tf_op jit(solution)/shard_map/ppermute | solution.py:315
  1604.9 109.6 %collective-permute-start.23 = (bf16[512,7168]{1,0:T(8,128)(2,1)}, bf16[512,7168]{1,0:T(8,128)(2,1)}, u32[]{:S(2)}, u32[]{:S(2)}) collective-permute-start(bf16[512,7168]{1,0:T(8,128)(2,1)} %collective-permute-done.21.refs_4_), channel_id=1, source_target_pairs={{0,1},{1,0},{2,3},{3,2},{4,5},{5,4},{6,7},{7,6}} | collective-permute-start | bytes 22020104 | tf_op jit(solution)/shard_map/ppermute | solution.py:315
  1605.4 111.2 %collective-permute-start.24 = (bf16[512,7168]{1,0:T(8,128)(2,1)}, bf16[512,7168]{1,0:T(8,128)(2,1)}, u32[]{:S(2)}, u32[]{:S(2)}) collective-permute-start(bf16[512,7168]{1,0:T(8,128)(2,1)} %collective-permute-done.22.refs_5_), channel_id=1, source_target_pairs={{0,1},{1,0},{2,3},{3,2},{4,5},{5,4},{6,7},{7,6}} | collective-permute-start | bytes 22020104 | tf_op jit(solution)/shard_map/ppermute | solution.py:315
  1712.5 641.6 %collective-permute-start.37 = (bf16[64,16000]{1,0:T(8,128)(2,1)}, bf16[64,16000]{1,0:T(8,128)(2,1)}, u32[]{:S(2)}, u32[]{:S(2)}) collective-permute-start(bf16[64,16000]{1,0:T(8,128)(2,1)} %get-tuple-element.87), channel_id=1, source_target_pairs={{0,4},{4,0},{1,5},{5,1},{2,6},{6,2},{3,7},{7,3}} | collective-permute-start | bytes 6144008 | tf_op jit(solution)/shard_map/ppermute | solution.py:312
  1714.0 530.2 %collective-permute-start.65 = (bf16[48,16000]{1,0:T(8,128)(2,1)}, bf16[48,16000]{1,0:T(8,128)(2,1)}, u32[]{:S(2)}, u32[]{:S(2)}) collective-permute-start(bf16[48,16000]{1,0:T(8,128)(2,1)} %constant_dynamic-slice_fusion.7), channel_id=1, source_target_pairs={{0,4},{4,0},{1,5},{5,1},{2,6},{6,2},{3,7},{7,3}} | collective-permute-start | bytes 4608008 | tf_op jit(solution)/shard_map/ppermute | solution.py:312
  1714.6 528.2 %collective-permute-start.71 = (bf16[16,16000]{1,0:T(8,128)(2,1)}, bf16[16,16000]{1,0:T(8,128)(2,1)}, u32[]{:S(2)}, u32[]{:S(2)}) collective-permute-start(bf16[16,16000]{1,0:T(8,128)(2,1)} %collective-permute-done.69.refs_2_), channel_id=1, source_target_pairs={{0,2},{1,3},{2,0},{3,1},{4,6},{5,7},{6,4},{7,5}} | collective-permute-start | bytes 1536008 | tf_op jit(solution)/shard_map/ppermute | solution.py:309
  1714.9 392.4 %collective-permute-start.26 = (bf16[1792,4096]{1,0:T(8,128)(2,1)}, bf16[1792,4096]{1,0:T(8,128)(2,1)}, u32[]{:S(2)}, u32[]{:S(2)}) collective-permute-start(bf16[1792,4096]{1,0:T(8,128)(2,1)} %get-tuple-element.88), channel_id=1, source_target_pairs={{0,4},{4,0},{1,5},{5,1},{2,6},{6,2},{3,7},{7,3}} | collective-permute-start | bytes 44040200 | tf_op jit(solution)/shard_map/ppermute | solution.py:312
  1716.6 528.2 %collective-permute-start.27 = (bf16[1792,4096]{1,0:T(8,128)(2,1)}, bf16[1792,4096]{1,0:T(8,128)(2,1)}, u32[]{:S(2)}, u32[]{:S(2)}) collective-permute-start(bf16[1792,4096]{1,0:T(8,128)(2,1)} %get-tuple-element.89.refs_0_), channel_id=1, source_target_pairs={{0,1},{1,0},{2,3},{3,2},{4,5},{5,4},{6,7},{7,6}} | collective-permute-start | bytes 44040200 | tf_op jit(solution)/shard_map/ppermute | solution.py:315
  2107.3 139.0 %collective-permute-start.28 = (bf16[1792,4096]{1,0:T(8,128)(2,1)}, bf16[1792,4096]{1,0:T(8,128)(2,1)}, u32[]{:S(2)}, u32[]{:S(2)}) collective-permute-start(bf16[1792,4096]{1,0:T(8,128)(2,1)} %collective-permute-done.26.refs_1_), channel_id=1, source_target_pairs={{0,1},{1,0},{2,3},{3,2},{4,5},{5,4},{6,7},{7,6}} | collective-permute-start | bytes 44040200 | tf_op jit(solution)/shard_map/ppermute | solution.py:315
  2242.8 111.8 %collective-permute-start.41 = (bf16[64,16000]{1,0:T(8,128)(2,1)}, bf16[64,16000]{1,0:T(8,128)(2,1)}, u32[]{:S(2)}, u32[]{:S(2)}) collective-permute-start(bf16[64,16000]{1,0:T(8,128)(2,1)} %get-tuple-element.86), channel_id=1, source_target_pairs={{0,4},{4,0},{1,5},{5,1},{2,6},{6,2},{3,7},{7,3}} | collective-permute-start | bytes 6144008 | tf_op jit(solution)/shard_map/ppermute | solution.py:312
  2244.3 112.0 %collective-permute-start.45 = (bf16[64,16000]{1,0:T(8,128)(2,1)}, bf16[64,16000]{1,0:T(8,128)(2,1)}, u32[]{:S(2)}, u32[]{:S(2)}) collective-permute-start(bf16[64,16000]{1,0:T(8,128)(2,1)} %get-tuple-element.85), channel_id=1, source_target_pairs={{0,4},{4,0},{1,5},{5,1},{2,6},{6,2},{3,7},{7,3}} | collective-permute-start | bytes 6144008 | tf_op jit(solution)/shard_map/ppermute | solution.py:312
  2244.8 133.5 %collective-permute-start.49 = (bf16[64,16000]{1,0:T(8,128)(2,1)}, bf16[64,16000]{1,0:T(8,128)(2,1)}, u32[]{:S(2)}, u32[]{:S(2)}) collective-permute-start(bf16[64,16000]{1,0:T(8,128)(2,1)} %get-tuple-element.84), channel_id=1, source_target_pairs={{0,4},{4,0},{1,5},{5,1},{2,6},{6,2},{3,7},{7,3}} | collective-permute-start | bytes 6144008 | tf_op jit(solution)/shard_map/ppermute | solution.py:312
  2246.3 175.9 %collective-permute-start.53 = (bf16[64,16000]{1,0:T(8,128)(2,1)}, bf16[64,16000]{1,0:T(8,128)(2,1)}, u32[]{:S(2)}, u32[]{:S(2)}) collective-permute-start(bf16[64,16000]{1,0:T(8,128)(2,1)} %get-tuple-element.83), channel_id=1, source_target_pairs={{0,4},{4,0},{1,5},{5,1},{2,6},{6,2},{3,7},{7,3}} | collective-permute-start | bytes 6144008 | tf_op jit(solution)/shard_map/ppermute | solution.py:312
  2354.2 519.6 %collective-permute-start.35 = (bf16[512,16000]{1,0:T(8,128)(2,1)}, bf16[512,16000]{1,0:T(8,128)(2,1)}, u32[]{:S(2)}, u32[]{:S(2)}) collective-permute-start(bf16[512,16000]{1,0:T(8,128)(2,1)} %constant_dynamic-slice_fusion.1.refs_0_), channel_id=1, source_target_pairs={{0,2},{1,3},{2,0},{3,1},{4,6},{5,7},{6,4},{7,5}} | collective-permute-start | bytes 49152008 | tf_op jit(solution)/shard_map/ppermute | solution.py:309
  2354.5 141.3 %collective-permute-start.57 = (bf16[64,16000]{1,0:T(8,128)(2,1)}, bf16[64,16000]{1,0:T(8,128)(2,1)}, u32[]{:S(2)}, u32[]{:S(2)}) collective-permute-start(bf16[64,16000]{1,0:T(8,128)(2,1)} %get-tuple-element.82), channel_id=1, source_target_pairs={{0,4},{4,0},{1,5},{5,1},{2,6},{6,2},{3,7},{7,3}} | collective-permute-start | bytes 6144008 | tf_op jit(solution)/shard_map/ppermute | solution.py:312
  2356.3 153.2 %collective-permute-start.61 = (bf16[64,16000]{1,0:T(8,128)(2,1)}, bf16[64,16000]{1,0:T(8,128)(2,1)S(1)}, u32[]{:S(2)}, u32[]{:S(2)}) collective-permute-start(bf16[64,16000]{1,0:T(8,128)(2,1)} %get-tuple-element.81), channel_id=1, source_target_pairs={{0,4},{4,0},{1,5},{5,1},{2,6},{6,2},{3,7},{7,3}} | collective-permute-start | bytes 6144008 | tf_op jit(solution)/shard_map/ppermute | solution.py:312
  2378.3 363.8 %collective-permute-start.67 = (bf16[48,16000]{1,0:T(8,128)(2,1)}, bf16[48,16000]{1,0:T(8,128)(2,1)}, u32[]{:S(2)}, u32[]{:S(2)}) collective-permute-start(bf16[48,16000]{1,0:T(8,128)(2,1)} %collective-permute-done.65.refs_2_), channel_id=1, source_target_pairs={{0,2},{1,3},{2,0},{3,1},{4,6},{5,7},{6,4},{7,5}} | collective-permute-start | bytes 4608008 | tf_op jit(solution)/shard_map/ppermute | solution.py:309
  2422.2 363.8 %collective-permute-start.39 = (bf16[64,16000]{1,0:T(8,128)(2,1)}, bf16[64,16000]{1,0:T(8,128)(2,1)}, u32[]{:S(2)}, u32[]{:S(2)}) collective-permute-start(bf16[64,16000]{1,0:T(8,128)(2,1)} %collective-permute-done.37.refs_2_), channel_id=1, source_target_pairs={{0,2},{1,3},{2,0},{3,1},{4,6},{5,7},{6,4},{7,5}} | collective-permute-start | bytes 6144008 | tf_op jit(solution)/shard_map/ppermute | solution.py:309
  2495.8 364.1 %collective-permute-start.38 = (bf16[64,16000]{1,0:T(8,128)(2,1)}, bf16[64,16000]{1,0:T(8,128)(2,1)}, u32[]{:S(2)}, u32[]{:S(2)}) collective-permute-start(bf16[64,16000]{1,0:T(8,128)(2,1)} %collective-permute-done.37.refs_2_), channel_id=1, source_target_pairs={{0,1},{1,0},{2,3},{3,2},{4,5},{5,4},{6,7},{7,6}} | collective-permute-start | bytes 6144008 | tf_op jit(solution)/shard_map/ppermute | solution.py:315
  2509.4 350.5 %collective-permute-start.43 = (bf16[64,16000]{1,0:T(8,128)(2,1)}, bf16[64,16000]{1,0:T(8,128)(2,1)}, u32[]{:S(2)}, u32[]{:S(2)}) collective-permute-start(bf16[64,16000]{1,0:T(8,128)(2,1)} %collective-permute-done.41.refs_2_), channel_id=1, source_target_pairs={{0,2},{1,3},{2,0},{3,1},{4,6},{5,7},{6,4},{7,5}} | collective-permute-start | bytes 6144008 | tf_op jit(solution)/shard_map/ppermute | solution.py:309
  2742.1 118.3 %collective-permute-start.42 = (bf16[64,16000]{1,0:T(8,128)(2,1)}, bf16[64,16000]{1,0:T(8,128)(2,1)}, u32[]{:S(2)}, u32[]{:S(2)}) collective-permute-start(bf16[64,16000]{1,0:T(8,128)(2,1)} %collective-permute-done.41.refs_2_), channel_id=1, source_target_pairs={{0,1},{1,0},{2,3},{3,2},{4,5},{5,4},{6,7},{7,6}} | collective-permute-start | bytes 6144008 | tf_op jit(solution)/shard_map/ppermute | solution.py:315
  2786.0 87.8 %collective-permute-start.47 = (bf16[64,16000]{1,0:T(8,128)(2,1)}, bf16[64,16000]{1,0:T(8,128)(2,1)}, u32[]{:S(2)}, u32[]{:S(2)}) collective-permute-start(bf16[64,16000]{1,0:T(8,128)(2,1)} %collective-permute-done.45.refs_2_), channel_id=1, source_target_pairs={{0,2},{1,3},{2,0},{3,1},{4,6},{5,7},{6,4},{7,5}} | collective-permute-start | bytes 6144008 | tf_op jit(solution)/shard_map/ppermute | solution.py:309
  2859.9 179.2 %collective-permute-start.34 = (bf16[512,16000]{1,0:T(8,128)(2,1)}, bf16[512,16000]{1,0:T(8,128)(2,1)}, u32[]{:S(2)}, u32[]{:S(2)}) collective-permute-start(bf16[512,16000]{1,0:T(8,128)(2,1)} %constant_dynamic-slice_fusion.1.refs_0_), channel_id=1, source_target_pairs={{0,1},{1,0},{2,3},{3,2},{4,5},{5,4},{6,7},{7,6}} | collective-permute-start | bytes 49152008 | tf_op jit(solution)/shard_map/ppermute | solution.py:315
  2859.9 87.5 %collective-permute-start.46 = (bf16[64,16000]{1,0:T(8,128)(2,1)}, bf16[64,16000]{1,0:T(8,128)(2,1)}, u32[]{:S(2)}, u32[]{:S(2)}) collective-permute-start(bf16[64,16000]{1,0:T(8,128)(2,1)} %collective-permute-done.45.refs_2_), channel_id=1, source_target_pairs={{0,1},{1,0},{2,3},{3,2},{4,5},{5,4},{6,7},{7,6}} | collective-permute-start | bytes 6144008 | tf_op jit(solution)/shard_map/ppermute | solution.py:315
  2860.4 87.3 %collective-permute-start.51 = (bf16[64,16000]{1,0:T(8,128)(2,1)}, bf16[64,16000]{1,0:T(8,128)(2,1)}, u32[]{:S(2)}, u32[]{:S(2)}) collective-permute-start(bf16[64,16000]{1,0:T(8,128)(2,1)} %collective-permute-done.49.refs_2_), channel_id=1, source_target_pairs={{0,2},{1,3},{2,0},{3,1},{4,6},{5,7},{6,4},{7,5}} | collective-permute-start | bytes 6144008 | tf_op jit(solution)/shard_map/ppermute | solution.py:309
  2873.8 73.9 %collective-permute-start.50 = (bf16[64,16000]{1,0:T(8,128)(2,1)}, bf16[64,16000]{1,0:T(8,128)(2,1)}, u32[]{:S(2)}, u32[]{:S(2)}) collective-permute-start(bf16[64,16000]{1,0:T(8,128)(2,1)} %collective-permute-done.49.refs_2_), channel_id=1, source_target_pairs={{0,1},{1,0},{2,3},{3,2},{4,5},{5,4},{6,7},{7,6}} | collective-permute-start | bytes 6144008 | tf_op jit(solution)/shard_map/ppermute | solution.py:315
  2873.8 165.9 %collective-permute-start.36 = (bf16[512,16000]{1,0:T(8,128)(2,1)}, bf16[512,16000]{1,0:T(8,128)(2,1)}, u32[]{:S(2)}, u32[]{:S(2)}) collective-permute-start(bf16[512,16000]{1,0:T(8,128)(2,1)} %collective-permute-done.35.refs_2_), channel_id=1, source_target_pairs={{0,1},{1,0},{2,3},{3,2},{4,5},{5,4},{6,7},{7,6}} | collective-permute-start | bytes 49152008 | tf_op jit(solution)/shard_map/ppermute | solution.py:315
  2947.4 77.0 %collective-permute-start.55 = (bf16[64,16000]{1,0:T(8,128)(2,1)}, bf16[64,16000]{1,0:T(8,128)(2,1)}, u32[]{:S(2)}, u32[]{:S(2)}) collective-permute-start(bf16[64,16000]{1,0:T(8,128)(2,1)} %collective-permute-done.53.refs_2_), channel_id=1, source_target_pairs={{0,2},{1,3},{2,0},{3,1},{4,6},{5,7},{6,4},{7,5}} | collective-permute-start | bytes 6144008 | tf_op jit(solution)/shard_map/ppermute | solution.py:309
  2947.7 76.9 %collective-permute-start.54 = (bf16[64,16000]{1,0:T(8,128)(2,1)}, bf16[64,16000]{1,0:T(8,128)(2,1)}, u32[]{:S(2)}, u32[]{:S(2)}) collective-permute-start(bf16[64,16000]{1,0:T(8,128)(2,1)} %collective-permute-done.53.refs_2_), channel_id=1, source_target_pairs={{0,1},{1,0},{2,3},{3,2},{4,5},{5,4},{6,7},{7,6}} | collective-permute-start | bytes 6144008 | tf_op jit(solution)/shard_map/ppermute | solution.py:315
  2947.7 91.3 %collective-permute-start.59 = (bf16[64,16000]{1,0:T(8,128)(2,1)}, bf16[64,16000]{1,0:T(8,128)(2,1)}, u32[]{:S(2)}, u32[]{:S(2)}) collective-permute-start(bf16[64,16000]{1,0:T(8,128)(2,1)} %collective-permute-done.57.refs_2_), channel_id=1, source_target_pairs={{0,2},{1,3},{2,0},{3,1},{4,6},{5,7},{6,4},{7,5}} | collective-permute-start | bytes 6144008 | tf_op jit(solution)/shard_map/ppermute | solution.py:309
  3024.4 66.7 %collective-permute-start.58 = (bf16[64,16000]{1,0:T(8,128)(2,1)}, bf16[64,16000]{1,0:T(8,128)(2,1)S(1)}, u32[]{:S(2)}, u32[]{:S(2)}) collective-permute-start(bf16[64,16000]{1,0:T(8,128)(2,1)} %collective-permute-done.57.refs_2_), channel_id=1, source_target_pairs={{0,1},{1,0},{2,3},{3,2},{4,5},{5,4},{6,7},{7,6}} | collective-permute-start | bytes 6144008 | tf_op jit(solution)/shard_map/ppermute | solution.py:315
  3024.6 67.0 %collective-permute-start.63 = (bf16[64,16000]{1,0:T(8,128)(2,1)S(1)}, bf16[64,16000]{1,0:T(8,128)(2,1)}, u32[]{:S(2)}, u32[]{:S(2)}) collective-permute-start(bf16[64,16000]{1,0:T(8,128)(2,1)S(1)} %copy-done.3), channel_id=1, source_target_pairs={{0,2},{1,3},{2,0},{3,1},{4,6},{5,7},{6,4},{7,5}} | collective-permute-start | bytes 6144008 | tf_op jit(solution)/shard_map/ppermute | solution.py:309
  3095.0 66.9 %collective-permute-start.64 = (bf16[64,16000]{1,0:T(8,128)(2,1)}, bf16[64,16000]{1,0:T(8,128)(2,1)}, u32[]{:S(2)}, u32[]{:S(2)}) collective-permute-start(bf16[64,16000]{1,0:T(8,128)(2,1)} %collective-permute-done.63.refs_4_), channel_id=1, source_target_pairs={{0,1},{1,0},{2,3},{3,2},{4,5},{5,4},{6,7},{7,6}} | collective-permute-start | bytes 6144008 | tf_op jit(solution)/shard_map/ppermute | solution.py:315
  3103.7 64.6 %collective-permute-start.66 = (bf16[48,16000]{1,0:T(8,128)(2,1)}, bf16[48,16000]{1,0:T(8,128)(2,1)}, u32[]{:S(2)}, u32[]{:S(2)}) collective-permute-start(bf16[48,16000]{1,0:T(8,128)(2,1)} %collective-permute-done.65.refs_2_), channel_id=1, source_target_pairs={{0,1},{1,0},{2,3},{3,2},{4,5},{5,4},{6,7},{7,6}} | collective-permute-start | bytes 4608008 | tf_op jit(solution)/shard_map/ppermute | solution.py:315
  3103.8 64.5 %collective-permute-start.68 = (bf16[48,16000]{1,0:T(8,128)(2,1)}, bf16[48,16000]{1,0:T(8,128)(2,1)}, u32[]{:S(2)}, u32[]{:S(2)}) collective-permute-start(bf16[48,16000]{1,0:T(8,128)(2,1)} %collective-permute-done.67.refs_4_), channel_id=1, source_target_pairs={{0,1},{1,0},{2,3},{3,2},{4,5},{5,4},{6,7},{7,6}} | collective-permute-start | bytes 4608008 | tf_op jit(solution)/shard_map/ppermute | solution.py:315
  3112.5 61.2 %collective-permute-start.70 = (bf16[16,16000]{1,0:T(8,128)(2,1)}, bf16[16,16000]{1,0:T(8,128)(2,1)}, u32[]{:S(2)}, u32[]{:S(2)}) collective-permute-start(bf16[16,16000]{1,0:T(8,128)(2,1)} %collective-permute-done.69.refs_2_), channel_id=1, source_target_pairs={{0,1},{1,0},{2,3},{3,2},{4,5},{5,4},{6,7},{7,6}} | collective-permute-start | bytes 1536008 | tf_op jit(solution)/shard_map/ppermute | solution.py:315
  3112.9 60.8 %collective-permute-start.72 = (bf16[16,16000]{1,0:T(8,128)(2,1)}, bf16[16,16000]{1,0:T(8,128)(2,1)}, u32[]{:S(2)}, u32[]{:S(2)}) collective-permute-start(bf16[16,16000]{1,0:T(8,128)(2,1)} %collective-permute-done.71.refs_4_), channel_id=1, source_target_pairs={{0,1},{1,0},{2,3},{3,2},{4,5},{5,4},{6,7},{7,6}} | collective-permute-start | bytes 1536008 | tf_op jit(solution)/shard_map/ppermute | solution.py:315
  (52 other events, 2069.2 us)

commit v3 on v2

--- a/solution.py
+++ b/solution.py
@@ -15,9 +15,13 @@
 LAG = 4
 TILE_BYTES = 1 << 20
 
-HEAD_CUTS = (0, 64, 128, 192, 256, 320, 384, 448, 496, 512)
-HEAD_TILE = 256
+HEAD_CUTS = (0, 192, 224, 320, 416, 480, 512)
+HEAD_TILE = 96
 TOKEN_TILE = 256
+PROJECT_TILE = 512
+HEADS_AT_ONCE = 2
+MASKED = -1e30
+EXP2_SCALE = HEAD_DIM ** -0.5 * 1.4426950408889634
 LOGIT_ROWS = 16
 
 
@@ -124,7 +128,7 @@
 def project(prompts, gain, weight, kv_heads, cosines, sines):
     batch, seq_len, model = prompts.shape
     q_heads = weight.shape[1] // HEAD_DIM - 2 * kv_heads
-    tile = TOKEN_TILE
+    tile = PROJECT_TILE
     cos_both = jnp.concatenate([cosines, cosines], axis=-1)
     sin_both = jnp.concatenate([-sines, sines], axis=-1)
 
@@ -158,24 +162,40 @@
     block = pl.program_id(1)
     rows = q_ref.shape[2]
     length = length_ref[prompt]
-    for count in range(1, k_ref.shape[2] // rows + 1):
-
-        @pl.when(block == count - 1)
+    contract = (((1,), (1,)), ((), ()))
+    for count in range(k_ref.shape[2] // rows):
+
+        @pl.when(block == count)
         def _(count=count):
-            keys = count * rows
-
-            @pl.loop(0, q_ref.shape[1])
-            def _(head):
-                scores = lax.dot_general(
-                    q_ref[0, head], k_ref[0, 0, :keys], (((1,), (1,)), ((), ())), preferred_element_type=jnp.float32
-                ) * HEAD_DIM ** -0.5
-                query_pos = (count - 1) * rows + lax.broadcasted_iota(jnp.int32, (rows, keys), 0)
-                key_pos = lax.broadcasted_iota(jnp.int32, (rows, keys), 1)
-                scores = jnp.where((key_pos <= query_pos) & (key_pos < length), scores, -1e30)
-                weights = jnp.exp(scores - jnp.max(scores, axis=-1, keepdims=True))
-                probs = (weights * (1.0 / jnp.sum(weights, axis=-1, keepdims=True))).astype(jnp.bfloat16)
-                out = jnp.dot(probs, v_ref[0, 0, :keys], preferred_element_type=jnp.float32)
+            first = count * rows
+            keys = first + rows
+            bias = jnp.where(lax.broadcasted_iota(jnp.int32, (1, keys), 1) < length, 0.0, MASKED)
+            causal = lax.broadcasted_iota(jnp.int32, (rows, rows), 1) <= lax.broadcasted_iota(jnp.int32, (rows, rows), 0)
+
+            def one_head(head):
+                query = q_ref[0, head]
+                near = lax.dot_general(query, k_ref[0, 0, first:keys], contract, preferred_element_type=jnp.float32)
+                near = jnp.where(causal, near * EXP2_SCALE + bias[:, first:], MASKED)
+                top = jnp.max(near, axis=-1, keepdims=True)
+                if count:
+                    far = lax.dot_general(query, k_ref[0, 0, :first], contract, preferred_element_type=jnp.float32)
+                    far = far * EXP2_SCALE + bias[:, :first]
+                    top = jnp.maximum(top, jnp.max(far, axis=-1, keepdims=True))
+                    far = jnp.exp2(far - top)
+                near = jnp.exp2(near - top)
+                total = jnp.sum(near, axis=-1, keepdims=True)
+                if count:
+                    total += jnp.sum(far, axis=-1, keepdims=True)
+                inverse = 1.0 / total
+                out = jnp.dot((near * inverse).astype(jnp.bfloat16), v_ref[0, 0, first:keys], preferred_element_type=jnp.float32)
+                if count:
+                    out += jnp.dot((far * inverse).astype(jnp.bfloat16), v_ref[0, 0, :first], preferred_element_type=jnp.float32)
                 o_ref[:, pl.ds(pl.multiple_of(head * HEAD_DIM, HEAD_DIM), HEAD_DIM)] = out.astype(jnp.bfloat16)
+
+            @pl.loop(0, q_ref.shape[1] // HEADS_AT_ONCE)
+            def _(step):
+                for side in range(HEADS_AT_ONCE):
+                    one_head(HEADS_AT_ONCE * step + side)
 
 
 def attend(prompt, lengths, queries, keys, values):
@@ -272,6 +292,49 @@
         store(s).wait()
 
 
+def near_kernel(numbers, tile, slot_of, z_ref, *refs):
+    ins = refs[: len(numbers)]
+    logits_ref, buf, sem = refs[len(numbers) :]
+    me = lax.axis_index("dp") * 2 + lax.axis_index("tp")
+    slots = buf.shape[0]
+    cols = buf.shape[2]
+    width = cols // 5
+    steps = [(piece, row) for piece in range(len(numbers)) for row in range(0, ins[0].shape[0], tile)]
+
+    def load(s):
+        piece, row = steps[s]
+        return pltpu.make_async_copy(ins[piece].at[pl.ds(row, tile)], buf.at[s % slots], sem.at[s % slots])
+
+    for s in range(slots - 1):
+        load(s).start()
+    for s, (piece, row) in enumerate(steps):
+        if s + slots - 1 < len(steps):
+            load(s + slots - 1).start()
+        load(s).wait()
+        z = z_ref[slot_of(numbers[piece], me)][:, row : row + tile]
+
+        @pl.loop(0, 5)
+        def _(j, z=z, s=s):
+            at = pl.ds(pl.multiple_of(j * width, 128), width)
+            part = jnp.dot(z, buf[s % slots, :, at], preferred_element_type=jnp.float32)
+            logits_ref[:, at] = part if s == 0 else logits_ref[:, at] + part
+
+
+def near_logits(numbers, pieces, slot_of, z):
+    _, cols = pieces[0].shape
+    tile, slots = 256, 5
+    vmem = pl.BlockSpec(memory_space=pltpu.VMEM)
+    return pl.pallas_call(
+        functools.partial(near_kernel, numbers, tile, slot_of),
+        out_shape=jax.ShapeDtypeStruct((LOGIT_ROWS, cols), jnp.float32),
+        in_specs=[vmem] + [pl.BlockSpec(memory_space=pl.ANY)] * len(pieces),
+        out_specs=vmem,
+        scratch_shapes=[pltpu.VMEM((slots, tile, cols), jnp.bfloat16), pltpu.SemaphoreType.DMA((slots,))],
+        compiler_params=pltpu.CompilerParams(vmem_limit_bytes=52 << 20),
+        name="near_logits",
+    )(z, *pieces)
+
+
 def place_head(numbers, pieces, shape, slot_of, block, base, z, acc, into):
     rows, cols = pieces[0].shape
     tile = min(rows, HEAD_TILE)
@@ -378,9 +441,18 @@
         up = column_pieces([w_up[0]])
         (o_weight,) = place(o_pieces, [((q_half, model), 0)], row_slot, block)
         (gate_weight,) = place(gate, [((model, ffn_half), 0)], column_slot, block)
-        (up_weight,) = place(up, [((model, ffn_half), 0)], column_slot, block)
-        down = row_pieces(w_down[0])
-        (down_weight,) = place(down, [((ffn_half, model), 0)], row_slot, w_down.shape[1])
+        (up_weight,) = place([up[j] for j in (0, 2, 4, 6)], [((model, ffn_half), 0)], lambda j, me: column_slot(2 * j, me), block)
+        (up_weight,) = place(
+            [up[j] for j in (1, 3, 5, 7)], [((model, ffn_half), 0)], lambda j, me: column_slot(2 * j + 1, me), block, into=[up_weight]
+        )
+        rows = w_down.shape[1]
+        down_weight = None
+        for n, (first, end) in enumerate(((0, 4 * rows // 7), (4 * rows // 7, rows))):
+            half = lax.slice_in_dim(w_down[0], first, end, axis=0)
+            pieces = row_pieces(half)
+            (down_weight,) = place(
+                pieces, [((ffn_half, model), 0)], row_slot, rows, base=first, into=None if n == 0 else [down_weight]
+            )
 
         batch, seq_len, _ = prompts.shape
         kv_count = kv_half // HEAD_DIM
@@ -413,11 +485,11 @@
         own, _ = halves([w_head])
         own_x = over_x(own)
         near = {0: own, 2: over_core(own), 4: own_x, 6: over_core(own_x)}
+        (head,) = place([near[0], near[2]], [((model, vocab_half), 0)], lambda j, me: column_slot((0, 2)[j], me), block)
         (head,) = place(
-            list(near.values()), [((model, vocab_half), 0)], lambda j, me: column_slot(list(near)[j], me), block
+            [near[4], near[6]], [((model, vocab_half), 0)], lambda j, me: column_slot((4, 6)[j], me), block, into=[head]
         )
-        me = 2 * dp_idx + tp_idx
-        acc = sum(jnp.dot(per_block[column_slot(j, me)], piece, preferred_element_type=jnp.float32) for j, piece in near.items())
+        acc = near_logits(tuple(near), list(near.values()), column_slot, per_block)
         for first, last_row in zip(HEAD_CUTS, HEAD_CUTS[1:]):
             _, other = halves([w_head], (first, last_row))
             far = over_y(other)

time: 3190 us -> 3260 us (1.022)
  waiting for transfers between devices: 1430 us -> 1520 us
    ppermute x18 -> x16, waiting for transfers between devices: 757 us -> 849 us  [over_x(): return lax.ppermute(value, 'dp', x_pairs)]
    ppermute x18 -> x16, waiting for transfers between devices: 666 us -> 664 us  [over_y(): return lax.ppermute(value, 'tp', y_pairs)]
    pallas_call x6 -> x9, Pallas kernels: 200 us -> 200 us  [place(): pl.pallas_call(functools.partial(place_kernel, steps, len(pieces), len(al...]
  transfers between devices with their start and end apart: 74 -> 66, of which waited for: 19 -> 16; matrix products, arithmetic and copies ran while one was open for 33% -> 32% of each run, Pallas kernels for 20% -> 19%
where the time goes in v3:
time: 3260 us; the launch traced here: 3250 us
  waiting for transfers between devices  1520 us (47%)
  matrix products  929 us (28%)
  Pallas kernels  608 us (19%)
  local copies, waits for them, and re-layouts  104 us (3%)
  starting transfers between devices  42.5 us (1%)
  other arithmetic  38.5 us (1%)
    ppermute x16, waiting for transfers between devices, over_x(): return lax.ppermute(value, 'dp', x_pairs)  849 us
    ppermute x16, waiting for transfers between devices, over_y(): return lax.ppermute(value, 'tp', y_pairs)  664 us
    dot_general x4, matrix products, layer_program(): jnp.dot(act, down_weight, preferred_element_type=jnp.float32)  293 us
    dot_general x4, matrix products, layer_program(): jnp.dot(normed_mlp, gate_weight, preferred_element_type=jnp.float32)  276 us
    dot_general x4, matrix products, layer_program(): up_proj = jnp.dot(normed_mlp, up_weight, preferred_element_type=jnp.float32)  273 us
    pallas_call x9, Pallas kernels, place(): pl.pallas_call(functools.partial(place_kernel, steps, len(pieces), len(al...  200 us
    pallas_call x4, Pallas kernels, attend(): pl.pallas_call(functools.partial(attend_kernel, prompt), grid=(kv_heads,...  151 us
    pallas_call x1, Pallas kernels, project(): pl.pallas_call(project_kernel, grid=(batch, seq_len // tile), out_shape=[...  136 us
  transfers between devices with their start and end apart: 66, of which 16 were waited for; matrix products, arithmetic and copies ran while one was open for 32% of the time, Pallas kernels for 19%

profile of v3, /device:TPU:0, one launch (start us, length us, event | category | flops | bytes accessed | tf_op | source)
XLA Modules:
  0.0 3249.9 jit_solution(8308525940560823971)
XLA Ops:
  11.6 7.9 slice_bitcast_fusion
  19.4 13.5 constant_dynamic-slice_fusion.1.refs_0_
  32.9 47.4 %collective-permute-done.refs_1_ = bf16[512,3072]{1,0:T(8,128)(2,1)} collective-permute-done((bf16[512,3072]{1,0:T(8,128)(2,1)}, bf16[512,3072]{1,0:T(8,128)(2,1)}, u32[]{:S(2)}, u32[]{:S(2)}) %collective-permute-start) | collective-permute-done | bytes 3145760 | tf_op jit(solution)/shard_map/ppermute | solution.py:375
  80.6 6.3 slice_bitcast_fusion.1
  87.0 79.5 %collective-permute-done.7 = bf16[512,4096]{1,0:T(8,128)(2,1)} collective-permute-done((bf16[512,4096]{1,0:T(8,128)(2,1)}, bf16[512,4096]{1,0:T(8,128)(2,1)}, u32[]{:S(2)}, u32[]{:S(2)}) %collective-permute-start.7) | collective-permute-done | bytes 4194336 | tf_op jit(solution)/shard_map/ppermute | solution.py:372
  166.4 5.9 broadcast_select_fusion.4
  174.4 5.5 dynamic-slice_bitcast_fusion.2
  180.5 52.5 %collective-permute-done.4.refs_5_ = bf16[512,3072]{1,0:T(8,128)(2,1)} collective-permute-done((bf16[512,3072]{1,0:T(8,128)(2,1)}, bf16[512,3072]{1,0:T(8,128)(2,1)}, u32[]{:S(2)}, u32[]{:S(2)}) %collective-permute-start.4) | collective-permute-done | bytes 3145760 | tf_op jit(solution)/shard_map/ppermute | solution.py:372
  243.4 10.4 dynamic-slice_bitcast_fusion
  255.4 24.5 shard_map.221
  279.9 5.6 collective-permute-done.45.refs_2_
  288.6 135.9 %project.1 = (bf16[4,4,1024,128]{3,2,1,0:T(8,128)(2,1)}, bf16[4,4,1024,128]{3,2,1,0:T(8,128)(2,1)}, bf16[4,16,1024,128]{3,2,1,0:T(8,128)(2,1)}) custom-call(bf16[4,1024,4096]{2,1,0:T(8,128)(2,1)} %x_ref.9, bf16[1,4096]{1,0:T(2,128)(2,1)} %gain_ref.5, bf16[4096,3072]{1,0:T(8,128)(2,1)} %get-tuple-element.41.w_ref, f32[1024,128]{1,0:T(8,128)} %get-tuple-element.102.cos_ref, ...), custom_call_target="tpu_custom_call" | custom-call | flops 103079215104 | bytes 33554432 | tf_op jit(solution)/shard_map/project/pallas_call | solution.py:143
  429.3 37.8 %attend.4 = bf16[1024,2048]{1,0:T(8,128)(2,1)S(1)} custom-call(s32[4]{0:T(128)S(1)} %copy-done.15, bf16[4,16,1024,128]{3,2,1,0:T(8,128)(2,1)} %get-tuple-element.42.q_ref, bf16[4,4,1024,128]{3,2,1,0:T(8,128)(2,1)S(1)} %copy-done.16, bf16[4,4,1024,128]{3,2,1,0:T(8,128)(2,1)S(1)} %copy-done.17), custom_call_target="tpu_custom_call" | custom-call | flops 8589934592 | bytes 16777216 | tf_op jit(solution)/shard_map/attend/pallas_call | solution.py:207
  467.1 37.7 %attend.5 = bf16[1024,2048]{1,0:T(8,128)(2,1)S(1)} custom-call(s32[4]{0:T(128)S(1)} %copy-done.15, bf16[4,16,1024,128]{3,2,1,0:T(8,128)(2,1)} %get-tuple-element.42.q_ref, bf16[4,4,1024,128]{3,2,1,0:T(8,128)(2,1)S(1)} %copy-done.16, bf16[4,4,1024,128]{3,2,1,0:T(8,128)(2,1)S(1)} %copy-done.17), custom_call_target="tpu_custom_call" | custom-call | flops 8589934592 | bytes 16777216 | tf_op jit(solution)/shard_map/attend/pallas_call | solution.py:207
  504.8 37.7 %attend.6 = bf16[1024,2048]{1,0:T(8,128)(2,1)S(1)} custom-call(s32[4]{0:T(128)S(1)} %copy-done.15, bf16[4,16,1024,128]{3,2,1,0:T(8,128)(2,1)} %get-tuple-element.42.q_ref, bf16[4,4,1024,128]{3,2,1,0:T(8,128)(2,1)S(1)} %copy-done.16, bf16[4,4,1024,128]{3,2,1,0:T(8,128)(2,1)S(1)} %copy-done.17), custom_call_target="tpu_custom_call" | custom-call | flops 8589934592 | bytes 16777216 | tf_op jit(solution)/shard_map/attend/pallas_call | solution.py:207
  542.6 38.1 %attend.7 = bf16[1024,2048]{1,0:T(8,128)(2,1)S(1)} custom-call(s32[4]{0:T(128)S(1)} %copy-done.15, bf16[4,16,1024,128]{3,2,1,0:T(8,128)(2,1)} %get-tuple-element.42.q_ref, bf16[4,4,1024,128]{3,2,1,0:T(8,128)(2,1)S(1)} %copy-done.16, bf16[4,4,1024,128]{3,2,1,0:T(8,128)(2,1)S(1)} %copy-done.17), custom_call_target="tpu_custom_call" | custom-call | flops 8589934592 | bytes 16777216 | tf_op jit(solution)/shard_map/attend/pallas_call | solution.py:207
  580.7 12.4 shard_map.222
  593.2 21.6 convolution_convert_fusion.3.mine_ref
  614.8 91.7 %collective-permute-done.25 = bf16[768,4096]{1,0:T(8,128)(2,1)} collective-permute-done((bf16[768,4096]{1,0:T(8,128)(2,1)}, bf16[768,4096]{1,0:T(8,128)(2,1)}, u32[]{:S(2)}, u32[]{:S(2)}) %collective-permute-start.25) | collective-permute-done | bytes 6291488 | tf_op jit(solution)/shard_map/ppermute | solution.py:372
  709.0 21.6 convolution_convert_fusion.2.mine_ref
  730.6 21.7 convolution_convert_fusion.1.mine_ref
  752.3 21.5 convolution_convert_fusion.mine_ref
  773.8 92.2 %collective-permute-done.18.refs_0_ = bf16[512,7168]{1,0:T(8,128)(2,1)} collective-permute-done((bf16[512,7168]{1,0:T(8,128)(2,1)}, bf16[512,7168]{1,0:T(8,128)(2,1)}, u32[]{:S(2)}, u32[]{:S(2)}) %collective-permute-start.18) | collective-permute-done | bytes 7340064 | tf_op jit(solution)/shard_map/ppermute | solution.py:375
  866.3 23.9 collective-permute-done.29
  892.0 153.8 %collective-permute-done.15.refs_5_ = bf16[512,7168]{1,0:T(8,128)(2,1)} collective-permute-done((bf16[512,7168]{1,0:T(8,128)(2,1)}, bf16[512,7168]{1,0:T(8,128)(2,1)}, u32[]{:S(2)}, u32[]{:S(2)}) %collective-permute-start.15) | collective-permute-done | bytes 7340064 | tf_op jit(solution)/shard_map/ppermute | solution.py:372
  1060.1 5.7 constant_dynamic-slice_fusion
  1066.4 163.0 %collective-permute-done.34.other_ref = bf16[1024,4096]{1,0:T(8,128)(2,1)} collective-permute-done((bf16[1024,4096]{1,0:T(8,128)(2,1)}, bf16[1024,4096]{1,0:T(8,128)(2,1)}, u32[]{:S(2)}, u32[]{:S(2)}) %collective-permute-start.34) | collective-permute-done | bytes 8388640 | tf_op jit(solution)/shard_map/ppermute | solution.py:375
  1229.4 179.8 %collective-permute-done.35.other_ref = bf16[1024,4096]{1,0:T(8,128)(2,1)} collective-permute-done((bf16[1024,4096]{1,0:T(8,128)(2,1)}, bf16[1024,4096]{1,0:T(8,128)(2,1)}, u32[]{:S(2)}, u32[]{:S(2)}) %collective-permute-start.35) | collective-permute-done | bytes 8388640 | tf_op jit(solution)/shard_map/ppermute | solution.py:375
  1410.7 175.8 %collective-permute-done.36.other_ref = bf16[1024,4096]{1,0:T(8,128)(2,1)} collective-permute-done((bf16[1024,4096]{1,0:T(8,128)(2,1)}, bf16[1024,4096]{1,0:T(8,128)(2,1)}, u32[]{:S(2)}, u32[]{:S(2)}) %collective-permute-start.36) | collective-permute-done | bytes 8388640 | tf_op jit(solution)/shard_map/ppermute | solution.py:375
  1589.5 5.9 constant_dynamic-slice_fusion.8
  1595.4 11.1 broadcast_select_fusion.2
  1606.6 10.2 broadcast_select_fusion
  1616.8 17.8 shard_map.224.refs_4_
  1634.6 23.0 shard_map.228.refs_2_
  1657.7 12.0 mix.4
  1676.1 12.0 mix.5
  1694.7 12.0 mix.6
  1713.4 12.2 mix.7
  1736.5 37.9 %shard_map.223 = bf16[4096,7168]{1,0:T(8,128)(2,1)} custom-call(bf16[512,7168]{1,0:T(8,128)(2,1)} %get-tuple-element.80.refs_0_, bf16[512,7168]{1,0:T(8,128)(2,1)} %collective-permute-done.11.refs_1_, bf16[512,7168]{1,0:T(8,128)(2,1)S(1)} %collective-permute-done.12.refs_2_, bf16[512,7168]{1,0:T(8,128)(2,1)} %collective-permute-done.13.refs_3_, ...), custom_call_target="tpu_custom_call" | custom-call | tf_op jit(solution)/shard_map/pallas_call | solution.py:89
  1774.5 69.5 %fusion.16 = f32[1024,7168]{1,0:T(8,128)} fusion(bf16[1024,4096]{1,0:T(8,128)(2,1)} %copy-done.9, bf16[4096,7168]{1,0:T(8,128)(2,1)} %shard_map.223), kind=kOutput, calls=%fused_computation.90 | convolution fusion | flops 60129542144 | bytes 96468992 | tf_op jit(solution)/shard_map/dot_general | solution.py:469
  1844.5 23.1 shard_map.225
  1867.6 67.5 %fusion.17 = f32[1024,7168]{1,0:T(8,128)} fusion(bf16[1024,4096]{1,0:T(8,128)(2,1)S(1)} %bitcast.104, bf16[4096,7168]{1,0:T(8,128)(2,1)} %shard_map.225), kind=kOutput, calls=%fused_computation.91 | convolution fusion | flops 60129542144 | bytes 96468992 | tf_op jit(solution)/shard_map/dot_general | solution.py:470
  1935.1 71.9 %fusion.18 = f32[1024,7168]{1,0:T(8,128)} fusion(bf16[1024,4096]{1,0:T(8,128)(2,1)} %copy-done.10, bf16[4096,7168]{1,0:T(8,128)(2,1)} %shard_map.223), kind=kOutput, calls=%fused_computation.92 | convolution fusion | flops 60129542144 | bytes 96468992 | tf_op jit(solution)/shard_map/dot_general | solution.py:469
  2007.0 67.8 %fusion.19 = f32[1024,7168]{1,0:T(8,128)} fusion(bf16[1024,4096]{1,0:T(8,128)(2,1)S(1)} %copy-done.11, bf16[4096,7168]{1,0:T(8,128)(2,1)} %shard_map.225), kind=kOutput, calls=%fused_computation.93 | convolution fusion | flops 60129542144 | bytes 96468992 | tf_op jit(solution)/shard_map/dot_general | solution.py:470
  2074.8 67.6 %fusion.20 = f32[1024,7168]{1,0:T(8,128)} fusion(bf16[1024,4096]{1,0:T(8,128)(2,1)S(1)} %copy-done.13, bf16[4096,7168]{1,0:T(8,128)(2,1)} %shard_map.223), kind=kOutput, calls=%fused_computation.94 | convolution fusion | flops 60129542144 | bytes 96468992 | tf_op jit(solution)/shard_map/dot_general | solution.py:469
  2142.4 67.8 %fusion.21 = f32[1024,7168]{1,0:T(8,128)} fusion(bf16[1024,4096]{1,0:T(8,128)(2,1)S(1)} %copy-done.14, bf16[4096,7168]{1,0:T(8,128)(2,1)} %shard_map.225), kind=kOutput, calls=%fused_computation.95 | convolution fusion | flops 60129542144 | bytes 96468992 | tf_op jit(solution)/shard_map/dot_general | solution.py:470
  2210.2 67.2 %fusion.22 = f32[1024,7168]{1,0:T(8,128)} fusion(bf16[1024,4096]{1,0:T(8,128)(2,1)S(1)} %copy-done.8, bf16[4096,7168]{1,0:T(8,128)(2,1)} %shard_map.223), kind=kOutput, calls=%fused_computation.96 | convolution fusion | flops 60129542144 | bytes 96468992 | tf_op jit(solution)/shard_map/dot_general | solution.py:469
  2277.9 69.9 %fusion.23 = f32[1024,7168]{1,0:T(8,128)} fusion(bf16[1024,4096]{1,0:T(8,128)(2,1)} %copy-done.7, bf16[4096,7168]{1,0:T(8,128)(2,1)} %shard_map.225), kind=kOutput, calls=%fused_computation.97 | convolution fusion | flops 60129542144 | bytes 96468992 | tf_op jit(solution)/shard_map/dot_general | solution.py:470
  2348.2 23.0 shard_map.226.refs_4_
  2374.7 14.8 shard_map.227
  2389.5 73.2 %fusion = bf16[1024,4096]{1,0:T(8,128)(2,1)} fusion(bf16[7168,4096]{1,0:T(8,128)(2,1)} %shard_map.227, f32[1024,7168]{1,0:T(8,128)} %fusion.17, f32[1024,7168]{1,0:T(8,128)} %fusion.16), kind=kOutput, calls=%fused_computation.4 | convolution fusion | flops 60173582336 | bytes 125829120 | tf_op jit(solution)/shard_map/dot_general | solution.py:472
  2464.7 259.6 %collective-permute-done.63.refs_4_ = bf16[32,16000]{1,0:T(8,128)(2,1)} collective-permute-done((bf16[32,16000]{1,0:T(8,128)(2,1)}, bf16[32,16000]{1,0:T(8,128)(2,1)}, u32[]{:S(2)}, u32[]{:S(2)}) %collective-permute-start.63) | collective-permute-done | bytes 1024032 | tf_op jit(solution)/shard_map/ppermute | solution.py:372
  2726.4 73.2 %fusion.1 = bf16[1024,4096]{1,0:T(8,128)(2,1)} fusion(bf16[7168,4096]{1,0:T(8,128)(2,1)} %shard_map.227, f32[1024,7168]{1,0:T(8,128)} %fusion.19, f32[1024,7168]{1,0:T(8,128)} %fusion.18), kind=kOutput, calls=%fused_computation.5 | convolution fusion | flops 60173582336 | bytes 125829120 | tf_op jit(solution)/shard_map/dot_general | solution.py:472
  2803.2 73.3 %fusion.2 = bf16[1024,4096]{1,0:T(8,128)(2,1)} fusion(bf16[7168,4096]{1,0:T(8,128)(2,1)} %shard_map.227, f32[1024,7168]{1,0:T(8,128)} %fusion.21, f32[1024,7168]{1,0:T(8,128)} %fusion.20), kind=kOutput, calls=%fused_computation.6 | convolution fusion | flops 60173582336 | bytes 125829120 | tf_op jit(solution)/shard_map/dot_general | solution.py:472
  2877.0 58.1 %collective-permute-done.55.refs_4_ = bf16[96,16000]{1,0:T(8,128)(2,1)} collective-permute-done((bf16[96,16000]{1,0:T(8,128)(2,1)S(1)}, bf16[96,16000]{1,0:T(8,128)(2,1)}, u32[]{:S(2)}, u32[]{:S(2)}) %collective-permute-start.55) | collective-permute-done | bytes 3072032 | tf_op jit(solution)/shard_map/ppermute | solution.py:372
  2935.2 129.8 %collective-permute-done.43.refs_4_ = bf16[192,16000]{1,0:T(8,128)(2,1)} collective-permute-done((bf16[192,16000]{1,0:T(8,128)(2,1)}, bf16[192,16000]{1,0:T(8,128)(2,1)}, u32[]{:S(2)}, u32[]{:S(2)}) %collective-permute-start.43) | collective-permute-done | bytes 6144032 | tf_op jit(solution)/shard_map/ppermute | solution.py:372
  3064.9 73.2 %fusion.3 = bf16[1024,4096]{1,0:T(8,128)(2,1)} fusion(bf16[7168,4096]{1,0:T(8,128)(2,1)} %shard_map.227, f32[1024,7168]{1,0:T(8,128)} %fusion.23, f32[1024,7168]{1,0:T(8,128)} %fusion.22), kind=kOutput, calls=%fused_computation.7 | convolution fusion | flops 60173582336 | bytes 125829120 | tf_op jit(solution)/shard_map/dot_general | solution.py:472
  3148.3 21.8 near_logits.1.refs_1_
  3170.1 23.0 shard_map.229.refs_6_
  3193.1 17.1 shard_map.230
  3215.0 8.7 shard_map.232
  3223.7 9.1 shard_map.233
  3232.8 6.9 shard_map.234
  3239.8 4.7 shard_map.235
  (234 shorter events, 113.5 us)
Async XLA Ops:
  4.2 82.8 %collective-permute-start.3 = (bf16[512,3072]{1,0:T(8,128)(2,1)S(1)}, bf16[512,3072]{1,0:T(8,128)(2,1)}, u32[]{:S(2)}, u32[]{:S(2)}) collective-permute-start(bf16[512,3072]{1,0:T(8,128)(2,1)S(1)} %pad_maximum_fusion.refs_0_), channel_id=1, source_target_pairs={{0,2},{1,3},{2,0},{3,1},{4,6},{5,7},{6,4},{7,5}} | collective-permute-start | bytes 9437192 | tf_op jit(solution)/shard_map/ppermute | solution.py:372
  7.5 172.5 %collective-permute-start.1 = (bf16[512,3072]{1,0:T(8,128)(2,1)S(1)}, bf16[512,3072]{1,0:T(8,128)(2,1)}, u32[]{:S(2)}, u32[]{:S(2)}) collective-permute-start(bf16[512,3072]{1,0:T(8,128)(2,1)S(1)} %pad_maximum_fusion.refs_0_), channel_id=1, source_target_pairs={{0,1},{1,0},{2,3},{3,2},{4,5},{5,4},{6,7},{7,6}} | collective-permute-start | bytes 9437192 | tf_op jit(solution)/shard_map/ppermute | solution.py:378
  9.5 70.8 %collective-permute-start = (bf16[512,3072]{1,0:T(8,128)(2,1)}, bf16[512,3072]{1,0:T(8,128)(2,1)}, u32[]{:S(2)}, u32[]{:S(2)}) collective-permute-start(bf16[512,3072]{1,0:T(8,128)(2,1)} %pad_maximum_fusion.1), channel_id=1, source_target_pairs={{0,4},{4,0},{1,5},{5,1},{2,6},{6,2},{3,7},{7,3}} | collective-permute-start | bytes 9437192 | tf_op jit(solution)/shard_map/ppermute | solution.py:375
  11.0 155.4 %collective-permute-start.7 = (bf16[512,4096]{1,0:T(8,128)(2,1)}, bf16[512,4096]{1,0:T(8,128)(2,1)}, u32[]{:S(2)}, u32[]{:S(2)}) collective-permute-start(bf16[512,4096]{1,0:T(8,128)(2,1)} %bitcast.9), channel_id=1, source_target_pairs={{0,2},{1,3},{2,0},{3,1},{4,6},{5,7},{6,4},{7,5}} | collective-permute-start | bytes 12582920 | tf_op jit(solution)/shard_map/ppermute | solution.py:372
  80.3 152.7 %collective-permute-start.4 = (bf16[512,3072]{1,0:T(8,128)(2,1)}, bf16[512,3072]{1,0:T(8,128)(2,1)}, u32[]{:S(2)}, u32[]{:S(2)}) collective-permute-start(bf16[512,3072]{1,0:T(8,128)(2,1)} %collective-permute-done.refs_1_), channel_id=1, source_target_pairs={{0,2},{1,3},{2,0},{3,1},{4,6},{5,7},{6,4},{7,5}} | collective-permute-start | bytes 9437192 | tf_op jit(solution)/shard_map/ppermute | solution.py:372
  86.9 154.7 %collective-permute-start.5 = (bf16[512,3072]{1,0:T(8,128)(2,1)}, bf16[512,3072]{1,0:T(8,128)(2,1)}, u32[]{:S(2)}, u32[]{:S(2)}) collective-permute-start(bf16[512,3072]{1,0:T(8,128)(2,1)} %collective-permute-done.3.refs_4_), channel_id=1, source_target_pairs={{0,1},{1,0},{2,3},{3,2},{4,5},{5,4},{6,7},{7,6}} | collective-permute-start | bytes 9437192 | tf_op jit(solution)/shard_map/ppermute | solution.py:378
  172.3 114.7 %collective-permute-start.8 = (bf16[512,4096]{1,0:T(8,128)(2,1)}, bf16[512,4096]{1,0:T(8,128)(2,1)}, u32[]{:S(2)}, u32[]{:S(2)}) collective-permute-start(bf16[512,4096]{1,0:T(8,128)(2,1)} %get-tuple-element.81), channel_id=1, source_target_pairs={{0,4},{4,0},{1,5},{5,1},{2,6},{6,2},{3,7},{7,3}} | collective-permute-start | bytes 12582920 | tf_op jit(solution)/shard_map/ppermute | solution.py:375
  174.4 114.2 %collective-permute-start.9 = (bf16[512,4096]{1,0:T(8,128)(2,1)}, bf16[512,4096]{1,0:T(8,128)(2,1)}, u32[]{:S(2)}, u32[]{:S(2)}) collective-permute-start(bf16[512,4096]{1,0:T(8,128)(2,1)} %get-tuple-element.82.refs_0_), channel_id=1, source_target_pairs={{0,1},{1,0},{2,3},{3,2},{4,5},{5,4},{6,7},{7,6}} | collective-permute-start | bytes 12582920 | tf_op jit(solution)/shard_map/ppermute | solution.py:378
  180.0 73.9 %collective-permute-start.2 = (bf16[512,3072]{1,0:T(8,128)(2,1)}, bf16[512,3072]{1,0:T(8,128)(2,1)}, u32[]{:S(2)}, u32[]{:S(2)}) collective-permute-start(bf16[512,3072]{1,0:T(8,128)(2,1)} %collective-permute-done.refs_1_), channel_id=1, source_target_pairs={{0,1},{1,0},{2,3},{3,2},{4,5},{5,4},{6,7},{7,6}} | collective-permute-start | bytes 9437192 | tf_op jit(solution)/shard_map/ppermute | solution.py:378
  233.0 22.4 collective-permute-start.6
  241.7 43.8 %collective-permute-start.45 = (bf16[32,16000]{1,0:T(8,128)(2,1)S(1)}, bf16[32,16000]{1,0:T(8,128)(2,1)}, u32[]{:S(2)}, u32[]{:S(2)}) collective-permute-start(bf16[32,16000]{1,0:T(8,128)(2,1)S(1)} %get-tuple-element.70), channel_id=1, source_target_pairs={{0,4},{4,0},{1,5},{5,1},{2,6},{6,2},{3,7},{7,3}} | collective-permute-start | bytes 3072008 | tf_op jit(solution)/shard_map/ppermute | solution.py:375
  253.9 454.6 %collective-permute-start.23 = (bf16[512,7168]{1,0:T(8,128)(2,1)}, bf16[512,7168]{1,0:T(8,128)(2,1)}, u32[]{:S(2)}, u32[]{:S(2)}) collective-permute-start(bf16[512,7168]{1,0:T(8,128)(2,1)} %get-tuple-element.77.refs_0_), channel_id=1, source_target_pairs={{0,2},{1,3},{2,0},{3,1},{4,6},{5,7},{6,4},{7,5}} | collective-permute-start | bytes 22020104 | tf_op jit(solution)/shard_map/ppermute | solution.py:372
  255.4 453.4 %collective-permute-start.22 = (bf16[512,7168]{1,0:T(8,128)(2,1)}, bf16[512,7168]{1,0:T(8,128)(2,1)}, u32[]{:S(2)}, u32[]{:S(2)}) collective-permute-start(bf16[512,7168]{1,0:T(8,128)(2,1)} %get-tuple-element.77.refs_0_), channel_id=1, source_target_pairs={{0,1},{1,0},{2,3},{3,2},{4,5},{5,4},{6,7},{7,6}} | collective-permute-start | bytes 22020104 | tf_op jit(solution)/shard_map/ppermute | solution.py:378
  285.5 421.2 %collective-permute-start.11 = (bf16[512,7168]{1,0:T(8,128)(2,1)}, bf16[512,7168]{1,0:T(8,128)(2,1)}, u32[]{:S(2)}, u32[]{:S(2)}) collective-permute-start(bf16[512,7168]{1,0:T(8,128)(2,1)} %get-tuple-element.79), channel_id=1, source_target_pairs={{0,4},{4,0},{1,5},{5,1},{2,6},{6,2},{3,7},{7,3}} | collective-permute-start | bytes 22020104 | tf_op jit(solution)/shard_map/ppermute | solution.py:375
  287.1 421.3 %collective-permute-start.14 = (bf16[512,7168]{1,0:T(8,128)(2,1)}, bf16[512,7168]{1,0:T(8,128)(2,1)}, u32[]{:S(2)}, u32[]{:S(2)}) collective-permute-start(bf16[512,7168]{1,0:T(8,128)(2,1)} %get-tuple-element.80.refs_0_), channel_id=1, source_target_pairs={{0,2},{1,3},{2,0},{3,1},{4,6},{5,7},{6,4},{7,5}} | collective-permute-start | bytes 22020104 | tf_op jit(solution)/shard_map/ppermute | solution.py:372
  288.6 135.9 %collective-permute-start.10 = (bf16[512,4096]{1,0:T(8,128)(2,1)}, bf16[512,4096]{1,0:T(8,128)(2,1)}, u32[]{:S(2)}, u32[]{:S(2)}) collective-permute-start(bf16[512,4096]{1,0:T(8,128)(2,1)} %collective-permute-done.8.refs_1_), channel_id=1, source_target_pairs={{0,1},{1,0},{2,3},{3,2},{4,5},{5,4},{6,7},{7,6}} | collective-permute-start | bytes 12582920 | tf_op jit(solution)/shard_map/ppermute | solution.py:378
  424.4 282.0 %collective-permute-start.25 = (bf16[768,4096]{1,0:T(8,128)(2,1)}, bf16[768,4096]{1,0:T(8,128)(2,1)}, u32[]{:S(2)}, u32[]{:S(2)}) collective-permute-start(bf16[768,4096]{1,0:T(8,128)(2,1)} %slice_bitcast_fusion.1), channel_id=1, source_target_pairs={{0,2},{1,3},{2,0},{3,1},{4,6},{5,7},{6,4},{7,5}} | collective-permute-start | bytes 18874376 | tf_op jit(solution)/shard_map/ppermute | solution.py:372
  706.4 159.6 %collective-permute-start.18 = (bf16[512,7168]{1,0:T(8,128)(2,1)}, bf16[512,7168]{1,0:T(8,128)(2,1)}, u32[]{:S(2)}, u32[]{:S(2)}) collective-permute-start(bf16[512,7168]{1,0:T(8,128)(2,1)} %get-tuple-element.78), channel_id=1, source_target_pairs={{0,4},{4,0},{1,5},{5,1},{2,6},{6,2},{3,7},{7,3}} | collective-permute-start | bytes 22020104 | tf_op jit(solution)/shard_map/ppermute | solution.py:375
  706.7 183.5 %collective-permute-start.29 = (bf16[1024,4096]{1,0:T(8,128)(2,1)}, bf16[1024,4096]{1,0:T(8,128)(2,1)S(1)}, u32[]{:S(2)}, u32[]{:S(2)}) collective-permute-start(bf16[1024,4096]{1,0:T(8,128)(2,1)} %slice_bitcast_fusion), channel_id=1, source_target_pairs={{0,2},{1,3},{2,0},{3,1},{4,6},{5,7},{6,4},{7,5}} | collective-permute-start | bytes 25165832 | tf_op jit(solution)/shard_map/ppermute | solution.py:372
  708.4 357.4 %collective-permute-start.38 = (bf16[512,16000]{1,0:T(8,128)(2,1)}, bf16[512,16000]{1,0:T(8,128)(2,1)}, u32[]{:S(2)}, u32[]{:S(2)}) collective-permute-start(bf16[512,16000]{1,0:T(8,128)(2,1)} %constant_dynamic-slice_fusion.1.refs_0_), channel_id=1, source_target_pairs={{0,1},{1,0},{2,3},{3,2},{4,5},{5,4},{6,7},{7,6}} | collective-permute-start | bytes 49152008 | tf_op jit(solution)/shard_map/ppermute | solution.py:378
  708.4 337.4 %collective-permute-start.15 = (bf16[512,7168]{1,0:T(8,128)(2,1)}, bf16[512,7168]{1,0:T(8,128)(2,1)}, u32[]{:S(2)}, u32[]{:S(2)}) collective-permute-start(bf16[512,7168]{1,0:T(8,128)(2,1)} %collective-permute-done.11.refs_1_), channel_id=1, source_target_pairs={{0,2},{1,3},{2,0},{3,1},{4,6},{5,7},{6,4},{7,5}} | collective-permute-start | bytes 22020104 | tf_op jit(solution)/shard_map/ppermute | solution.py:372
  708.8 338.7 %collective-permute-start.24 = (bf16[512,7168]{1,0:T(8,128)(2,1)}, bf16[512,7168]{1,0:T(8,128)(2,1)S(1)}, u32[]{:S(2)}, u32[]{:S(2)}) collective-permute-start(bf16[512,7168]{1,0:T(8,128)(2,1)} %collective-permute-done.23.refs_2_), channel_id=1, source_target_pairs={{0,1},{1,0},{2,3},{3,2},{4,5},{5,4},{6,7},{7,6}} | collective-permute-start | bytes 22020104 | tf_op jit(solution)/shard_map/ppermute | solution.py:378
  866.0 199.9 %collective-permute-start.33 = (bf16[1024,4096]{1,0:T(8,128)(2,1)}, bf16[1024,4096]{1,0:T(8,128)(2,1)}, u32[]{:S(2)}, u32[]{:S(2)}) collective-permute-start(bf16[1024,4096]{1,0:T(8,128)(2,1)} %convolution_convert_fusion.3.mine_ref), channel_id=1, source_target_pairs={{0,4},{4,0},{1,5},{5,1},{2,6},{6,2},{3,7},{7,3}} | collective-permute-start | bytes 25165832 | tf_op jit(solution)/shard_map/ppermute | solution.py:375
  890.2 339.2 %collective-permute-start.34 = (bf16[1024,4096]{1,0:T(8,128)(2,1)}, bf16[1024,4096]{1,0:T(8,128)(2,1)}, u32[]{:S(2)}, u32[]{:S(2)}) collective-permute-start(bf16[1024,4096]{1,0:T(8,128)(2,1)} %convolution_convert_fusion.2.mine_ref), channel_id=1, source_target_pairs={{0,4},{4,0},{1,5},{5,1},{2,6},{6,2},{3,7},{7,3}} | collective-permute-start | bytes 25165832 | tf_op jit(solution)/shard_map/ppermute | solution.py:375
  1045.8 363.4 %collective-permute-start.35 = (bf16[1024,4096]{1,0:T(8,128)(2,1)}, bf16[1024,4096]{1,0:T(8,128)(2,1)}, u32[]{:S(2)}, u32[]{:S(2)}) collective-permute-start(bf16[1024,4096]{1,0:T(8,128)(2,1)} %convolution_convert_fusion.1.mine_ref), channel_id=1, source_target_pairs={{0,4},{4,0},{1,5},{5,1},{2,6},{6,2},{3,7},{7,3}} | collective-permute-start | bytes 25165832 | tf_op jit(solution)/shard_map/ppermute | solution.py:375
  1050.6 535.9 %collective-permute-start.36 = (bf16[1024,4096]{1,0:T(8,128)(2,1)}, bf16[1024,4096]{1,0:T(8,128)(2,1)}, u32[]{:S(2)}, u32[]{:S(2)}) collective-permute-start(bf16[1024,4096]{1,0:T(8,128)(2,1)} %convolution_convert_fusion.mine_ref), channel_id=1, source_target_pairs={{0,4},{4,0},{1,5},{5,1},{2,6},{6,2},{3,7},{7,3}} | collective-permute-start | bytes 25165832 | tf_op jit(solution)/shard_map/ppermute | solution.py:375
  1065.9 666.6 %collective-permute-start.12 = (bf16[512,7168]{1,0:T(8,128)(2,1)}, bf16[512,7168]{1,0:T(8,128)(2,1)S(1)}, u32[]{:S(2)}, u32[]{:S(2)}) collective-permute-start(bf16[512,7168]{1,0:T(8,128)(2,1)} %get-tuple-element.80.refs_0_), channel_id=1, source_target_pairs={{0,1},{1,0},{2,3},{3,2},{4,5},{5,4},{6,7},{7,6}} | collective-permute-start | bytes 22020104 | tf_op jit(solution)/shard_map/ppermute | solution.py:378
  1065.9 668.6 %collective-permute-start.13 = (bf16[512,7168]{1,0:T(8,128)(2,1)}, bf16[512,7168]{1,0:T(8,128)(2,1)}, u32[]{:S(2)}, u32[]{:S(2)}) collective-permute-start(bf16[512,7168]{1,0:T(8,128)(2,1)} %collective-permute-done.11.refs_1_), channel_id=1, source_target_pairs={{0,1},{1,0},{2,3},{3,2},{4,5},{5,4},{6,7},{7,6}} | collective-permute-start | bytes 22020104 | tf_op jit(solution)/shard_map/ppermute | solution.py:378
  1229.4 503.4 %collective-permute-start.16 = (bf16[512,7168]{1,0:T(8,128)(2,1)}, bf16[512,7168]{1,0:T(8,128)(2,1)}, u32[]{:S(2)}, u32[]{:S(2)}) collective-permute-start(bf16[512,7168]{1,0:T(8,128)(2,1)} %collective-permute-done.14.refs_4_), channel_id=1, source_target_pairs={{0,1},{1,0},{2,3},{3,2},{4,5},{5,4},{6,7},{7,6}} | collective-permute-start | bytes 22020104 | tf_op jit(solution)/shard_map/ppermute | solution.py:378
  1409.2 326.8 %collective-permute-start.20 = (bf16[512,7168]{1,0:T(8,128)(2,1)}, bf16[512,7168]{1,0:T(8,128)(2,1)}, u32[]{:S(2)}, u32[]{:S(2)}) collective-permute-start(bf16[512,7168]{1,0:T(8,128)(2,1)} %collective-permute-done.18.refs_0_), channel_id=1, source_target_pairs={{0,2},{1,3},{2,0},{3,1},{4,6},{5,7},{6,4},{7,5}} | collective-permute-start | bytes 22020104 | tf_op jit(solution)/shard_map/ppermute | solution.py:372
  1586.5 149.5 %collective-permute-start.17 = (bf16[512,7168]{1,0:T(8,128)(2,1)}, bf16[512,7168]{1,0:T(8,128)(2,1)}, u32[]{:S(2)}, u32[]{:S(2)}) collective-permute-start(bf16[512,7168]{1,0:T(8,128)(2,1)} %collective-permute-done.15.refs_5_), channel_id=1, source_target_pairs={{0,1},{1,0},{2,3},{3,2},{4,5},{5,4},{6,7},{7,6}} | collective-permute-start | bytes 22020104 | tf_op jit(solution)/shard_map/ppermute | solution.py:378
  1732.5 638.7 %collective-permute-start.61 = (bf16[32,16000]{1,0:T(8,128)(2,1)}, bf16[32,16000]{1,0:T(8,128)(2,1)}, u32[]{:S(2)}, u32[]{:S(2)}) collective-permute-start(bf16[32,16000]{1,0:T(8,128)(2,1)} %get-tuple-element.69), channel_id=1, source_target_pairs={{0,4},{4,0},{1,5},{5,1},{2,6},{6,2},{3,7},{7,3}} | collective-permute-start | bytes 3072008 | tf_op jit(solution)/shard_map/ppermute | solution.py:375
  1732.8 640.1 %collective-permute-start.47 = (bf16[32,16000]{1,0:T(8,128)(2,1)}, bf16[32,16000]{1,0:T(8,128)(2,1)}, u32[]{:S(2)}, u32[]{:S(2)}) collective-permute-start(bf16[32,16000]{1,0:T(8,128)(2,1)} %collective-permute-done.45.refs_2_), channel_id=1, source_target_pairs={{0,2},{1,3},{2,0},{3,1},{4,6},{5,7},{6,4},{7,5}} | collective-permute-start | bytes 3072008 | tf_op jit(solution)/shard_map/ppermute | solution.py:372
  1734.5 542.9 %collective-permute-start.26 = (bf16[768,4096]{1,0:T(8,128)(2,1)}, bf16[768,4096]{1,0:T(8,128)(2,1)}, u32[]{:S(2)}, u32[]{:S(2)}) collective-permute-start(bf16[768,4096]{1,0:T(8,128)(2,1)} %get-tuple-element.75), channel_id=1, source_target_pairs={{0,4},{4,0},{1,5},{5,1},{2,6},{6,2},{3,7},{7,3}} | collective-permute-start | bytes 18874376 | tf_op jit(solution)/shard_map/ppermute | solution.py:375
  1736.0 108.0 %collective-permute-start.19 = (bf16[512,7168]{1,0:T(8,128)(2,1)}, bf16[512,7168]{1,0:T(8,128)(2,1)}, u32[]{:S(2)}, u32[]{:S(2)}) collective-permute-start(bf16[512,7168]{1,0:T(8,128)(2,1)} %collective-permute-done.18.refs_0_), channel_id=1, source_target_pairs={{0,1},{1,0},{2,3},{3,2},{4,5},{5,4},{6,7},{7,6}} | collective-permute-start | bytes 22020104 | tf_op jit(solution)/shard_map/ppermute | solution.py:378
  1736.0 108.5 %collective-permute-start.21 = (bf16[512,7168]{1,0:T(8,128)(2,1)}, bf16[512,7168]{1,0:T(8,128)(2,1)}, u32[]{:S(2)}, u32[]{:S(2)}) collective-permute-start(bf16[512,7168]{1,0:T(8,128)(2,1)} %collective-permute-done.20.refs_2_), channel_id=1, source_target_pairs={{0,1},{1,0},{2,3},{3,2},{4,5},{5,4},{6,7},{7,6}} | collective-permute-start | bytes 22020104 | tf_op jit(solution)/shard_map/ppermute | solution.py:378
  1844.0 433.4 %collective-permute-start.30 = (bf16[1024,4096]{1,0:T(8,128)(2,1)}, bf16[1024,4096]{1,0:T(8,128)(2,1)}, u32[]{:S(2)}, u32[]{:S(2)}) collective-permute-start(bf16[1024,4096]{1,0:T(8,128)(2,1)} %get-tuple-element.73), channel_id=1, source_target_pairs={{0,4},{4,0},{1,5},{5,1},{2,6},{6,2},{3,7},{7,3}} | collective-permute-start | bytes 25165832 | tf_op jit(solution)/shard_map/ppermute | solution.py:375
  1844.5 433.4 %collective-permute-start.31 = (bf16[1024,4096]{1,0:T(8,128)(2,1)}, bf16[1024,4096]{1,0:T(8,128)(2,1)}, u32[]{:S(2)}, u32[]{:S(2)}) collective-permute-start(bf16[1024,4096]{1,0:T(8,128)(2,1)} %get-tuple-element.74.refs_0_), channel_id=1, source_target_pairs={{0,1},{1,0},{2,3},{3,2},{4,5},{5,4},{6,7},{7,6}} | collective-permute-start | bytes 25165832 | tf_op jit(solution)/shard_map/ppermute | solution.py:378
  2277.4 95.6 %collective-permute-start.27 = (bf16[768,4096]{1,0:T(8,128)(2,1)S(1)}, bf16[768,4096]{1,0:T(8,128)(2,1)S(1)}, u32[]{:S(2)}, u32[]{:S(2)}) collective-permute-start(bf16[768,4096]{1,0:T(8,128)(2,1)S(1)} %copy-done), channel_id=1, source_target_pairs={{0,1},{1,0},{2,3},{3,2},{4,5},{5,4},{6,7},{7,6}} | collective-permute-start | bytes 18874376 | tf_op jit(solution)/shard_map/ppermute | solution.py:378
  2277.4 97.1 %collective-permute-start.28 = (bf16[768,4096]{1,0:T(8,128)(2,1)}, bf16[768,4096]{1,0:T(8,128)(2,1)}, u32[]{:S(2)}, u32[]{:S(2)}) collective-permute-start(bf16[768,4096]{1,0:T(8,128)(2,1)} %collective-permute-done.26.refs_1_), channel_id=1, source_target_pairs={{0,1},{1,0},{2,3},{3,2},{4,5},{5,4},{6,7},{7,6}} | collective-permute-start | bytes 18874376 | tf_op jit(solution)/shard_map/ppermute | solution.py:378
  2277.9 70.0 %collective-permute-start.32 = (bf16[1024,4096]{1,0:T(8,128)(2,1)}, bf16[1024,4096]{1,0:T(8,128)(2,1)}, u32[]{:S(2)}, u32[]{:S(2)}) collective-permute-start(bf16[1024,4096]{1,0:T(8,128)(2,1)} %collective-permute-done.30.refs_1_), channel_id=1, source_target_pairs={{0,1},{1,0},{2,3},{3,2},{4,5},{5,4},{6,7},{7,6}} | collective-permute-start | bytes 25165832 | tf_op jit(solution)/shard_map/ppermute | solution.py:378
  2347.9 455.3 %collective-permute-start.39 = (bf16[512,16000]{1,0:T(8,128)(2,1)}, bf16[512,16000]{1,0:T(8,128)(2,1)}, u32[]{:S(2)}, u32[]{:S(2)}) collective-permute-start(bf16[512,16000]{1,0:T(8,128)(2,1)} %constant_dynamic-slice_fusion.1.refs_0_), channel_id=1, source_target_pairs={{0,2},{1,3},{2,0},{3,1},{4,6},{5,7},{6,4},{7,5}} | collective-permute-start | bytes 49152008 | tf_op jit(solution)/shard_map/ppermute | solution.py:372
  2371.2 91.9 %collective-permute-start.57 = (bf16[64,16000]{1,0:T(8,128)(2,1)}, bf16[64,16000]{1,0:T(8,128)(2,1)}, u32[]{:S(2)}, u32[]{:S(2)}) collective-permute-start(bf16[64,16000]{1,0:T(8,128)(2,1)} %constant_dynamic-slice_fusion.7), channel_id=1, source_target_pairs={{0,4},{4,0},{1,5},{5,1},{2,6},{6,2},{3,7},{7,3}} | collective-permute-start | bytes 6144008 | tf_op jit(solution)/shard_map/ppermute | solution.py:375
  2372.9 89.7 %collective-permute-start.46 = (bf16[32,16000]{1,0:T(8,128)(2,1)}, bf16[32,16000]{1,0:T(8,128)(2,1)}, u32[]{:S(2)}, u32[]{:S(2)}) collective-permute-start(bf16[32,16000]{1,0:T(8,128)(2,1)} %collective-permute-done.45.refs_2_), channel_id=1, source_target_pairs={{0,1},{1,0},{2,3},{3,2},{4,5},{5,4},{6,7},{7,6}} | collective-permute-start | bytes 3072008 | tf_op jit(solution)/shard_map/ppermute | solution.py:378
  2372.9 351.4 %collective-permute-start.63 = (bf16[32,16000]{1,0:T(8,128)(2,1)}, bf16[32,16000]{1,0:T(8,128)(2,1)}, u32[]{:S(2)}, u32[]{:S(2)}) collective-permute-start(bf16[32,16000]{1,0:T(8,128)(2,1)} %collective-permute-done.61.refs_2_), channel_id=1, source_target_pairs={{0,2},{1,3},{2,0},{3,1},{4,6},{5,7},{6,4},{7,5}} | collective-permute-start | bytes 3072008 | tf_op jit(solution)/shard_map/ppermute | solution.py:372
  2374.5 351.4 %collective-permute-start.48 = (bf16[32,16000]{1,0:T(8,128)(2,1)}, bf16[32,16000]{1,0:T(8,128)(2,1)}, u32[]{:S(2)}, u32[]{:S(2)}) collective-permute-start(bf16[32,16000]{1,0:T(8,128)(2,1)} %collective-permute-done.47.refs_4_), channel_id=1, source_target_pairs={{0,1},{1,0},{2,3},{3,2},{4,5},{5,4},{6,7},{7,6}} | collective-permute-start | bytes 3072008 | tf_op jit(solution)/shard_map/ppermute | solution.py:378
  2462.6 339.0 %collective-permute-start.41 = (bf16[192,16000]{1,0:T(8,128)(2,1)}, bf16[192,16000]{1,0:T(8,128)(2,1)}, u32[]{:S(2)}, u32[]{:S(2)}) collective-permute-start(bf16[192,16000]{1,0:T(8,128)(2,1)} %constant_dynamic-slice_fusion), channel_id=1, source_target_pairs={{0,4},{4,0},{1,5},{5,1},{2,6},{6,2},{3,7},{7,3}} | collective-permute-start | bytes 18432008 | tf_op jit(solution)/shard_map/ppermute | solution.py:375
  2463.2 336.5 %collective-permute-start.49 = (bf16[96,16000]{1,0:T(8,128)(2,1)}, bf16[96,16000]{1,0:T(8,128)(2,1)}, u32[]{:S(2)}, u32[]{:S(2)}) collective-permute-start(bf16[96,16000]{1,0:T(8,128)(2,1)} %get-tuple-element.72), channel_id=1, source_target_pairs={{0,4},{4,0},{1,5},{5,1},{2,6},{6,2},{3,7},{7,3}} | collective-permute-start | bytes 9216008 | tf_op jit(solution)/shard_map/ppermute | solution.py:375
  2724.3 76.8 %collective-permute-start.53 = (bf16[96,16000]{1,0:T(8,128)(2,1)}, bf16[96,16000]{1,0:T(8,128)(2,1)S(1)}, u32[]{:S(2)}, u32[]{:S(2)}) collective-permute-start(bf16[96,16000]{1,0:T(8,128)(2,1)} %get-tuple-element.71), channel_id=1, source_target_pairs={{0,4},{4,0},{1,5},{5,1},{2,6},{6,2},{3,7},{7,3}} | collective-permute-start | bytes 9216008 | tf_op jit(solution)/shard_map/ppermute | solution.py:375
  2725.8 75.3 %collective-permute-start.59 = (bf16[64,16000]{1,0:T(8,128)(2,1)}, bf16[64,16000]{1,0:T(8,128)(2,1)}, u32[]{:S(2)}, u32[]{:S(2)}) collective-permute-start(bf16[64,16000]{1,0:T(8,128)(2,1)} %collective-permute-done.57.refs_2_), channel_id=1, source_target_pairs={{0,2},{1,3},{2,0},{3,1},{4,6},{5,7},{6,4},{7,5}} | collective-permute-start | bytes 6144008 | tf_op jit(solution)/shard_map/ppermute | solution.py:372
  2799.6 76.9 %collective-permute-start.51 = (bf16[96,16000]{1,0:T(8,128)(2,1)}, bf16[96,16000]{1,0:T(8,128)(2,1)}, u32[]{:S(2)}, u32[]{:S(2)}) collective-permute-start(bf16[96,16000]{1,0:T(8,128)(2,1)} %collective-permute-done.49.refs_2_), channel_id=1, source_target_pairs={{0,2},{1,3},{2,0},{3,1},{4,6},{5,7},{6,4},{7,5}} | collective-permute-start | bytes 9216008 | tf_op jit(solution)/shard_map/ppermute | solution.py:372
  2801.1 75.9 %collective-permute-start.50 = (bf16[96,16000]{1,0:T(8,128)(2,1)}, bf16[96,16000]{1,0:T(8,128)(2,1)}, u32[]{:S(2)}, u32[]{:S(2)}) collective-permute-start(bf16[96,16000]{1,0:T(8,128)(2,1)} %collective-permute-done.49.refs_2_), channel_id=1, source_target_pairs={{0,1},{1,0},{2,3},{3,2},{4,5},{5,4},{6,7},{7,6}} | collective-permute-start | bytes 9216008 | tf_op jit(solution)/shard_map/ppermute | solution.py:378
  2801.1 134.0 %collective-permute-start.55 = (bf16[96,16000]{1,0:T(8,128)(2,1)S(1)}, bf16[96,16000]{1,0:T(8,128)(2,1)}, u32[]{:S(2)}, u32[]{:S(2)}) collective-permute-start(bf16[96,16000]{1,0:T(8,128)(2,1)S(1)} %collective-permute-done.53.refs_2_), channel_id=1, source_target_pairs={{0,2},{1,3},{2,0},{3,1},{4,6},{5,7},{6,4},{7,5}} | collective-permute-start | bytes 9216008 | tf_op jit(solution)/shard_map/ppermute | solution.py:372
  2801.7 263.2 %collective-permute-start.43 = (bf16[192,16000]{1,0:T(8,128)(2,1)}, bf16[192,16000]{1,0:T(8,128)(2,1)}, u32[]{:S(2)}, u32[]{:S(2)}) collective-permute-start(bf16[192,16000]{1,0:T(8,128)(2,1)} %collective-permute-done.41.refs_2_), channel_id=1, source_target_pairs={{0,2},{1,3},{2,0},{3,1},{4,6},{5,7},{6,4},{7,5}} | collective-permute-start | bytes 18432008 | tf_op jit(solution)/shard_map/ppermute | solution.py:372
  2803.2 344.8 %collective-permute-start.40 = (bf16[512,16000]{1,0:T(8,128)(2,1)}, bf16[512,16000]{1,0:T(8,128)(2,1)}, u32[]{:S(2)}, u32[]{:S(2)}) collective-permute-start(bf16[512,16000]{1,0:T(8,128)(2,1)} %collective-permute-done.39.refs_2_.refs_0_), channel_id=1, source_target_pairs={{0,1},{1,0},{2,3},{3,2},{4,5},{5,4},{6,7},{7,6}} | collective-permute-start | bytes 49152008 | tf_op jit(solution)/shard_map/ppermute | solution.py:378
  2876.5 265.2 %collective-permute-start.54 = (bf16[96,16000]{1,0:T(8,128)(2,1)S(1)}, bf16[96,16000]{1,0:T(8,128)(2,1)}, u32[]{:S(2)}, u32[]{:S(2)}) collective-permute-start(bf16[96,16000]{1,0:T(8,128)(2,1)S(1)} %collective-permute-done.53.refs_2_), channel_id=1, source_target_pairs={{0,1},{1,0},{2,3},{3,2},{4,5},{5,4},{6,7},{7,6}} | collective-permute-start | bytes 9216008 | tf_op jit(solution)/shard_map/ppermute | solution.py:378
  2877.0 266.5 %collective-permute-start.42 = (bf16[192,16000]{1,0:T(8,128)(2,1)}, bf16[192,16000]{1,0:T(8,128)(2,1)}, u32[]{:S(2)}, u32[]{:S(2)}) collective-permute-start(bf16[192,16000]{1,0:T(8,128)(2,1)} %collective-permute-done.41.refs_2_), channel_id=1, source_target_pairs={{0,1},{1,0},{2,3},{3,2},{4,5},{5,4},{6,7},{7,6}} | collective-permute-start | bytes 18432008 | tf_op jit(solution)/shard_map/ppermute | solution.py:378
  2935.2 207.1 %collective-permute-start.52 = (bf16[96,16000]{1,0:T(8,128)(2,1)}, bf16[96,16000]{1,0:T(8,128)(2,1)}, u32[]{:S(2)}, u32[]{:S(2)}) collective-permute-start(bf16[96,16000]{1,0:T(8,128)(2,1)} %collective-permute-done.51.refs_4_), channel_id=1, source_target_pairs={{0,1},{1,0},{2,3},{3,2},{4,5},{5,4},{6,7},{7,6}} | collective-permute-start | bytes 9216008 | tf_op jit(solution)/shard_map/ppermute | solution.py:378
  3064.9 82.5 %collective-permute-start.44 = (bf16[192,16000]{1,0:T(8,128)(2,1)}, bf16[192,16000]{1,0:T(8,128)(2,1)}, u32[]{:S(2)}, u32[]{:S(2)}) collective-permute-start(bf16[192,16000]{1,0:T(8,128)(2,1)} %collective-permute-done.43.refs_4_), channel_id=1, source_target_pairs={{0,1},{1,0},{2,3},{3,2},{4,5},{5,4},{6,7},{7,6}} | collective-permute-start | bytes 18432008 | tf_op jit(solution)/shard_map/ppermute | solution.py:378
  3141.6 82.1 %collective-permute-start.56 = (bf16[96,16000]{1,0:T(8,128)(2,1)}, bf16[96,16000]{1,0:T(8,128)(2,1)}, u32[]{:S(2)}, u32[]{:S(2)}) collective-permute-start(bf16[96,16000]{1,0:T(8,128)(2,1)} %collective-permute-done.55.refs_4_), channel_id=1, source_target_pairs={{0,1},{1,0},{2,3},{3,2},{4,5},{5,4},{6,7},{7,6}} | collective-permute-start | bytes 9216008 | tf_op jit(solution)/shard_map/ppermute | solution.py:378
  3143.5 89.4 %collective-permute-start.58 = (bf16[64,16000]{1,0:T(8,128)(2,1)}, bf16[64,16000]{1,0:T(8,128)(2,1)}, u32[]{:S(2)}, u32[]{:S(2)}) collective-permute-start(bf16[64,16000]{1,0:T(8,128)(2,1)} %collective-permute-done.57.refs_2_), channel_id=1, source_target_pairs={{0,1},{1,0},{2,3},{3,2},{4,5},{5,4},{6,7},{7,6}} | collective-permute-start | bytes 6144008 | tf_op jit(solution)/shard_map/ppermute | solution.py:378
  3146.2 86.7 %collective-permute-start.60 = (bf16[64,16000]{1,0:T(8,128)(2,1)}, bf16[64,16000]{1,0:T(8,128)(2,1)}, u32[]{:S(2)}, u32[]{:S(2)}) collective-permute-start(bf16[64,16000]{1,0:T(8,128)(2,1)} %collective-permute-done.59.refs_4_), channel_id=1, source_target_pairs={{0,1},{1,0},{2,3},{3,2},{4,5},{5,4},{6,7},{7,6}} | collective-permute-start | bytes 6144008 | tf_op jit(solution)/shard_map/ppermute | solution.py:378
  3147.4 92.4 %collective-permute-start.62 = (bf16[32,16000]{1,0:T(8,128)(2,1)}, bf16[32,16000]{1,0:T(8,128)(2,1)}, u32[]{:S(2)}, u32[]{:S(2)}) collective-permute-start(bf16[32,16000]{1,0:T(8,128)(2,1)} %collective-permute-done.61.refs_2_), channel_id=1, source_target_pairs={{0,1},{1,0},{2,3},{3,2},{4,5},{5,4},{6,7},{7,6}} | collective-permute-start | bytes 3072008 | tf_op jit(solution)/shard_map/ppermute | solution.py:378
  3147.9 91.8 %collective-permute-start.64 = (bf16[32,16000]{1,0:T(8,128)(2,1)}, bf16[32,16000]{1,0:T(8,128)(2,1)}, u32[]{:S(2)}, u32[]{:S(2)}) collective-permute-start(bf16[32,16000]{1,0:T(8,128)(2,1)} %collective-permute-done.63.refs_4_), channel_id=1, source_target_pairs={{0,1},{1,0},{2,3},{3,2},{4,5},{5,4},{6,7},{7,6}} | collective-permute-start | bytes 3072008 | tf_op jit(solution)/shard_map/ppermute | solution.py:378
  (39 other events, 2305.0 us)
